TPU v7x, 16 devices: a whole 2x2x2 slice. The times are simulated.
16 devices in a mesh: pp: 2 (over z), ep: 8 (over y, x, core).
Axes of the slice: x: 2, y: 2, z: 2, core: 2. Of those that a mesh axis runs over, the one named last changes fastest.
Arguments:
- x_fwd: bfloat16 [2, 8192, 512], P('pp', 'ep')
- ids_fwd: int32 [2, 8192, 8], P('pp', 'ep')
- slots_fwd: int32 [2, 8192, 8], P('pp', 'ep')
- gates_fwd: bfloat16 [2, 8192, 8], P('pp', 'ep')
- x_saved: bfloat16 [2, 8192, 512], P('pp', 'ep')
- grad_in: bfloat16 [2, 8192, 512], P('pp', 'ep')
- ids_bwd: int32 [2, 8192, 8], P('pp', 'ep')
- slots_bwd: int32 [2, 8192, 8], P('pp', 'ep')
- gates_bwd: bfloat16 [2, 8192, 8], P('pp', 'ep')
- w_one: bfloat16 [2, 512, 1536], P('pp')
- w_two: bfloat16 [2, 1536, 512], P('pp')
- w_gate: bfloat16 [2, 128, 512, 384], P('pp', 'ep')
- w_up: bfloat16 [2, 128, 512, 384], P('pp', 'ep')
- w_down: bfloat16 [2, 128, 384, 512], P('pp', 'ep')
Outputs:
- output 1: bfloat16 [2, 8192, 512], P('pp', 'ep')
- output 2: bfloat16 [2, 8192, 512], P('pp', 'ep')
- output 3: float32 [2, 128, 512, 384], P('pp', 'ep')
- output 4: float32 [2, 128, 512, 384], P('pp', 'ep')
- output 5: float32 [2, 128, 384, 512], P('pp', 'ep')
All inputs are finite; a program needn't handle non-finite values.
Results may differ from a plain program's by a relative error of at most 0.0104412.
Values are sent between devices in bfloat16 or wider.
A program may use at most 1 GiB of HBM per device.

v0:
```python
import jax
import jax.numpy as jnp
from jax import lax
from jax.sharding import PartitionSpec as P

NORM_EPS = 1e-6


def rms_norm(values):
    return values * lax.rsqrt(jnp.mean(values * values, axis=-1, keepdims=True) + NORM_EPS)


def silu_grad(values):
    sigmoid_vals = jax.nn.sigmoid(values)
    return sigmoid_vals * (1.0 + values * (1.0 - sigmoid_vals))


def capacity(tok_rows, top_k, n_experts):
    return 8 * ((2 * tok_rows * top_k + 8 * n_experts - 1) // (8 * n_experts))


def dense_forward(x_rows, w_one, w_two):
    normed = rms_norm(x_rows.astype(jnp.float32)).astype(jnp.bfloat16)
    hidden_pre = jnp.dot(normed, w_one, preferred_element_type=jnp.float32)
    dense_act = jax.nn.silu(hidden_pre).astype(jnp.bfloat16)
    dense_out = jnp.dot(dense_act, w_two, preferred_element_type=jnp.float32)
    return (x_rows.astype(jnp.float32) + dense_out).astype(jnp.bfloat16), hidden_pre


def dense_backward(x_rows, hidden_pre, w_one, w_two, grad_h):
    _, norm_vjp = jax.vjp(rms_norm, x_rows.astype(jnp.float32))
    grad_act = jnp.einsum("th,fh->tf", grad_h.astype(jnp.bfloat16), w_two, preferred_element_type=jnp.float32)
    grad_pre = (grad_act * silu_grad(hidden_pre)).astype(jnp.bfloat16)
    grad_norm = jnp.einsum("tf,hf->th", grad_pre, w_one, preferred_element_type=jnp.float32)
    return grad_h + norm_vjp(grad_norm)[0]


def expert_forward(buf_rows, w_gate, w_up, w_down):
    pre_gate = jnp.einsum("ech,ehf->ecf", buf_rows, w_gate, preferred_element_type=jnp.float32)
    pre_up = jnp.einsum("ech,ehf->ecf", buf_rows, w_up, preferred_element_type=jnp.float32)
    expert_act = (jax.nn.silu(pre_gate) * pre_up).astype(jnp.bfloat16)
    return jnp.einsum("ecf,efh->ech", expert_act, w_down, preferred_element_type=jnp.float32).astype(jnp.bfloat16)


def expert_backward(buf_rows, grad_out, w_gate, w_up, w_down):
    pre_gate = jnp.einsum("ech,ehf->ecf", buf_rows, w_gate, preferred_element_type=jnp.float32)
    pre_up = jnp.einsum("ech,ehf->ecf", buf_rows, w_up, preferred_element_type=jnp.float32)
    silu_gate = jax.nn.silu(pre_gate)
    expert_act = (silu_gate * pre_up).astype(jnp.bfloat16)
    dw_down = jnp.einsum("ecf,ech->efh", expert_act, grad_out, preferred_element_type=jnp.float32)
    grad_act = jnp.einsum("ech,efh->ecf", grad_out, w_down, preferred_element_type=jnp.float32).astype(jnp.bfloat16).astype(jnp.float32)
    grad_gate = (grad_act * pre_up * silu_grad(pre_gate)).astype(jnp.bfloat16)
    grad_up = (grad_act * silu_gate).astype(jnp.bfloat16)
    dw_gate = jnp.einsum("ech,ecf->ehf", buf_rows, grad_gate, preferred_element_type=jnp.float32)
    dw_up = jnp.einsum("ech,ecf->ehf", buf_rows, grad_up, preferred_element_type=jnp.float32)
    grad_rows = jnp.einsum("ecf,ehf->ech", grad_gate, w_gate, preferred_element_type=jnp.float32) + jnp.einsum("ecf,ehf->ech", grad_up, w_up, preferred_element_type=jnp.float32)
    return grad_rows.astype(jnp.bfloat16), dw_gate, dw_up, dw_down


def route_maps(expert_ids, slot_ids, n_experts, cap_rows):
    tok_rows = expert_ids.shape[0]
    row_index = jnp.where(slot_ids >= 0, expert_ids * cap_rows + slot_ids, n_experts * cap_rows)
    token_ids = jnp.broadcast_to(jnp.arange(tok_rows, dtype=jnp.int32)[:, None], expert_ids.shape)
    token_of_row = jnp.full((n_experts * cap_rows,), tok_rows, jnp.int32).at[row_index.reshape(-1)].set(token_ids.reshape(-1), mode="drop")
    return row_index, token_of_row


def solution(mesh):
    stages = mesh.shape["pp"]
    ep_size = mesh.shape["ep"]
    next_perm = [(stage_idx, (stage_idx + 1) % stages) for stage_idx in range(stages)]
    prev_perm = [(stage_idx, (stage_idx - 1) % stages) for stage_idx in range(stages)]
    tok_spec = P("pp", "ep", None)
    dense_spec = P("pp", None, None)
    expert_spec = P("pp", "ep", None, None)

    def device_step(x_fwd, ids_fwd, slots_fwd, gates_fwd, x_saved, grad_in, ids_bwd, slots_bwd, gates_bwd, w_one, w_two, w_gate, w_up, w_down):
        x_fwd, ids_fwd, slots_fwd, gates_fwd = x_fwd[0], ids_fwd[0], slots_fwd[0], gates_fwd[0]
        x_saved, grad_in, ids_bwd, slots_bwd, gates_bwd = x_saved[0], grad_in[0], ids_bwd[0], slots_bwd[0], gates_bwd[0]
        w_one, w_two, w_gate, w_up, w_down = w_one[0], w_two[0], w_gate[0], w_up[0], w_down[0]
        tok_rows, top_k = ids_fwd.shape
        hidden = x_fwd.shape[1]
        n_experts = w_gate.shape[0] * ep_size
        cap_rows = capacity(tok_rows, top_k, n_experts)
        n_rows = n_experts * cap_rows

        h_fwd, _ = dense_forward(x_fwd, w_one, w_two)
        xn_fwd = rms_norm(h_fwd.astype(jnp.float32)).astype(jnp.bfloat16)
        row_fwd, tok_fwd = route_maps(ids_fwd, slots_fwd, n_experts, cap_rows)
        send_fwd = jnp.take(xn_fwd, tok_fwd, axis=0, mode="fill", fill_value=0).reshape(n_experts, cap_rows, hidden)
        recv_fwd = lax.all_to_all(send_fwd, "ep", 0, 1, tiled=True)
        out_fwd = expert_forward(recv_fwd, w_gate, w_up, w_down)
        back_fwd = lax.all_to_all(out_fwd, "ep", 1, 0, tiled=True).reshape(n_rows, hidden)
        routed = jnp.take(back_fwd, row_fwd, axis=0, mode="fill", fill_value=0)
        mix_sum = jnp.einsum("tr,trh->th", gates_fwd, routed, preferred_element_type=jnp.float32)
        y_out = (h_fwd.astype(jnp.float32) + mix_sum).astype(jnp.bfloat16)

        h_bwd, hidden_pre = dense_forward(x_saved, w_one, w_two)
        xn_bwd = rms_norm(h_bwd.astype(jnp.float32)).astype(jnp.bfloat16)
        row_bwd, tok_bwd = route_maps(ids_bwd, slots_bwd, n_experts, cap_rows)
        gate_of_row = jnp.zeros((n_rows,), jnp.bfloat16).at[row_bwd.reshape(-1)].set(gates_bwd.reshape(-1), mode="drop")
        send_rows = jnp.take(xn_bwd, tok_bwd, axis=0, mode="fill", fill_value=0).reshape(n_experts, cap_rows, hidden)
        send_grad = (jnp.take(grad_in, tok_bwd, axis=0, mode="fill", fill_value=0) * gate_of_row[:, None]).reshape(n_experts, cap_rows, hidden)
        recv_rows = lax.all_to_all(send_rows, "ep", 0, 1, tiled=True)
        recv_grad = lax.all_to_all(send_grad, "ep", 0, 1, tiled=True)
        grad_rows, dw_gate, dw_up, dw_down = expert_backward(recv_rows, recv_grad, w_gate, w_up, w_down)
        back_grad = lax.all_to_all(grad_rows, "ep", 1, 0, tiled=True).reshape(n_rows, hidden)
        grad_xn = jnp.sum(jnp.take(back_grad, row_bwd, axis=0, mode="fill", fill_value=0), axis=1, dtype=jnp.float32)
        _, rms_vjp = jax.vjp(rms_norm, h_bwd.astype(jnp.float32))
        grad_h = grad_in.astype(jnp.float32) + rms_vjp(grad_xn)[0]
        grad_x = dense_backward(x_saved, hidden_pre, w_one, w_two, grad_h).astype(jnp.bfloat16)

        y_next = lax.ppermute(y_out, "pp", next_perm)
        dx_prev = lax.ppermute(grad_x, "pp", prev_perm)
        return y_next[None], dx_prev[None], dw_gate[None], dw_up[None], dw_down[None]

    in_specs = (tok_spec,) * 9 + (dense_spec, dense_spec, expert_spec, expert_spec, expert_spec)
    out_specs = (tok_spec, tok_spec, expert_spec, expert_spec, expert_spec)
    return jax.shard_map(device_step, mesh=mesh, in_specs=in_specs, out_specs=out_specs, check_vma=False)
```

profile of v0, /device:TPU:0, one launch (start us, length us, event | category | flops | bytes accessed | tf_op | source)
XLA Modules:
  0.0 1317.4 jit_solution(10780245371834865159)
XLA Ops:
  3.0 30.5 %scatter_custom_fusion.1 = s32[16384]{0:T(1024)S(1)} fusion(s32[8192]{0:T(1024)S(1)} %bitcast.191, s32[8192]{0:T(1024)S(1)} %reshape.289, s32[]{:T(128)} %constant.30.clone.1), kind=kCustom, calls=%fused_computation.112 | custom fusion | bytes 65540 | tf_op jit(solution)/shard_map/scatter | solution.py:64
  44.9 68.3 %gather_fusion.3 = bf16[16384,512]{1,0:T(8,128)(2,1)} fusion(bf16[1024,512]{1,0:T(8,128)(2,1)} %copy.72, s32[16384]{0:T(1024)S(1)} %fusion.81), kind=kCustom, calls=%fused_computation.3.clone | custom fusion | bytes 33619968 | tf_op jit(solution)/shard_map/jit(_take)/gather | solution.py:102
  113.2 66.1 %gather_fusion.2 = bf16[16384,512]{1,0:T(8,128)(2,1)} fusion(bf16[1024,512]{1,0:T(8,128)(2,1)S(1)} %bitcast.175, s32[16384]{0:T(1024)S(1)} %fusion.81), kind=kCustom, calls=%fused_computation.2.clone | custom fusion | bytes 33619968 | tf_op jit(solution)/shard_map/jit(_take)/gather | solution.py:103
  179.3 56.6 %scatter_custom_fusion.2 = bf16[16384]{0:T(1024)(128)(2,1)S(1)} fusion(s32[8192]{0:T(1024)S(1)} %bitcast.192, bf16[8192]{0:T(1024)(128)(2,1)S(1)} %reshape.297, bf16[]{:T(256)} %constant.34.clone.1), kind=kCustom, calls=%fused_computation.121 | custom fusion | bytes 32770 | tf_op jit(solution)/shard_map/scatter | solution.py:101
  235.9 23.8 %select_multiply_fusion = (bf16[16384,512]{1,0:T(8,128)(2,1)}, bf16[16384,512]{1,0:T(8,128)(2,1)}) fusion(bf16[16384,512]{1,0:T(8,128)(2,1)} %gather_fusion.2, pred[16384]{0:T(1024)(128)(4,1)S(1)} %compare_and_fusion, bf16[16384]{0:T(1024)(128)(2,1)S(1)} %scatter_custom_fusion.2, bf16[16384,512]{1,0:T(8,128)(2,1)} %gather_fusion.3), kind=kLoop, calls=%fused_computation.19 | loop fusion | flops 25165824 | bytes 67158016 | tf_op jit(solution)/shard_map/mul | solution.py:103
  259.7 192.0 %all_to_all.84 = bf16[128,128,512]{2,1,0:T(8,128)(2,1)} all-to-all(bf16[128,128,512]{2,1,0:T(8,128)(2,1)} %bitcast.187), channel_id=1, replica_groups=mesh['pp'=2,'ep'=8] {'ep'}, dimensions={0} | all-to-all | bytes 33554432 | tf_op jit(solution)/shard_map/all_to_all | solution.py:104
  459.0 30.5 %scatter_custom_fusion = s32[16384]{0:T(1024)S(1)} fusion(s32[8192]{0:T(1024)S(1)} %bitcast.193, s32[8192]{0:T(1024)S(1)} %reshape.289, s32[]{:T(128)} %constant.30.clone.1), kind=kCustom, calls=%fused_computation.114 | custom fusion | bytes 65540 | tf_op jit(solution)/shard_map/scatter | solution.py:64
  501.8 66.4 %gather_fusion = bf16[16384,512]{1,0:T(8,128)(2,1)} fusion(bf16[1024,512]{1,0:T(8,128)(2,1)S(1)} %copy.60, s32[16384]{0:T(1024)S(1)} %fusion.80), kind=kCustom, calls=%fused_computation.clone | custom fusion | bytes 33619968 | tf_op jit(solution)/shard_map/jit(_take)/gather | solution.py:90
  568.2 14.5 %broadcast_select_fusion.1 = bf16[16384,512]{1,0:T(8,128)(2,1)} fusion(bf16[16384,512]{1,0:T(8,128)(2,1)} %gather_fusion, pred[16384]{0:T(1024)(128)(4,1)S(1)} %compare_and_fusion.1), kind=kLoop, calls=%fused_computation.22 | loop fusion | flops 8388608 | bytes 33570816 | tf_op jit(solution)/shard_map/jit(_take)/select_n | solution.py:90
  582.7 59.0 %all-to-all-done.2 = bf16[128,128,512]{2,1,0:T(8,128)(2,1)} async-done(((bf16[128,128,512]{2,1,0:T(8,128)(2,1)}), bf16[128,128,512]{2,1,0:T(8,128)(2,1)}, u32[]{:S(2)}, u32[]{:S(2)}) %all-to-all-start.2) | async-done | bytes 16777248 | tf_op jit(solution)/shard_map/all_to_all | solution.py:105
  661.6 13.9 %copy.70 = bf16[16,8,128,512]{3,2,1,0:T(8,128)(2,1)} copy(bf16[16,8,128,512]{3,2,0,1:T(8,128)(2,1)} %bitcast.25) | data formatting | bytes 33554432 | tf_op jit(solution)/shard_map/all_to_all | solution.py:105
  675.6 18.8 %fusion.20 = f32[16,1024,384]{2,1,0:T(8,128)} fusion(bf16[16,1024,512]{2,1,0:T(8,128)(2,1)} %bitcast.178, bf16[1,16,512,384]{3,2,1,0:T(8,128)(2,1)} %param.29), kind=kOutput, calls=%fused_computation.38 | convolution fusion | flops 6442450944 | bytes 48234496 | tf_op jit(solution)/shard_map/ech,ehf->ecf/dot_general | solution.py:46
  694.3 18.8 %fusion.10 = f32[16,1024,384]{2,1,0:T(8,128)} fusion(bf16[16,1024,512]{2,1,0:T(8,128)(2,1)} %bitcast.179, bf16[1,16,512,384]{3,2,1,0:T(8,128)(2,1)} %param.30), kind=kOutput, calls=%fused_computation.32 | convolution fusion | flops 6442450944 | bytes 48234496 | tf_op jit(solution)/shard_map/ech,ehf->ecf/dot_general | solution.py:47
  713.1 35.2 %fusion.2 = (bf16[16,1024,384]{2,1,0:T(8,128)(2,1)}, bf16[16,1024,384]{2,1,0:T(8,128)(2,1)}) fusion(f32[16,1024,384]{2,1,0:T(8,128)} %fusion.20, f32[16,1024,384]{2,1,0:T(8,128)} %fusion.10, bf16[16,1024,512]{2,1,0:T(8,128)(2,1)} %bitcast.188, bf16[1,16,384,512]{3,2,1,0:T(8,128)(2,1)} %param.31), kind=kOutput, calls=%fused_computation.13 | convolution fusion | flops 6536822784 | bytes 98566144 | tf_op jit(solution)/shard_map/ech,efh->ecf/dot_general | solution.py:51
  748.3 20.0 %fusion.18 = f32[16,1024,512]{2,1,0:T(8,128)} fusion(bf16[16,1024,384]{2,1,0:T(8,128)(2,1)} %get-tuple-element.27, bf16[1,16,512,384]{3,2,1,0:T(8,128)(2,1)} %param.29), kind=kOutput, calls=%fused_computation.36 | convolution fusion | flops 6442450944 | bytes 52428800 | tf_op jit(solution)/shard_map/ecf,ehf->ech/dot_general | solution.py:56
  768.2 23.5 %add_convert_fusion = bf16[16,1024,512]{2,1,0:T(8,128)(2,1)} fusion(f32[16,1024,512]{2,1,0:T(8,128)} %fusion.18, bf16[16,1024,384]{2,1,0:T(8,128)(2,1)} %get-tuple-element.26, bf16[1,16,512,384]{3,2,1,0:T(8,128)(2,1)} %param.30), kind=kOutput, calls=%fused_computation.8 | convolution fusion | flops 6459228160 | bytes 69206016 | tf_op jit(solution)/shard_map/ecf,ehf->ech/dot_general | solution.py:56
  791.8 18.5 %copy.74 = bf16[16,1024,512]{2,0,1:T(8,128)(2,1)} copy(bf16[16,1024,512]{2,1,0:T(8,128)(2,1)} %add_convert_fusion) | data formatting | bytes 33554432 | tf_op jit(solution)/shard_map/convert_element_type | solution.py:57
  810.3 21.4 %all-to-all-done = bf16[128,128,512]{2,1,0:T(8,128)(2,1)} async-done(((bf16[128,128,512]{2,1,0:T(8,128)(2,1)}), bf16[128,128,512]{2,1,0:T(8,128)(2,1)}, u32[]{:S(2)}, u32[]{:S(2)}) %all-to-all-start) | async-done | bytes 16777248 | tf_op jit(solution)/shard_map/all_to_all | solution.py:91
  837.9 14.0 %copy.61 = bf16[16,8,128,512]{3,2,1,0:T(8,128)(2,1)} copy(bf16[16,8,128,512]{3,2,0,1:T(8,128)(2,1)} %bitcast.8) | data formatting | bytes 33554432 | tf_op jit(solution)/shard_map/all_to_all | solution.py:91
  851.9 18.8 %fusion.22 = f32[16,1024,384]{2,1,0:T(8,128)} fusion(bf16[16,1024,512]{2,1,0:T(8,128)(2,1)} %bitcast.182, bf16[1,16,512,384]{3,2,1,0:T(8,128)(2,1)} %param.29), kind=kOutput, calls=%fused_computation.40 | convolution fusion | flops 6442450944 | bytes 48234496 | tf_op jit(solution)/shard_map/ech,ehf->ecf/dot_general | solution.py:39
  870.7 30.6 %fusion.6 = bf16[16,1024,512]{2,1,0:T(8,128)(2,1)} fusion(f32[16,1024,384]{2,1,0:T(8,128)} %fusion.22, bf16[1,16,384,512]{3,2,1,0:T(8,128)(2,1)} %param.31, bf16[16,1024,512]{2,1,0:T(8,128)(2,1)} %bitcast.183, bf16[1,16,512,384]{3,2,1,0:T(8,128)(2,1)} %param.30), kind=kOutput, calls=%fused_computation.25 | convolution fusion | flops 12931039232 | bytes 71303168 | tf_op jit(solution)/shard_map/ecf,efh->ech/dot_general | solution.py:42
  901.3 18.5 %copy.62 = bf16[16,1024,512]{2,0,1:T(8,128)(2,1)} copy(bf16[16,1024,512]{2,1,0:T(8,128)(2,1)} %fusion.6) | data formatting | bytes 33554432 | tf_op jit(solution)/shard_map/convert_element_type | solution.py:42
  919.8 102.0 %all-to-all-done.4 = bf16[16,1024,512]{2,0,1:T(8,128)(2,1)} async-done(((bf16[16,1024,512]{2,0,1:T(8,128)(2,1)}), bf16[16,1024,512]{2,0,1:T(8,128)(2,1)}, u32[]{:S(2)}, u32[]{:S(2)}) %all-to-all-start.4) | async-done | bytes 16777248 | tf_op jit(solution)/shard_map/all_to_all | solution.py:107
  1031.4 18.8 %convolution_bitcast_fusion = f32[1,16,512,384]{3,2,1,0:T(8,128)} fusion(bf16[16,1024,512]{2,1,0:T(8,128)(2,1)} %bitcast.180, bf16[16,1024,384]{2,1,0:T(8,128)(2,1)} %get-tuple-element.26), kind=kOutput, calls=%fused_computation.47 | convolution fusion | flops 6442450944 | bytes 41943040 | tf_op jit(solution)/shard_map/ech,ecf->ehf/dot_general | solution.py:55
  1050.2 28.2 %fusion.25 = f32[1,16,384,512]{3,2,1,0:T(8,128)} fusion(bf16[16,1024,512]{2,1,0:T(8,128)(2,1)} %bitcast.189, f32[16,1024,384]{2,1,0:T(8,128)} %fusion.10, f32[16,1024,384]{2,1,0:T(8,128)} %fusion.20), kind=kOutput, calls=%fused_computation.46 | convolution fusion | flops 6480199680 | bytes 79691776 | tf_op jit(solution)/shard_map/ecf,ech->efh/dot_general | solution.py:50
  1078.4 18.7 %copy.75 = bf16[16,8,128,512]{3,2,0,1:T(8,128)(2,1)} copy(bf16[16,8,128,512]{3,0,2,1:T(8,128)(2,1)} %bitcast.33) | data formatting | bytes 33554432 | tf_op jit(solution)/shard_map/all_to_all | solution.py:107
  1097.0 41.9 %gather_fusion.4 = bf16[8192,512]{1,0:T(8,128)(2,1)} fusion(bf16[16384,512]{1,0:T(8,128)(2,1)} %bitcast.176, s32[8192]{0:T(1024)S(1)} %broadcast_clamp_fusion), kind=kCustom, calls=%fused_computation.4.clone | custom fusion | bytes 16809984 | tf_op jit(solution)/shard_map/jit(_take)/gather | solution.py:108
  1170.8 40.9 %all-to-all-done.1 = bf16[16,1024,512]{2,0,1:T(8,128)(2,1)} async-done(((bf16[16,1024,512]{2,0,1:T(8,128)(2,1)}), bf16[16,1024,512]{2,0,1:T(8,128)(2,1)}, u32[]{:S(2)}, u32[]{:S(2)}) %all-to-all-start.1) | async-done | bytes 16777248 | tf_op jit(solution)/shard_map/all_to_all | solution.py:93
  1211.7 18.7 %copy.63 = bf16[16,8,128,512]{3,2,0,1:T(8,128)(2,1)} copy(bf16[16,8,128,512]{3,0,2,1:T(8,128)(2,1)} %bitcast.13) | data formatting | bytes 33554432 | tf_op jit(solution)/shard_map/all_to_all | solution.py:93
  1230.5 41.9 %gather_fusion.1 = bf16[8192,512]{1,0:T(8,128)(2,1)} fusion(bf16[16384,512]{1,0:T(8,128)(2,1)} %bitcast.177, s32[8192]{0:T(1024)S(1)} %broadcast_clamp_fusion.1), kind=kCustom, calls=%fused_computation.1.clone | custom fusion | bytes 16809984 | tf_op jit(solution)/shard_map/jit(_take)/gather | solution.py:94
  1272.3 14.2 %multiply_reduce_fusion = f32[1024,512]{1,0:T(8,128)} fusion(f32[1024,8]{1,0:T(8,128)S(1)} %copy.92, bf16[8192,512]{1,0:T(8,128)(2,1)} %gather_fusion.1, pred[1024,8]{1,0:T(8,128)(4,1)S(1)} %copy-done.7), kind=kLoop, calls=%fused_computation.18 | loop fusion | flops 16252928 | bytes 10526720
  1294.6 18.8 %convolution_bitcast_fusion.1 = f32[1,16,512,384]{3,2,1,0:T(8,128)} fusion(bf16[16,1024,512]{2,1,0:T(8,128)(2,1)} %bitcast.181, bf16[16,1024,384]{2,1,0:T(8,128)(2,1)} %get-tuple-element.27), kind=kOutput, calls=%fused_computation.48 | convolution fusion | flops 6442450944 | bytes 41943040 | tf_op jit(solution)/shard_map/ech,ecf->ehf/dot_general | solution.py:54
  (118 shorter events, 112.4 us)
Async XLA Ops:
  0.6 37.0 %copy-start = (bf16[1,512,1536]{2,1,0:T(8,128)(2,1)S(1)}, bf16[1,512,1536]{2,1,0:T(8,128)(2,1)}, u32[]{:S(2)}) copy-start(bf16[1,512,1536]{2,1,0:T(8,128)(2,1)} %param.27) | copy-start | bytes 4718596
  2.2 32.3 %copy-start.8 = (s32[1,1024,8]{1,2,0:T(8,128)}, s32[1,1024,8]{1,2,0:T(8,128)S(1)}, u32[]{:S(2)}) copy-start(s32[1,1024,8]{1,2,0:T(8,128)S(1)} %get-tuple-element.23) | copy-start | bytes 98308
  36.2 5.9 copy-start.3
  36.2 3.3 copy-start.25
  36.5 0.6 copy-start.14
  37.1 0.6 copy-start.20
  39.5 2.6 copy-start.26
  42.1 1.0 copy-start.5
  42.7 0.6 copy-start.12
  44.9 68.3 %copy-start.1 = (bf16[1,1024,512]{2,1,0:T(8,128)(2,1)S(1)}, bf16[1,1024,512]{2,1,0:T(8,128)(2,1)}, u32[]{:S(2)}) copy-start(bf16[1,1024,512]{2,1,0:T(8,128)(2,1)} %param.23) | copy-start | bytes 3145732
  451.7 6.1 copy-start.16
  451.7 6.1 copy-start.17
  451.7 190.0 %all-to-all-start.2 = ((bf16[128,128,512]{2,1,0:T(8,128)(2,1)}), bf16[128,128,512]{2,1,0:T(8,128)(2,1)}, u32[]{:S(2)}, u32[]{:S(2)}) async-start(bf16[128,128,512]{2,1,0:T(8,128)(2,1)} %bitcast.186), calls=%async_computation.2 | async-start | bytes 33554432 | tf_op jit(solution)/shard_map/all_to_all | solution.py:105
  458.4 0.6 copy-start.10
  641.7 189.9 %all-to-all-start = ((bf16[128,128,512]{2,1,0:T(8,128)(2,1)}), bf16[128,128,512]{2,1,0:T(8,128)(2,1)}, u32[]{:S(2)}, u32[]{:S(2)}) async-start(bf16[128,128,512]{2,1,0:T(8,128)(2,1)} %bitcast.185), calls=%async_computation | async-start | bytes 33554432 | tf_op jit(solution)/shard_map/all_to_all | solution.py:91
  831.6 190.2 %all-to-all-start.4 = ((bf16[16,1024,512]{2,0,1:T(8,128)(2,1)}), bf16[16,1024,512]{2,0,1:T(8,128)(2,1)}, u32[]{:S(2)}, u32[]{:S(2)}) async-start(bf16[16,1024,512]{2,0,1:T(8,128)(2,1)} %copy.74), calls=%async_computation.4 | async-start | bytes 33554432 | tf_op jit(solution)/shard_map/all_to_all | solution.py:107
  919.8 107.9 %copy-start.2 = (bf16[1,1024,512]{2,1,0:T(8,128)(2,1)S(1)}, bf16[1,1024,512]{2,1,0:T(8,128)(2,1)}, u32[]{:S(2)}) copy-start(bf16[1,1024,512]{2,1,0:T(8,128)(2,1)} %param.23) | copy-start | bytes 3145732
  919.8 109.3 %copy-start.18 = (pred[1024,8]{0,1:T(8,128)(4,1)S(1)}, pred[1024,8]{0,1:T(8,128)(4,1)}, u32[]{:S(2)}) copy-start(pred[1024,8]{0,1:T(8,128)(4,1)} %get-tuple-element.22) | copy-start | bytes 24580
  919.8 109.5 %copy-start.19 = (pred[1024,8]{0,1:T(8,128)(4,1)S(1)}, pred[1024,8]{0,1:T(8,128)(4,1)}, u32[]{:S(2)}) copy-start(pred[1024,8]{0,1:T(8,128)(4,1)} %get-tuple-element.24) | copy-start | bytes 24580
  919.8 110.4 %copy-start.9 = (s32[1,1024,8]{1,2,0:T(8,128)S(1)}, s32[1,1024,8]{1,2,0:T(8,128)}, u32[]{:S(2)}) copy-start(s32[1,1024,8]{1,2,0:T(8,128)} %copy-done.8) | copy-start | bytes 98308
  919.8 110.8 %copy-start.11 = (s32[1,1024,8]{1,2,0:T(8,128)S(1)}, s32[1,1024,8]{1,2,0:T(8,128)}, u32[]{:S(2)}) copy-start(s32[1,1024,8]{1,2,0:T(8,128)} %copy-done.10) | copy-start | bytes 98308
  919.8 111.3 %copy-start.22 = (bf16[1,1024,8]{1,2,0:T(8,128)(2,1)S(1)}, bf16[1,1024,8]{1,2,0:T(8,128)(2,1)}, u32[]{:S(2)}) copy-start(bf16[1,1024,8]{1,2,0:T(8,128)(2,1)} %param.21) | copy-start | bytes 49156
  1021.8 189.9 %all-to-all-start.1 = ((bf16[16,1024,512]{2,0,1:T(8,128)(2,1)}), bf16[16,1024,512]{2,0,1:T(8,128)(2,1)}, u32[]{:S(2)}, u32[]{:S(2)}) async-start(bf16[16,1024,512]{2,0,1:T(8,128)(2,1)} %copy.62), calls=%async_computation.1 | async-start | bytes 33554432 | tf_op jit(solution)/shard_map/all_to_all | solution.py:93
  1138.9 14.4 %copy-start.24 = (f32[1024]{0:T(1024)S(1)}, f32[1024]{0:T(1024)}, u32[]{:S(2)}) copy-start(f32[1024]{0:T(1024)} %copy-done.23) | copy-start | bytes 12292
  1138.9 14.4 %copy-start.4 = (bf16[1,1024,512]{1,2,0:T(8,128)(2,1)S(1)}, bf16[1,1024,512]{1,2,0:T(8,128)(2,1)}, u32[]{:S(2)}) copy-start(bf16[1,1024,512]{1,2,0:T(8,128)(2,1)} %copy-done.3) | copy-start | bytes 3145732
  1138.9 14.4 %copy-start.13 = (f32[1024]{0:T(1024)S(1)}, f32[1024]{0:T(1024)}, u32[]{:S(2)}) copy-start(f32[1024]{0:T(1024)} %copy-done.12) | copy-start | bytes 12292
  1153.3 10.3 copy-start.15
  1153.3 10.3 copy-start.21
  1168.5 144.9 %collective-permute-start.1 = (bf16[1024,512]{0,1:T(8,128)(2,1)}, bf16[1024,512]{0,1:T(8,128)(2,1)}, u32[]{:S(2)}, u32[]{:S(2)}) collective-permute-start(bf16[1024,512]{0,1:T(8,128)(2,1)} %fusion.48), channel_id=1, source_target_pairs={{0,8},{8,0},{1,9},{9,1},{2,10},{10,2},{3,11},{11,3},{4,12},{12,4},... | collective-permute-start | bytes 3145736 | tf_op jit(solution)/shard_map/ppermute | solution.py:114
  1230.4 41.9 %copy-start.7 = (pred[1024,8]{1,0:T(8,128)(4,1)S(1)}, pred[1024,8]{1,0:T(8,128)(4,1)}, u32[]{:S(2)}) copy-start(pred[1024,8]{1,0:T(8,128)(4,1)} %copy.58) | copy-start | bytes 24580
  1272.3 17.0 %copy-start.6 = (bf16[1024,512]{0,1:T(8,128)(2,1)S(1)}, bf16[1024,512]{0,1:T(8,128)(2,1)}, u32[]{:S(2)}) copy-start(bf16[1024,512]{0,1:T(8,128)(2,1)} %get-tuple-element.31) | copy-start | bytes 3145732
  1292.3 23.4 %collective-permute-start = (bf16[1024,512]{0,1:T(8,128)(2,1)}, bf16[1024,512]{0,1:T(8,128)(2,1)S(1)}, u32[]{:S(2)}, u32[]{:S(2)}) collective-permute-start(bf16[1024,512]{0,1:T(8,128)(2,1)} %fusion.45), channel_id=1, source_target_pairs={{0,8},{8,0},{1,9},{9,1},{2,10},{10,2},{3,11},{11,3},{4,12},{12,4},... | collective-permute-start | bytes 3145736 | tf_op jit(solution)/shard_map/ppermute | solution.py:113
  (1 other events, 0.6 us)
where the time goes:
time: 1330 us; the launch traced here: 1320 us
  local copies, waits for them, and re-layouts  542 us (41%)
  matrix products  253 us (19%)
  waiting for transfers between devices  223 us (17%)
  blocking collectives  192 us (14%)
  other arithmetic  77.3 us (6%)
  starting transfers between devices  28.7 us (2%)
    all_to_all x1, blocking collectives, device_step(): recv_rows = lax.all_to_all(send_rows, 'ep', 0, 1, tiled=True)  192 us
    all_to_all x1, waiting for transfers between devices, device_step(): lax.all_to_all(grad_rows, 'ep', 1, 0, tiled=True).reshape(n_rows, hidden)  102 us
    gather x1, local copies, waits for them, and re-layouts, device_step(): jnp.take(xn_bwd, tok_bwd, axis=0, mode='fill', fill_value=0)  68.3 us
    gather x1, local copies, waits for them, and re-layouts, device_step(): jnp.take(xn_fwd, tok_fwd, axis=0, mode='fill', fill_value=0)  66.4 us
    gather x1, local copies, waits for them, and re-layouts, device_step(): jnp.take(grad_in, tok_bwd, axis=0, mode='fill', fill_value=0)  66.1 us
    scatter x2, local copies, waits for them, and re-layouts, route_maps(): jnp.full((n_experts * cap_rows,), tok_rows, jnp.int32)  61 us
    all_to_all x1, waiting for transfers between devices, device_step(): recv_grad = lax.all_to_all(send_grad, 'ep', 0, 1, tiled=True)  59 us
    scatter x1, local copies, waits for them, and re-layouts, device_step(): jnp.zeros((n_rows,), jnp.bfloat16).at[row_bwd.reshape(-1)]  56.6 us
  transfers between devices with their start and end apart: 6, of which 4 were waited for; matrix products, arithmetic and copies ran while one was open for 46% of the time, Pallas kernels for 0%

commit v1 on v0

v1 whole, which is shorter than its diff:
```python
import functools

import jax
import jax.numpy as jnp
from jax import lax
from jax.experimental import pallas as pl
from jax.experimental.pallas import tpu as pltpu
from jax.sharding import PartitionSpec as P

NORM_EPS = 1e-6
CHUNK = 16
ROW_TILE = 256
VMEM_BYTES = 66_500_000
BF16 = jnp.bfloat16
F32 = jnp.float32


def rms_norm(values):
    return values * lax.rsqrt(jnp.mean(values * values, axis=-1, keepdims=True) + NORM_EPS)


def silu_grad(values):
    sigmoid_vals = jax.nn.sigmoid(values)
    return sigmoid_vals * (1.0 + values * (1.0 - sigmoid_vals))


def dense_forward(x_rows, w_one, w_two):
    normed = rms_norm(x_rows.astype(F32)).astype(BF16)
    hidden_pre = jnp.dot(normed, w_one, preferred_element_type=F32)
    dense_act = jax.nn.silu(hidden_pre).astype(BF16)
    dense_out = jnp.dot(dense_act, w_two, preferred_element_type=F32)
    return (x_rows.astype(F32) + dense_out).astype(BF16), hidden_pre


def dense_backward(x_rows, hidden_pre, w_one, w_two, grad_h):
    _, norm_vjp = jax.vjp(rms_norm, x_rows.astype(F32))
    grad_act = jnp.einsum("th,fh->tf", grad_h.astype(BF16), w_two, preferred_element_type=F32)
    grad_pre = (grad_act * silu_grad(hidden_pre)).astype(BF16)
    grad_norm = jnp.einsum("tf,hf->th", grad_pre, w_one, preferred_element_type=F32)
    return grad_h + norm_vjp(grad_norm)[0]


def dot_nn(lhs, rhs):
    return jnp.dot(lhs, rhs, preferred_element_type=F32)


def dot_nt(lhs, rhs):
    return lax.dot_general(lhs, rhs, (((1,), (1,)), ((), ())), preferred_element_type=F32)


def dot_tn(lhs, rhs):
    return lax.dot_general(lhs, rhs, (((0,), (0,)), ((), ())), preferred_element_type=F32)


def rows_at(index, count):
    return pl.ds(pl.multiple_of(index, CHUNK), count)


def fill_onehot(hot_ref, pos_ref, gate_ref, chunks_ref, src, n_local):
    tok_rows = pos_ref.shape[2]
    iota = lax.broadcasted_iota(jnp.int32, (CHUNK, tok_rows), 0)
    start = jnp.int32(0)
    for expert in range(n_local):
        pos_row = pos_ref[src, pl.ds(expert, 1), :]
        value = 1.0 if gate_ref is None else gate_ref[src, pl.ds(expert, 1), :]
        n_chunks = chunks_ref[src, expert]

        def body(c, carry, pos_row=pos_row, value=value, start=start):
            hot = jnp.where(iota + c * CHUNK == pos_row, value, 0.0)
            hot_ref[rows_at(start + c * CHUNK, CHUNK), :] = hot.astype(BF16)
            return carry

        lax.fori_loop(0, n_chunks, body, 0)
        start = start + n_chunks * CHUNK
    return start


def zero_tail(ref, offset, length, tile):
    n_tiles = (length + tile - 1) // tile

    def body(c, carry):
        ref[rows_at(offset + c * CHUNK, CHUNK), :] = jnp.zeros((CHUNK, ref.shape[1]), ref.dtype)
        return carry

    lax.fori_loop(length // CHUNK, n_tiles * (tile // CHUNK), body, 0)
    return n_tiles


def move_segments(pack_ref, wide_ref, base_ref, chunks_ref, src, n_local, cap, to_wide):
    start = jnp.int32(0)
    for expert in range(n_local):
        n_chunks = chunks_ref[src, expert]
        base = expert * cap + base_ref[src, expert]

        def body(c, carry, start=start, base=base):
            pack_rows = rows_at(start + c * CHUNK, CHUNK)
            wide_rows = rows_at(base + c * CHUNK, CHUNK)
            if to_wide:
                wide_ref[wide_rows, :] = pack_ref[pack_rows, :]
            else:
                pack_ref[pack_rows, :] = wide_ref[wide_rows, :]
            return carry

        lax.fori_loop(0, n_chunks, body, 0)
        start = start + n_chunks * CHUNK


def expert_bases(base_ref, total_ref, chunks_ref, n_src, n_local):
    for expert in range(n_local):
        total_ref[expert] = 0

    def body(src, carry):
        for expert in range(n_local):
            base_ref[src, expert] = total_ref[expert]
            total_ref[expert] = total_ref[expert] + chunks_ref[src, expert] * CHUNK
        return carry

    lax.fori_loop(0, n_src, body, 0)


def dispatch(pack_ref, hot_ref, table_ref, wide_ref, base_ref, chunks_ref, src, n_local, cap, length):
    def body(tile, carry):
        rows = rows_at(tile * ROW_TILE, ROW_TILE)
        pack_ref[rows, :] = dot_nn(hot_ref[rows, :], table_ref[...]).astype(BF16)
        return carry

    lax.fori_loop(0, (length + ROW_TILE - 1) // ROW_TILE, body, 0)
    move_segments(pack_ref, wide_ref, base_ref, chunks_ref, src, n_local, cap, True)


def combine(out_ref, pack_ref, hot_ref, wide_ref, base_ref, chunks_ref, src, n_local, cap, length, tile):
    move_segments(pack_ref, wide_ref, base_ref, chunks_ref, src, n_local, cap, False)
    n_tiles = zero_tail(pack_ref, 0, length, tile)
    zero_tail(hot_ref, 0, length, tile)
    out_ref[...] = jnp.zeros_like(out_ref)

    def body(step, carry):
        rows = rows_at(step * tile, tile)
        out_ref[...] += dot_tn(hot_ref[rows, :], pack_ref[rows, :])
        return carry

    lax.fori_loop(0, n_tiles, body, 0)


def weight_copies(expert, slot, wg_ref, wu_ref, wd_ref, gu_buf, dn_buf, sems):
    ff = wg_ref.shape[2]
    return (
        pltpu.make_async_copy(wg_ref.at[expert], gu_buf.at[slot, :, pl.ds(0, ff)], sems.at[slot, 0]),
        pltpu.make_async_copy(wu_ref.at[expert], gu_buf.at[slot, :, pl.ds(ff, ff)], sems.at[slot, 1]),
        pltpu.make_async_copy(wd_ref.at[expert], dn_buf.at[slot], sems.at[slot, 2]),
    )


def next_weights(expert, n_local, *refs):
    slot = lax.rem(expert, 2)

    @pl.when(expert + 1 < n_local)
    def _():
        for copy in weight_copies(expert + 1, lax.rem(expert + 1, 2), *refs):
            copy.start()

    for copy in weight_copies(expert, slot, *refs):
        copy.wait()
    return slot


def forward_kernel(n_src, n_local, cap, chunks_ref, tok_ref, pos_ref, gate_ref, wg_ref, wu_ref, wd_ref, out_ref,
                   wide, hot, pack, gu_buf, dn_buf, base, total, sems):
    step = pl.program_id(0)
    ff = wg_ref.shape[2]
    w_refs = (wg_ref, wu_ref, wd_ref, gu_buf, dn_buf, sems)

    @pl.when(step == 0)
    def _():
        for copy in weight_copies(0, 0, *w_refs):
            copy.start()
        expert_bases(base, total, chunks_ref, n_src, n_local)

    @pl.when(step < n_src)
    def _():
        length = fill_onehot(hot, pos_ref, None, chunks_ref, step, n_local)
        dispatch(pack, hot, tok_ref, wide, base, chunks_ref, step, n_local, cap, length)

    @pl.when((step >= n_src) & (step < n_src + n_local))
    def _():
        expert = step - n_src
        slot = next_weights(expert, n_local, *w_refs)

        def body(tile, carry):
            rows = rows_at(expert * cap + tile * ROW_TILE, ROW_TILE)
            pre = dot_nn(wide[rows, :], gu_buf[slot])
            gate = pre[:, :ff]
            act = (gate * jax.nn.sigmoid(gate) * pre[:, ff:]).astype(BF16)
            wide[rows, :] = dot_nn(act, dn_buf[slot]).astype(BF16)
            return carry

        lax.fori_loop(0, (total[expert] + ROW_TILE - 1) // ROW_TILE, body, 0)

    @pl.when(step >= n_src + n_local)
    def _():
        src = step - n_src - n_local
        length = fill_onehot(hot, pos_ref, gate_ref, chunks_ref, src, n_local)
        combine(out_ref, pack, hot, wide, base, chunks_ref, src, n_local, cap, length, 2 * ROW_TILE)


def backward_kernel(n_src, n_local, cap, chunks_ref, tok_ref, grad_ref, pos_ref, gate_ref, wg_ref, wu_ref, wd_ref,
                    out_ref, dwg_ref, dwu_ref, dwd_ref,
                    wide_x, wide_q, hot, pack, gu_buf, dn_buf, base, total, sems):
    step = pl.program_id(0)
    ff = wg_ref.shape[2]
    w_refs = (wg_ref, wu_ref, wd_ref, gu_buf, dn_buf, sems)

    @pl.when(step == 0)
    def _():
        for copy in weight_copies(0, 0, *w_refs):
            copy.start()
        expert_bases(base, total, chunks_ref, n_src, n_local)

    @pl.when(step < n_src)
    def _():
        length = fill_onehot(hot, pos_ref, None, chunks_ref, step, n_local)
        dispatch(pack, hot, tok_ref, wide_x, base, chunks_ref, step, n_local, cap, length)
        fill_onehot(hot, pos_ref, gate_ref, chunks_ref, step, n_local)
        dispatch(pack, hot, grad_ref, wide_q, base, chunks_ref, step, n_local, cap, length)

    @pl.when((step >= n_src) & (step < n_src + n_local))
    def _():
        expert = step - n_src
        slot = next_weights(expert, n_local, *w_refs)
        n_tiles = zero_tail(wide_x, expert * cap, total[expert], ROW_TILE)
        zero_tail(wide_q, expert * cap, total[expert], ROW_TILE)
        dwg_ref[...] = jnp.zeros_like(dwg_ref)
        dwu_ref[...] = jnp.zeros_like(dwu_ref)
        dwd_ref[...] = jnp.zeros_like(dwd_ref)

        def body(tile, carry):
            rows = rows_at(expert * cap + tile * ROW_TILE, ROW_TILE)
            x_rows = wide_x[rows, :]
            q_rows = wide_q[rows, :]
            pre = dot_nn(x_rows, gu_buf[slot])
            gate, up = pre[:, :ff], pre[:, ff:]
            sig = jax.nn.sigmoid(gate)
            silu = gate * sig
            act = (silu * up).astype(BF16)
            grad_act = dot_nt(q_rows, dn_buf[slot]).astype(BF16).astype(F32)
            grad_gate = (grad_act * up * (sig * (1.0 + gate * (1.0 - sig)))).astype(BF16)
            grad_up = (grad_act * silu).astype(BF16)
            grad_pre = jnp.concatenate([grad_gate, grad_up], axis=1)
            dwd_ref[0] += dot_tn(act, q_rows)
            dw_pre = dot_tn(x_rows, grad_pre)
            dwg_ref[0] += dw_pre[:, :ff]
            dwu_ref[0] += dw_pre[:, ff:]
            wide_x[rows, :] = dot_nt(grad_pre, gu_buf[slot]).astype(BF16)
            return carry

        lax.fori_loop(0, n_tiles, body, 0)

    @pl.when(step >= n_src + n_local)
    def _():
        src = step - n_src - n_local
        length = fill_onehot(hot, pos_ref, None, chunks_ref, src, n_local)
        combine(out_ref, pack, hot, wide_x, base, chunks_ref, src, n_local, cap, length, 2 * ROW_TILE)


def expert_call(backward, chunks, tables, pos, gate, w_gate, w_up, w_down):
    n_src, n_local, tok_rows = pos.shape
    hidden, ff = w_gate.shape[1:]
    cap = n_src * 128
    pack_rows = n_local * 128
    steps = 2 * n_src + n_local

    def src_in(i, *_):
        return (jnp.minimum(i, n_src - 1), 0)

    def src_out(i, *_):
        return (jnp.clip(i - n_src - n_local, 0, n_src - 1), 0)

    def weight_out(i, *_):
        return (jnp.clip(i - n_src, 0, n_local - 1), 0, 0)

    table_spec = pl.BlockSpec((tok_rows, hidden), src_in)
    whole = pl.BlockSpec(pos.shape, lambda i, *_: (0, 0, 0), pipeline_mode=pl.Buffered(1))
    raw = pl.BlockSpec(memory_space=pl.ANY)
    out_shape = [jax.ShapeDtypeStruct((n_src * tok_rows, hidden), F32)]
    out_specs = [pl.BlockSpec((tok_rows, hidden), src_out)]
    wide = pltpu.VMEM((n_local * cap, hidden), BF16)
    scratch = [wide]
    if backward:
        out_shape += [jax.ShapeDtypeStruct(w.shape, F32) for w in (w_gate, w_up, w_down)]
        out_specs += [pl.BlockSpec((1,) + w.shape[1:], weight_out) for w in (w_gate, w_up, w_down)]
        scratch += [wide]
    scratch += [
        pltpu.VMEM((pack_rows, tok_rows), BF16),
        pltpu.VMEM((pack_rows, hidden), BF16),
        pltpu.VMEM((2, hidden, 2 * ff), BF16),
        pltpu.VMEM((2, ff, hidden), BF16),
        pltpu.SMEM((n_src, n_local), jnp.int32),
        pltpu.SMEM((n_local,), jnp.int32),
        pltpu.SemaphoreType.DMA((2, 3)),
    ]
    body = backward_kernel if backward else forward_kernel
    flops = (100 if backward else 60) * 10 ** 9
    return pl.pallas_call(
        functools.partial(body, n_src, n_local, cap),
        grid_spec=pltpu.PrefetchScalarGridSpec(
            num_scalar_prefetch=1,
            grid=(steps,),
            in_specs=[table_spec] * len(tables) + [whole, whole, raw, raw, raw],
            out_specs=out_specs,
            scratch_shapes=scratch,
        ),
        out_shape=out_shape,
        compiler_params=pltpu.CompilerParams(dimension_semantics=("arbitrary",), vmem_limit_bytes=VMEM_BYTES),
        cost_estimate=pl.CostEstimate(flops=flops, bytes_accessed=60 * 10 ** 6, transcendentals=0),
        name="expert_backward" if backward else "expert_forward",
    )(chunks, *tables, pos, gate, w_gate, w_up, w_down)


def route_tables(ids, gates, first, n_local):
    tok_rows = ids.shape[2]
    experts = (first + jnp.arange(n_local)).astype(F32)
    match = ids[:, None] == experts[None, :, None, None]
    kept = jnp.any(match, axis=2)
    gate = jnp.sum(jnp.where(match, gates[:, None], 0.0), axis=2)
    upper = (jnp.arange(tok_rows)[:, None] <= jnp.arange(tok_rows)[None, :]).astype(BF16)
    rank = jnp.einsum("set,tu->seu", kept.astype(BF16), upper, preferred_element_type=F32)
    pos = jnp.where(kept, rank - 1.0, -1.0).astype(jnp.int32)
    chunks = (rank[:, :, -1].astype(jnp.int32) + CHUNK - 1) // CHUNK
    return pos, gate, chunks


def solution(mesh):
    stages = mesh.shape["pp"]
    ep_size = mesh.shape["ep"]
    next_perm = [(stage_idx, (stage_idx + 1) % stages) for stage_idx in range(stages)]
    prev_perm = [(stage_idx, (stage_idx - 1) % stages) for stage_idx in range(stages)]
    tok_spec = P("pp", "ep", None)
    dense_spec = P("pp", None, None)
    expert_spec = P("pp", "ep", None, None)

    def device_step(x_fwd, ids_fwd, slots_fwd, gates_fwd, x_saved, grad_in, ids_bwd, slots_bwd, gates_bwd, w_one, w_two, w_gate, w_up, w_down):
        x_fwd, ids_fwd, slots_fwd, gates_fwd = x_fwd[0], ids_fwd[0], slots_fwd[0], gates_fwd[0]
        x_saved, grad_in, ids_bwd, slots_bwd, gates_bwd = x_saved[0], grad_in[0], ids_bwd[0], slots_bwd[0], gates_bwd[0]
        w_one, w_two, w_gate, w_up, w_down = w_one[0], w_two[0], w_gate[0], w_up[0], w_down[0]
        top_k = ids_fwd.shape[1]
        n_local = w_gate.shape[0]
        first = lax.axis_index("ep") * n_local

        routes = jnp.concatenate([
            jnp.where(slots_fwd >= 0, ids_fwd, -1).astype(F32), gates_fwd.astype(F32),
            jnp.where(slots_bwd >= 0, ids_bwd, -1).astype(F32), gates_bwd.astype(F32),
        ], axis=1).T
        routes = lax.all_gather(routes, "ep", axis=0, tiled=False)
        id_f, gate_f, id_b, gate_b = (routes[:, i * top_k:(i + 1) * top_k] for i in range(4))
        pos_f, gate_f, chunks_f = route_tables(id_f, gate_f, first, n_local)
        pos_b, gate_b, chunks_b = route_tables(id_b, gate_b, first, n_local)

        h_fwd, _ = dense_forward(x_fwd, w_one, w_two)
        xn_fwd = rms_norm(h_fwd.astype(F32)).astype(BF16)
        all_fwd = lax.all_gather(xn_fwd, "ep", axis=0, tiled=True)
        all_grad = lax.all_gather(grad_in, "ep", axis=0, tiled=True)
        h_bwd, hidden_pre = dense_forward(x_saved, w_one, w_two)
        xn_bwd = rms_norm(h_bwd.astype(F32)).astype(BF16)
        all_bwd = lax.all_gather(xn_bwd, "ep", axis=0, tiled=True)

        (part_fwd,) = expert_call(False, chunks_f, (all_fwd,), pos_f, gate_f, w_gate, w_up, w_down)
        mix_sum = lax.psum_scatter(part_fwd, "ep", scatter_dimension=0, tiled=True)
        y_out = (h_fwd.astype(F32) + mix_sum).astype(BF16)

        part_bwd, dw_gate, dw_up, dw_down = expert_call(True, chunks_b, (all_bwd, all_grad), pos_b, gate_b, w_gate, w_up, w_down)
        grad_xn = lax.psum_scatter(part_bwd, "ep", scatter_dimension=0, tiled=True)
        _, rms_vjp = jax.vjp(rms_norm, h_bwd.astype(F32))
        grad_h = grad_in.astype(F32) + rms_vjp(grad_xn)[0]
        grad_x = dense_backward(x_saved, hidden_pre, w_one, w_two, grad_h).astype(BF16)

        y_next = lax.ppermute(y_out, "pp", next_perm)
        dx_prev = lax.ppermute(grad_x, "pp", prev_perm)
        return y_next[None], dx_prev[None], dw_gate[None], dw_up[None], dw_down[None]

    in_specs = (tok_spec,) * 9 + (dense_spec, dense_spec, expert_spec, expert_spec, expert_spec)
    out_specs = (tok_spec, tok_spec, expert_spec, expert_spec, expert_spec)
    return jax.shard_map(device_step, mesh=mesh, in_specs=in_specs, out_specs=out_specs, check_vma=False)
```

time: 1330 us -> 561 us (0.42); the launches traced: 1320 us -> 565 us
  local copies, waits for them, and re-layouts: 542 us -> 6.42 us
  matrix products: 253 us -> 23.9 us
  blocking collectives: 192 us -> 0 us
  Pallas kernels: 0 us -> 177 us
  waiting for transfers between devices: 223 us -> 317 us
  other arithmetic: 77.3 us -> 23.1 us
  starting transfers between devices: 28.7 us -> 3.62 us
    gather x5 -> x0, local copies, waits for them, and re-layouts: 285 us -> none  [the longest x1 68.3 us: device_step(): jnp.take(xn_bwd, tok_bwd, axis=0, mode='fill', fill_value=0)]
    dot_general x14 -> x6, matrix products: 253 us -> 23.9 us  [the longest x1 9.91 us: dense_backward(): jnp.einsum('tf,hf->th', grad_pre, w_one, preferred_element_type=F32)]
    all_to_all x4 -> x0, waiting for transfers between devices: 223 us -> none  [the longest x1 102 us: device_step(): lax.all_to_all(grad_rows, 'ep', 1, 0, tiled=True).reshape(n_rows, hidden)]
    reduce_scatter x0 -> x2, waiting for transfers between devices: none -> 195 us  [the longest x1 99.6 us: device_step(): grad_xn = lax.psum_scatter(part_bwd, 'ep', scatter_dimension=0, tiled=True)]
    all_to_all x1 -> x0, blocking collectives: 192 us -> none  [device_step(): recv_rows = lax.all_to_all(send_rows, 'ep', 0, 1, tiled=True)]
    pallas_call x0 -> x2, Pallas kernels: none -> 177 us  [expert_call(): pl.pallas_call(functools.partial(body, n_src, n_local, cap), grid_spec=pl...]
    scatter x3 -> x0, local copies, waits for them, and re-layouts: 118 us -> none  [the longest x2 61 us: route_maps(): jnp.full((n_experts * cap_rows,), tok_rows, jnp.int32)]
    all_gather x0 -> x4, waiting for transfers between devices: none -> 97.3 us  [the longest x1 52 us: device_step(): all_grad = lax.all_gather(grad_in, 'ep', axis=0, tiled=True)]
  transfers between devices with their start and end apart: 6 -> 8, of which waited for: 4 -> 6; matrix products, arithmetic and copies ran while one was open for 46% -> 8% of each run, Pallas kernels for 0% -> 31%
where the time goes in v1:
time: 561 us; the launch traced here: 565 us
  waiting for transfers between devices  317 us (57%)
  Pallas kernels  177 us (32%)
  matrix products  23.9 us (4%)
  other arithmetic  23.1 us (4%)
  between operations  14.3 us (3%)
  local copies, waits for them, and re-layouts  6.42 us (1%)
    pallas_call x2, Pallas kernels, expert_call(): pl.pallas_call(functools.partial(body, n_src, n_local, cap), grid_spec=pl...  177 us
    reduce_scatter x1, waiting for transfers between devices, device_step(): grad_xn = lax.psum_scatter(part_bwd, 'ep', scatter_dimension=0, tiled=True)  99.6 us
    reduce_scatter x1, waiting for transfers between devices, device_step(): mix_sum = lax.psum_scatter(part_fwd, 'ep', scatter_dimension=0, tiled=True)  95.9 us
    all_gather x1, waiting for transfers between devices, device_step(): all_grad = lax.all_gather(grad_in, 'ep', axis=0, tiled=True)  52 us
    all_gather x1, waiting for transfers between devices, device_step(): all_bwd = lax.all_gather(xn_bwd, 'ep', axis=0, tiled=True)  42.2 us
    ppermute x1, waiting for transfers between devices, device_step(): y_next = lax.ppermute(y_out, 'pp', next_perm)  23.2 us
  transfers between devices with their start and end apart: 8, of which 6 were waited for; matrix products, arithmetic and copies ran while one was open for 8% of the time, Pallas kernels for 31%

profile of v1, /device:TPU:0, one launch (start us, length us, event | category | flops | bytes accessed | tf_op | source)
XLA Modules:
  0.0 564.9 jit_solution(16888880446661541238)
XLA Ops:
  7.2 0.7 bitcast_convert_fusion
  8.0 0.8 convert_bitcast_fusion.2
  8.8 0.7 maximum_bitcast_fusion
  9.5 1.5 fusion.20
  12.2 3.7 fusion.39
  16.0 2.0 fusion.30
  18.0 0.7 copy-done.15
  19.9 1.3 fusion.31
  21.2 0.7 all-gather.13.cloned.1.call-update
  22.2 5.7 %fusion.24 = (f32[1024]{0:T(1024)S(1)}, bf16[1024,512]{1,0:T(8,128)(2,1)S(1)}) fusion(bf16[1,1536,512]{2,1,0:T(8,128)(2,1)} %param.24, bf16[1,512,1536]{2,1,0:T(8,128)(2,1)} %param.23, bf16[1,1024,512]{2,1,0:T(8,128)(2,1)S(1)} %copy-done.5, f32[1024]{0:T(1024)S(1)} %add_rsqrt_fusion.1), kind=kOutput, calls=%fused_computation.43 | convolution fusion | flops 3233807360 | bytes 5251072 | tf_op jit(solution)/shard_map/dot_general | solution.py:31
  27.9 1.3 fusion.25
  29.5 3.1 all-gather.11.cloned.1.call-done
  32.6 1.3 fusion.74
  33.9 3.4 compare_reduce_fusion
  37.3 1.3 select_convert_fusion
  39.5 3.6 fusion.1
  43.1 42.2 %all-gather.9.cloned.1.call-done.tok_ref = bf16[8192,512]{1,0:T(8,128)(2,1)} async-done(((bf16[1024,512]{1,0:T(8,128)(2,1)}), bf16[8192,512]{1,0:T(8,128)(2,1)}) %all-gather.9.cloned.1.call-update) | async-done | bytes 8388624 | tf_op jit(solution)/shard_map/all_gather | solution.py:364
  85.3 52.0 %all-gather.13.cloned.1.call-done = bf16[1,8192,512]{2,1,0:T(8,128)(2,1)} async-done(((bf16[1,1024,512]{2,1,0:T(8,128)(2,1)}), bf16[1,8192,512]{2,1,0:T(8,128)(2,1)}) %all-gather.13.cloned.1.call-update) | async-done | bytes 8388624 | tf_op jit(solution)/shard_map/all_gather | solution.py:361
  137.3 111.4 %expert_backward.1 = (f32[8192,512]{1,0:T(8,128)}, f32[16,512,384]{2,1,0:T(8,128)}, f32[16,512,384]{2,1,0:T(8,128)}, f32[16,384,512]{2,1,0:T(8,128)}) custom-call(s32[8,16]{1,0:T(8,128)} %add_select_fusion.chunks_ref, bf16[8192,512]{1,0:T(8,128)(2,1)} %all-gather.9.cloned.1.call-done.tok_ref, bf16[8192,512]{1,0:T(8,128)(2,1)} %bitcast.119, ...), custom_call_target="tpu_custom_call" | custom-call | flops 99999997952 | bytes 60000000 | tf_op jit(solution)/shard_map/expert_backward/pallas_call | solution.py:303
  249.0 1.3 select_convert_fusion.1
  251.1 65.4 %expert_forward.1 = f32[8192,512]{1,0:T(8,128)} custom-call(s32[8,16]{1,0:T(8,128)} %add_select_fusion.1.chunks_ref, bf16[8192,512]{1,0:T(8,128)(2,1)} %all-gather.7.cloned.1.call-done.tok_ref, s32[8,16,1024]{2,1,0:T(8,128)} %get-tuple-element.23.pos_ref, f32[8,16,1024]{2,1,0:T(8,128)} %get-tuple-element.14.gate_ref, bf16[16,512,384]{2,1,0:T(8,128)(2,1)} %bitcast.121, ...), custom_call_target="tpu_custom_call" | custom-call | flops 60000002048 | bytes 60000000 | tf_op jit(solution)/shard_map/expert_forward/pallas_call | solution.py:303
  316.6 99.6 %reduce-scatter.5.cloned.1.call-done = f32[1024,512]{1,0:T(8,128)} async-done(((f32[8192,512]{1,0:T(8,128)}), f32[1024,512]{1,0:T(8,128)}) %reduce-scatter.5.cloned.1.call-update) | async-done | bytes 2097168 | tf_op jit(solution)/shard_map/reduce_scatter | solution.py:371
  416.1 2.0 fusion.32
  418.4 9.9 %fusion.22 = (f32[1024]{0:T(1024)S(1)}, f32[1024,512]{1,0:T(8,128)}) fusion(bf16[1,1024,512]{2,1,0:T(8,128)(2,1)} %param.18, bf16[1,512,1536]{2,1,0:T(8,128)(2,1)} %param.23, f32[1024,1536]{1,0:T(8,128)} %copy-done.15, bf16[1,1536,512]{2,1,0:T(8,128)(2,1)} %param.24, bf16[1024,512]{1,0:T(8,128)(2,1)S(1)} %copy-done.1, f32[1024,512]{1,0:T(8,128)S(1)} %copy-done.2, ...), kind=kOutput, calls=%fused_computation.41 | convolution fusion | flops 3241147392 | bytes 16789504 | tf_op jit(solution)/shard_map/tf,hf->th/dot_general | solution.py:39
  428.3 3.5 fusion.29
  431.8 1.5 collective-permute-start.1
  433.3 95.9 %reduce-scatter.3.cloned.1.call-done = f32[1024,512]{1,0:T(8,128)} async-done(((f32[8192,512]{1,0:T(8,128)}), f32[1024,512]{1,0:T(8,128)}) %reduce-scatter.3.cloned.1.call-update) | async-done | bytes 2097168 | tf_op jit(solution)/shard_map/reduce_scatter | solution.py:367
  529.2 2.2 fusion.26
  531.4 1.5 collective-permute-start
  532.9 23.2 %collective-permute-done = bf16[1024,512]{1,0:T(8,128)(2,1)S(1)} collective-permute-done((bf16[1024,512]{1,0:T(8,128)(2,1)S(1)}, bf16[1024,512]{1,0:T(8,128)(2,1)S(1)}, u32[]{:S(2)}, u32[]{:S(2)}) %collective-permute-start) | collective-permute-done | bytes 1048608 | tf_op jit(solution)/shard_map/ppermute | solution.py:376
  556.1 1.0 copy.36
  557.1 1.0 copy.37
  (56 shorter events, 5.4 us)
Async XLA Ops:
  7.2 25.4 %all-gather.11.cloned.1.call-start = ((), (), s32[]{:S(2)}) async-start(), calls=%async_computation.6 | async-start | bytes 1179648 | tf_op jit(solution)/shard_map/all_gather | solution.py:353
  9.5 75.8 %all-gather.9.cloned.1.call-start = ((), (), s32[]{:S(2)}) async-start(), calls=%async_computation.4 | async-start | bytes 9437184 | tf_op jit(solution)/shard_map/all_gather | solution.py:364
  11.0 0.6 copy-start.8
  11.6 0.6 copy-start.10
  12.2 3.7 copy-start.4
  12.2 3.7 copy-start.14
  16.0 2.7 copy-start.15
  18.7 0.6 copy-start.12
  18.7 1.0 copy-start
  19.3 0.6 copy-start.6
  19.9 2.1 copy-start.5
  21.1 116.1 %all-gather.13.cloned.1.call-start = ((), (), s32[]{:S(2)}) async-start(), calls=%async_computation.7 | async-start | bytes 9437184 | tf_op jit(solution)/shard_map/all_gather | solution.py:361
  21.9 229.3 %all-gather.7.cloned.1.call-start = ((), (), s32[]{:S(2)}) async-start(), calls=%async_computation.2 | async-start | bytes 9437184 | tf_op jit(solution)/shard_map/all_gather | solution.py:360
  27.9 6.0 %copy-start.3 = (bf16[1024,512]{1,0:T(8,128)(2,1)}, bf16[1024,512]{1,0:T(8,128)(2,1)S(1)}, u32[]{:S(2)}) copy-start(bf16[1024,512]{1,0:T(8,128)(2,1)S(1)} %get-tuple-element.22) | copy-start | bytes 3145732
  29.3 386.9 %reduce-scatter.5.cloned.1.call-start = ((), (), s32[]{:S(2)}) async-start(), calls=%async_computation.5 | async-start | bytes 18874368 | tf_op jit(solution)/shard_map/reduce_scatter | solution.py:371
  248.7 280.5 %reduce-scatter.3.cloned.1.call-start = ((), (), s32[]{:S(2)}) async-start(), calls=%async_computation.3 | async-start | bytes 18874368 | tf_op jit(solution)/shard_map/reduce_scatter | solution.py:367
  316.5 99.6 %copy-start.1 = (bf16[1024,512]{1,0:T(8,128)(2,1)S(1)}, bf16[1024,512]{1,0:T(8,128)(2,1)}, u32[]{:S(2)}) copy-start(bf16[1024,512]{1,0:T(8,128)(2,1)} %copy-done) | copy-start | bytes 3145732
  316.6 101.6 %copy-start.13 = (f32[1024]{0:T(1024)S(1)}, f32[1024]{0:T(1024)}, u32[]{:S(2)}) copy-start(f32[1024]{0:T(1024)} %copy-done.12) | copy-start | bytes 12292
  316.6 101.6 %copy-start.7 = (f32[1024]{0:T(1024)S(1)}, f32[1024]{0:T(1024)}, u32[]{:S(2)}) copy-start(f32[1024]{0:T(1024)} %copy-done.6) | copy-start | bytes 12292
  416.1 2.2 copy-start.2
  418.4 9.9 %copy-start.9 = (f32[1024]{0:T(1024)S(1)}, f32[1024]{0:T(1024)}, u32[]{:S(2)}) copy-start(f32[1024]{0:T(1024)} %copy-done.8) | copy-start | bytes 12292
  418.4 9.9 %copy-start.11 = (f32[1024]{0:T(1024)S(1)}, f32[1024]{0:T(1024)}, u32[]{:S(2)}) copy-start(f32[1024]{0:T(1024)} %copy-done.10) | copy-start | bytes 12292
  431.8 101.1 %collective-permute-start.1 = (bf16[1024,512]{1,0:T(8,128)(2,1)}, bf16[1024,512]{1,0:T(8,128)(2,1)S(1)}, u32[]{:S(2)}, u32[]{:S(2)}) collective-permute-start(bf16[1024,512]{1,0:T(8,128)(2,1)} %fusion.29), channel_id=1, source_target_pairs={{0,8},{8,0},{1,9},{9,1},{2,10},{10,2},{3,11},{11,3},{4,12},{12,4},... | collective-permute-start | bytes 3145736 | tf_op jit(solution)/shard_map/ppermute | solution.py:377
  531.4 24.7 %collective-permute-start = (bf16[1024,512]{1,0:T(8,128)(2,1)S(1)}, bf16[1024,512]{1,0:T(8,128)(2,1)S(1)}, u32[]{:S(2)}, u32[]{:S(2)}) collective-permute-start(bf16[1024,512]{1,0:T(8,128)(2,1)S(1)} %fusion.26), channel_id=1, source_target_pairs={{0,8},{8,0},{1,9},{9,1},{2,10},{10,2},{3,11},{11,3},{4,12},{12,4},... | collective-permute-start | bytes 3145736 | tf_op jit(solution)/shard_map/ppermute | solution.py:376
Sparse Core Ops, SparseCore 0:
  10.4 22.1 all-gather.10
  35.0 50.1 all-gather.8
  87.1 50.1 all-gather.12
  139.6 50.1 all-gather.6
  248.8 167.2 reduce-scatter.4
  419.5 109.6 reduce-scatter.2

commit v2 on v1

--- a/solution.py
+++ b/solution.py
@@ -9,7 +9,10 @@
 
 NORM_EPS = 1e-6
 CHUNK = 16
-ROW_TILE = 256
+BLOCK = 64
+ROW_TILE = 512
+BIG_TILE = 512
+SMALL_TILE = 256
 VMEM_BYTES = 66_500_000
 BF16 = jnp.bfloat16
 F32 = jnp.float32
@@ -57,22 +60,24 @@
 
 
 def fill_onehot(hot_ref, pos_ref, gate_ref, chunks_ref, src, n_local):
-    tok_rows = pos_ref.shape[2]
-    iota = lax.broadcasted_iota(jnp.int32, (CHUNK, tok_rows), 0)
-    start = jnp.int32(0)
-    for expert in range(n_local):
-        pos_row = pos_ref[src, pl.ds(expert, 1), :]
-        value = 1.0 if gate_ref is None else gate_ref[src, pl.ds(expert, 1), :]
+    tok_rows = pos_ref.shape[3]
+    iota = lax.broadcasted_iota(jnp.int32, (CHUNK, tok_rows), 0).astype(F32).astype(BF16)
+
+    def body(expert, start):
         n_chunks = chunks_ref[src, expert]
 
-        def body(c, carry, pos_row=pos_row, value=value, start=start):
-            hot = jnp.where(iota + c * CHUNK == pos_row, value, 0.0)
-            hot_ref[rows_at(start + c * CHUNK, CHUNK), :] = hot.astype(BF16)
-            return carry
-
-        lax.fori_loop(0, n_chunks, body, 0)
-        start = start + n_chunks * CHUNK
-    return start
+        def block(first):
+            pos_rows = pos_ref[0, expert]
+            value = jnp.ones((CHUNK, tok_rows), BF16) if gate_ref is None else gate_ref[0, expert]
+            for c in range(first, first + BLOCK // CHUNK):
+                hot = jnp.where(iota + jnp.bfloat16(c * CHUNK) == pos_rows, value, jnp.zeros_like(value))
+                hot_ref[rows_at(start + c * CHUNK, CHUNK), :] = hot
+
+        block(0)
+        pl.when(n_chunks > BLOCK // CHUNK)(functools.partial(block, BLOCK // CHUNK))
+        return start + n_chunks * CHUNK
+
+    return lax.fori_loop(0, n_local, body, jnp.int32(0))
 
 
 def zero_tail(ref, offset, length, tile):
@@ -87,22 +92,23 @@
 
 
 def move_segments(pack_ref, wide_ref, base_ref, chunks_ref, src, n_local, cap, to_wide):
-    start = jnp.int32(0)
-    for expert in range(n_local):
+    def body(expert, start):
         n_chunks = chunks_ref[src, expert]
         base = expert * cap + base_ref[src, expert]
 
-        def body(c, carry, start=start, base=base):
-            pack_rows = rows_at(start + c * CHUNK, CHUNK)
-            wide_rows = rows_at(base + c * CHUNK, CHUNK)
+        def block(first):
+            pack_rows = rows_at(start + first, BLOCK)
+            wide_rows = rows_at(base + first, BLOCK)
             if to_wide:
                 wide_ref[wide_rows, :] = pack_ref[pack_rows, :]
             else:
                 pack_ref[pack_rows, :] = wide_ref[wide_rows, :]
-            return carry
-
-        lax.fori_loop(0, n_chunks, body, 0)
-        start = start + n_chunks * CHUNK
+
+        block(0)
+        pl.when(n_chunks > BLOCK // CHUNK)(functools.partial(block, BLOCK))
+        return start + n_chunks * CHUNK
+
+    lax.fori_loop(0, n_local, body, jnp.int32(0))
 
 
 def expert_bases(base_ref, total_ref, chunks_ref, n_src, n_local):
@@ -140,6 +146,24 @@
         return carry
 
     lax.fori_loop(0, n_tiles, body, 0)
+
+
+def tiled_rows(first, count, step):
+    n_small = (count + SMALL_TILE - 1) // SMALL_TILE
+    per_big = BIG_TILE // SMALL_TILE
+    n_big = n_small // per_big
+
+    def big(tile, carry):
+        step(rows_at(first + tile * BIG_TILE, BIG_TILE))
+        return carry
+
+    def small(tile, carry):
+        step(rows_at(first + n_big * BIG_TILE + tile * SMALL_TILE, SMALL_TILE))
+        return carry
+
+    lax.fori_loop(0, n_big, big, 0)
+    if per_big > 1:
+        lax.fori_loop(0, n_small - n_big * per_big, small, 0)
 
 
 def weight_copies(expert, slot, wg_ref, wu_ref, wd_ref, gu_buf, dn_buf, sems):
@@ -186,21 +210,19 @@
         expert = step - n_src
         slot = next_weights(expert, n_local, *w_refs)
 
-        def body(tile, carry):
-            rows = rows_at(expert * cap + tile * ROW_TILE, ROW_TILE)
+        def rows_step(rows):
             pre = dot_nn(wide[rows, :], gu_buf[slot])
             gate = pre[:, :ff]
             act = (gate * jax.nn.sigmoid(gate) * pre[:, ff:]).astype(BF16)
             wide[rows, :] = dot_nn(act, dn_buf[slot]).astype(BF16)
-            return carry
-
-        lax.fori_loop(0, (total[expert] + ROW_TILE - 1) // ROW_TILE, body, 0)
+
+        tiled_rows(expert * cap, total[expert], rows_step)
 
     @pl.when(step >= n_src + n_local)
     def _():
         src = step - n_src - n_local
         length = fill_onehot(hot, pos_ref, gate_ref, chunks_ref, src, n_local)
-        combine(out_ref, pack, hot, wide, base, chunks_ref, src, n_local, cap, length, 2 * ROW_TILE)
+        combine(out_ref, pack, hot, wide, base, chunks_ref, src, n_local, cap, length, ROW_TILE)
 
 
 def backward_kernel(n_src, n_local, cap, chunks_ref, tok_ref, grad_ref, pos_ref, gate_ref, wg_ref, wu_ref, wd_ref,
@@ -227,14 +249,13 @@
     def _():
         expert = step - n_src
         slot = next_weights(expert, n_local, *w_refs)
-        n_tiles = zero_tail(wide_x, expert * cap, total[expert], ROW_TILE)
-        zero_tail(wide_q, expert * cap, total[expert], ROW_TILE)
+        zero_tail(wide_x, expert * cap, total[expert], SMALL_TILE)
+        zero_tail(wide_q, expert * cap, total[expert], SMALL_TILE)
         dwg_ref[...] = jnp.zeros_like(dwg_ref)
         dwu_ref[...] = jnp.zeros_like(dwu_ref)
         dwd_ref[...] = jnp.zeros_like(dwd_ref)
 
-        def body(tile, carry):
-            rows = rows_at(expert * cap + tile * ROW_TILE, ROW_TILE)
+        def rows_step(rows):
             x_rows = wide_x[rows, :]
             q_rows = wide_q[rows, :]
             pre = dot_nn(x_rows, gu_buf[slot])
@@ -251,22 +272,21 @@
             dwg_ref[0] += dw_pre[:, :ff]
             dwu_ref[0] += dw_pre[:, ff:]
             wide_x[rows, :] = dot_nt(grad_pre, gu_buf[slot]).astype(BF16)
-            return carry
-
-        lax.fori_loop(0, n_tiles, body, 0)
+
+        tiled_rows(expert * cap, total[expert], rows_step)
 
     @pl.when(step >= n_src + n_local)
     def _():
         src = step - n_src - n_local
         length = fill_onehot(hot, pos_ref, None, chunks_ref, src, n_local)
-        combine(out_ref, pack, hot, wide_x, base, chunks_ref, src, n_local, cap, length, 2 * ROW_TILE)
+        combine(out_ref, pack, hot, wide_x, base, chunks_ref, src, n_local, cap, length, ROW_TILE)
 
 
 def expert_call(backward, chunks, tables, pos, gate, w_gate, w_up, w_down):
-    n_src, n_local, tok_rows = pos.shape
+    n_src, n_local, _, tok_rows = pos.shape
     hidden, ff = w_gate.shape[1:]
-    cap = n_src * 128
-    pack_rows = n_local * 128
+    cap = n_src * 128 + BLOCK
+    pack_rows = n_local * 128 + BLOCK
     steps = 2 * n_src + n_local
 
     def src_in(i, *_):
@@ -279,7 +299,11 @@
         return (jnp.clip(i - n_src, 0, n_local - 1), 0, 0)
 
     table_spec = pl.BlockSpec((tok_rows, hidden), src_in)
-    whole = pl.BlockSpec(pos.shape, lambda i, *_: (0, 0, 0), pipeline_mode=pl.Buffered(1))
+
+    def route_in(i, *_):
+        return (jnp.where(i < n_src, i, jnp.clip(i - n_src - n_local, 0, n_src - 1)), 0, 0, 0)
+
+    route_spec = pl.BlockSpec((1,) + pos.shape[1:], route_in)
     raw = pl.BlockSpec(memory_space=pl.ANY)
     out_shape = [jax.ShapeDtypeStruct((n_src * tok_rows, hidden), F32)]
     out_specs = [pl.BlockSpec((tok_rows, hidden), src_out)]
@@ -305,7 +329,7 @@
         grid_spec=pltpu.PrefetchScalarGridSpec(
             num_scalar_prefetch=1,
             grid=(steps,),
-            in_specs=[table_spec] * len(tables) + [whole, whole, raw, raw, raw],
+            in_specs=[table_spec] * len(tables) + [route_spec, route_spec, raw, raw, raw],
             out_specs=out_specs,
             scratch_shapes=scratch,
         ),
@@ -324,9 +348,10 @@
     gate = jnp.sum(jnp.where(match, gates[:, None], 0.0), axis=2)
     upper = (jnp.arange(tok_rows)[:, None] <= jnp.arange(tok_rows)[None, :]).astype(BF16)
     rank = jnp.einsum("set,tu->seu", kept.astype(BF16), upper, preferred_element_type=F32)
-    pos = jnp.where(kept, rank - 1.0, -1.0).astype(jnp.int32)
+    pos = jnp.where(kept, rank - 1.0, -1.0).astype(BF16)
     chunks = (rank[:, :, -1].astype(jnp.int32) + CHUNK - 1) // CHUNK
-    return pos, gate, chunks
+    shape = pos.shape[:2] + (CHUNK, tok_rows)
+    return jnp.broadcast_to(pos[:, :, None], shape), jnp.broadcast_to(gate.astype(BF16)[:, :, None], shape), chunks
 
 
 def solution(mesh):
@@ -346,19 +371,20 @@
         n_local = w_gate.shape[0]
         first = lax.axis_index("ep") * n_local
 
+        h_fwd, _ = dense_forward(x_fwd, w_one, w_two)
+        xn_fwd = rms_norm(h_fwd.astype(F32)).astype(BF16)
+        all_fwd = lax.all_gather(xn_fwd, "ep", axis=0, tiled=True)
+
+        xn_fwd, x_saved, grad_in = lax.optimization_barrier((xn_fwd, x_saved, grad_in))
+        all_grad = lax.all_gather(grad_in, "ep", axis=0, tiled=True)
         routes = jnp.concatenate([
-            jnp.where(slots_fwd >= 0, ids_fwd, -1).astype(F32), gates_fwd.astype(F32),
-            jnp.where(slots_bwd >= 0, ids_bwd, -1).astype(F32), gates_bwd.astype(F32),
+            jnp.where(slots_fwd >= 0, ids_fwd, -1).astype(BF16), gates_fwd,
+            jnp.where(slots_bwd >= 0, ids_bwd, -1).astype(BF16), gates_bwd,
         ], axis=1).T
-        routes = lax.all_gather(routes, "ep", axis=0, tiled=False)
+        routes = lax.all_gather(routes, "ep", axis=0, tiled=False).astype(F32)
         id_f, gate_f, id_b, gate_b = (routes[:, i * top_k:(i + 1) * top_k] for i in range(4))
         pos_f, gate_f, chunks_f = route_tables(id_f, gate_f, first, n_local)
         pos_b, gate_b, chunks_b = route_tables(id_b, gate_b, first, n_local)
-
-        h_fwd, _ = dense_forward(x_fwd, w_one, w_two)
-        xn_fwd = rms_norm(h_fwd.astype(F32)).astype(BF16)
-        all_fwd = lax.all_gather(xn_fwd, "ep", axis=0, tiled=True)
-        all_grad = lax.all_gather(grad_in, "ep", axis=0, tiled=True)
         h_bwd, hidden_pre = dense_forward(x_saved, w_one, w_two)
         xn_bwd = rms_norm(h_bwd.astype(F32)).astype(BF16)
         all_bwd = lax.all_gather(xn_bwd, "ep", axis=0, tiled=True)
@@ -367,6 +393,7 @@
         mix_sum = lax.psum_scatter(part_fwd, "ep", scatter_dimension=0, tiled=True)
         y_out = (h_fwd.astype(F32) + mix_sum).astype(BF16)
 
+        chunks_b, _ = lax.optimization_barrier((chunks_b, part_fwd))
         part_bwd, dw_gate, dw_up, dw_down = expert_call(True, chunks_b, (all_bwd, all_grad), pos_b, gate_b, w_gate, w_up, w_down)
         grad_xn = lax.psum_scatter(part_bwd, "ep", scatter_dimension=0, tiled=True)
         _, rms_vjp = jax.vjp(rms_norm, h_bwd.astype(F32))

time: 561 us -> 487 us (0.87)
  waiting for transfers between devices: 317 us -> 222 us
  blocking collectives: 0 us -> 14.3 us
  local copies, waits for them, and re-layouts: 6.42 us -> 16.7 us
    reduce_scatter x1, waiting for transfers between devices: 95.9 us -> 5.2 us  [device_step(): mix_sum = lax.psum_scatter(part_fwd, 'ep', scatter_dimension=0, tiled=True)]
    all_gather x1, waiting for transfers between devices: 52 us -> 0.01 us  [device_step(): all_grad = lax.all_gather(grad_in, 'ep', axis=0, tiled=True)]
    reduce_scatter x1, waiting for transfers between devices: 99.6 us -> 142 us  [device_step(): grad_xn = lax.psum_scatter(part_bwd, 'ep', scatter_dimension=0, tiled=True)]
    ppermute x1, waiting for transfers between devices: 0.01 us -> 23.2 us  [device_step(): dx_prev = lax.ppermute(grad_x, 'pp', prev_perm)]
    ppermute x1, waiting for transfers between devices: 23.2 us -> 0.01 us  [device_step(): y_next = lax.ppermute(y_out, 'pp', next_perm)]
    all_gather x1, waiting for transfers between devices: 0.01 us -> 22.5 us  [device_step(): all_fwd = lax.all_gather(xn_fwd, 'ep', axis=0, tiled=True)]
    all_gather x0 -> x1, blocking collectives: none -> 14.3 us  [device_step(): routes = lax.all_gather(routes, 'ep', axis=0, tiled=False).astype(F32)]
    all_gather x1, waiting for transfers between devices: 42.2 us -> 28.3 us  [device_step(): all_bwd = lax.all_gather(xn_bwd, 'ep', axis=0, tiled=True)]
  transfers between devices with their start and end apart: 8 -> 7, of which waited for: 6 -> 5; matrix products, arithmetic and copies ran while one was open for 8% -> 9% of each run, Pallas kernels for 31% -> 35%
where the time goes in v2:
time: 487 us; the launch traced here: 486 us
  waiting for transfers between devices  222 us (46%)
  Pallas kernels  172 us (35%)
  matrix products  22.5 us (5%)
  other arithmetic  20 us (4%)
  local copies, waits for them, and re-layouts  16.7 us (3%)
  blocking collectives  14.3 us (3%)
  between operations  14.1 us (3%)
    pallas_call x2, Pallas kernels, expert_call(): pl.pallas_call(functools.partial(body, n_src, n_local, cap), grid_spec=pl...  172 us
    reduce_scatter x1, waiting for transfers between devices, device_step(): grad_xn = lax.psum_scatter(part_bwd, 'ep', scatter_dimension=0, tiled=True)  142 us
    all_gather x1, waiting for transfers between devices, device_step(): all_bwd = lax.all_gather(xn_bwd, 'ep', axis=0, tiled=True)  28.3 us
    ppermute x1, waiting for transfers between devices, device_step(): dx_prev = lax.ppermute(grad_x, 'pp', prev_perm)  23.2 us
    all_gather x1, waiting for transfers between devices, device_step(): all_fwd = lax.all_gather(xn_fwd, 'ep', axis=0, tiled=True)  22.5 us
    all_gather x1, blocking collectives, device_step(): routes = lax.all_gather(routes, 'ep', axis=0, tiled=False).astype(F32)  14.3 us
    dot_general x1, matrix products, dense_backward(): jnp.einsum('tf,hf->th', grad_pre, w_one, preferred_element_type=F32)  9.88 us
  transfers between devices with their start and end apart: 7, of which 5 were waited for; matrix products, arithmetic and copies ran while one was open for 9% of the time, Pallas kernels for 35%

profile of v2, /device:TPU:0, one launch (start us, length us, event | category | flops | bytes accessed | tf_op | source)
XLA Modules:
  0.0 485.8 jit_solution(13842998183746963553)
XLA Ops:
  7.2 1.5 fusion.13
  8.7 6.3 %fusion.16 = (f32[1024]{0:T(1024)S(1)}, bf16[1024,512]{1,0:T(8,128)(2,1)S(1)}) fusion(bf16[1,1536,512]{2,1,0:T(8,128)(2,1)} %param.24, bf16[1,512,1536]{2,1,0:T(8,128)(2,1)} %param.23, bf16[1,1024,512]{2,1,0:T(8,128)(2,1)} %param.14, f32[1024]{0:T(1024)S(1)} %add_rsqrt_fusion.1), kind=kOutput, calls=%fused_computation.38 | convolution fusion | flops 3233807360 | bytes 5251072 | tf_op jit(solution)/shard_map/dot_general | solution.py:34
  15.1 1.3 fusion.17
  16.4 0.7 all-gather.9.cloned.1.call-update
  18.6 3.4 fusion.35
  22.0 2.0 fusion.22
  24.7 0.9 copy-done
  25.6 1.3 fusion.23
  27.0 14.3 %all-gather = bf16[256,1024]{1,0:T(8,128)(2,1)S(1)} all-gather(bf16[32,1024]{1,0:T(8,128)(2,1)S(1)} %maximum_bitcast_fusion), channel_id=2, replica_groups=mesh['pp'=2,'ep'=8] {'ep'}, dimensions={0}, use_global_device_ids=true | all-gather | bytes 589824 | tf_op jit(solution)/shard_map/all_gather | solution.py:384
  41.4 3.4 compare_reduce_fusion
  45.6 0.6 add_select_fusion.1.chunks_ref
  46.2 2.8 fusion.1
  49.0 22.5 %all-gather.5.cloned.1.call-done.tok_ref = bf16[8192,512]{1,0:T(8,128)(2,1)} async-done(((bf16[1024,512]{1,0:T(8,128)(2,1)}), bf16[8192,512]{1,0:T(8,128)(2,1)}) %all-gather.5.cloned.1.call-update) | async-done | bytes 8388624 | tf_op jit(solution)/shard_map/all_gather | solution.py:376
  71.6 2.6 broadcast_in_dim.49.pos_ref
  74.2 2.6 broadcast_in_dim.91.gate_ref
  76.8 69.5 %expert_forward.1 = f32[8192,512]{1,0:T(8,128)} custom-call(s32[8,16]{1,0:T(8,128)} %add_select_fusion.1.chunks_ref, bf16[8192,512]{1,0:T(8,128)(2,1)} %all-gather.5.cloned.1.call-done.tok_ref, bf16[8,16,16,1024]{3,2,1,0:T(8,128)(2,1)} %broadcast_in_dim.49.pos_ref, bf16[8,16,16,1024]{3,2,1,0:T(8,128)(2,1)} %broadcast_in_dim.91.gate_ref, ...), custom_call_target="tpu_custom_call" | custom-call | flops 60000002048 | bytes 60000000 | tf_op jit(solution)/shard_map/expert_forward/pallas_call | solution.py:327
  147.4 0.6 add_select_fusion.chunks_ref
  148.0 28.3 %all-gather.7.cloned.1.call-done.tok_ref = bf16[8192,512]{1,0:T(8,128)(2,1)} async-done(((bf16[1024,512]{1,0:T(8,128)(2,1)}), bf16[8192,512]{1,0:T(8,128)(2,1)}) %all-gather.7.cloned.1.call-update) | async-done | bytes 8388624 | tf_op jit(solution)/shard_map/all_gather | solution.py:390
  176.2 2.6 broadcast_in_dim.93.pos_ref
  178.8 2.7 broadcast_in_dim.95.gate_ref
  181.5 102.6 %expert_backward.1 = (f32[8192,512]{1,0:T(8,128)}, f32[16,512,384]{2,1,0:T(8,128)}, f32[16,512,384]{2,1,0:T(8,128)}, f32[16,384,512]{2,1,0:T(8,128)}) custom-call(s32[8,16]{1,0:T(8,128)} %add_select_fusion.chunks_ref, bf16[8192,512]{1,0:T(8,128)(2,1)} %all-gather.7.cloned.1.call-done.tok_ref, bf16[8192,512]{1,0:T(8,128)(2,1)} %all-gather.9.cloned.1.call-done.grad_ref, ...), custom_call_target="tpu_custom_call" | custom-call | flops 99999997952 | bytes 60000000 | tf_op jit(solution)/shard_map/expert_backward/pallas_call | solution.py:327
  284.1 5.2 %reduce-scatter.3.cloned.1.call-done = f32[1024,512]{1,0:T(8,128)} async-done(((f32[8192,512]{1,0:T(8,128)}), f32[1024,512]{1,0:T(8,128)}) %reduce-scatter.3.cloned.1.call-update) | async-done | bytes 2097168 | tf_op jit(solution)/shard_map/reduce_scatter | solution.py:393
  289.3 2.9 fusion.18
  292.2 2.3 collective-permute-start
  294.5 141.9 %reduce-scatter.5.cloned.1.call-done = f32[1024,512]{1,0:T(8,128)} async-done(((f32[8192,512]{1,0:T(8,128)}), f32[1024,512]{1,0:T(8,128)}) %reduce-scatter.5.cloned.1.call-update) | async-done | bytes 2097168 | tf_op jit(solution)/shard_map/reduce_scatter | solution.py:398
  436.4 2.0 fusion.24
  438.7 9.9 %fusion.28 = (f32[1024]{0:T(1024)S(1)}, f32[1024,512]{1,0:T(8,128)}) fusion(bf16[1024,512]{1,0:T(8,128)(2,1)} %bitcast.82, bf16[1,512,1536]{2,1,0:T(8,128)(2,1)} %param.23, f32[1024,1536]{1,0:T(8,128)} %copy-done.21, bf16[1,1536,512]{2,1,0:T(8,128)(2,1)} %param.24, bf16[1024,512]{1,0:T(8,128)(2,1)S(1)} %copy-done.1, f32[1024,512]{1,0:T(8,128)S(1)} %copy-done.2, ...), kind=kOutput, calls=%fused_computation.50 | convolution fusion | flops 3241147392 | bytes 16789504 | tf_op jit(solution)/shard_map/tf,hf->th/dot_general | solution.py:42
  448.6 2.7 fusion.21
  451.3 1.5 collective-permute-start.1
  452.8 23.2 %collective-permute-done.1 = bf16[1024,512]{1,0:T(8,128)(2,1)S(1)} collective-permute-done((bf16[1024,512]{1,0:T(8,128)(2,1)S(1)}, bf16[1024,512]{1,0:T(8,128)(2,1)S(1)}, u32[]{:S(2)}, u32[]{:S(2)}) %collective-permute-start.1) | collective-permute-done | bytes 1048608 | tf_op jit(solution)/shard_map/ppermute | solution.py:404
  476.0 2.3 copy.36
  478.3 1.0 copy.37
  (69 shorter events, 4.4 us)
Async XLA Ops:
  7.2 64.4 %all-gather.5.cloned.1.call-start = ((), (), s32[]{:S(2)}) async-start(), calls=%async_computation.2 | async-start | bytes 9437184 | tf_op jit(solution)/shard_map/all_gather | solution.py:376
  15.0 2.1 copy-start.3
  15.0 2.1 copy-start.5
  16.3 131.6 %all-gather.9.cloned.1.call-start = ((), (), s32[]{:S(2)}) async-start(), calls=%async_computation.5 | async-start | bytes 9437184 | tf_op jit(solution)/shard_map/all_gather | solution.py:379
  17.1 159.1 %all-gather.7.cloned.1.call-start = ((), (), s32[]{:S(2)}) async-start(), calls=%async_computation.4 | async-start | bytes 9437184 | tf_op jit(solution)/shard_map/all_gather | solution.py:390
  17.4 0.6 copy-start.8
  18.0 0.6 copy-start.14
  18.6 3.4 copy-start.20
  22.0 2.6 copy-start.21
  24.6 1.0 copy-start
  24.6 16.8 %copy-start.16 = (f32[1024]{0:T(1024)}, f32[1024]{0:T(1024)S(1)}, u32[]{:S(2)}) copy-start(f32[1024]{0:T(1024)S(1)} %get-tuple-element.31) | copy-start | bytes 12292
  24.6 2.3 copy-start.10
  24.6 2.3 copy-start.11
  24.6 2.3 copy-start.12
  24.6 2.3 copy-start.13
  24.6 2.3 copy-start.18
  24.6 2.3 copy-start.19
  24.7 0.9 copy-start.6
  26.8 262.5 %reduce-scatter.3.cloned.1.call-start = ((), (), s32[]{:S(2)}) async-start(), calls=%async_computation.3 | async-start | bytes 18874368 | tf_op jit(solution)/shard_map/reduce_scatter | solution.py:393
  146.3 290.1 %reduce-scatter.5.cloned.1.call-start = ((), (), s32[]{:S(2)}) async-start(), calls=%async_computation.6 | async-start | bytes 18874368 | tf_op jit(solution)/shard_map/reduce_scatter | solution.py:398
  284.1 5.2 %copy-start.4 = (bf16[1024,512]{1,0:T(8,128)(2,1)S(1)}, bf16[1024,512]{1,0:T(8,128)(2,1)}, u32[]{:S(2)}) copy-start(bf16[1024,512]{1,0:T(8,128)(2,1)} %copy-done.3) | copy-start | bytes 3145732
  284.1 152.3 %copy-start.1 = (bf16[1024,512]{1,0:T(8,128)(2,1)S(1)}, bf16[1024,512]{1,0:T(8,128)(2,1)}, u32[]{:S(2)}) copy-start(bf16[1024,512]{1,0:T(8,128)(2,1)} %copy-done) | copy-start | bytes 3145732
  292.2 146.2 %copy-start.17 = (f32[1024]{0:T(1024)S(1)}, f32[1024]{0:T(1024)}, u32[]{:S(2)}) copy-start(f32[1024]{0:T(1024)} %copy-done.16) | copy-start | bytes 12292
  292.2 146.3 %copy-start.7 = (f32[1024]{0:T(1024)S(1)}, f32[1024]{0:T(1024)}, u32[]{:S(2)}) copy-start(f32[1024]{0:T(1024)} %copy-done.6) | copy-start | bytes 12292
  292.2 160.6 %collective-permute-start = (bf16[1024,512]{1,0:T(8,128)(2,1)}, bf16[1024,512]{1,0:T(8,128)(2,1)}, u32[]{:S(2)}, u32[]{:S(2)}) collective-permute-start(bf16[1024,512]{1,0:T(8,128)(2,1)} %fusion.18), channel_id=1, source_target_pairs={{0,8},{8,0},{1,9},{9,1},{2,10},{10,2},{3,11},{11,3},{4,12},{12,4},... | collective-permute-start | bytes 3145736 | tf_op jit(solution)/shard_map/ppermute | solution.py:403
  436.4 2.2 copy-start.2
  438.7 9.9 %copy-start.9 = (f32[1024]{0:T(1024)S(1)}, f32[1024]{0:T(1024)}, u32[]{:S(2)}) copy-start(f32[1024]{0:T(1024)} %copy-done.8) | copy-start | bytes 12292
  438.7 9.9 %copy-start.15 = (f32[1024]{0:T(1024)S(1)}, f32[1024]{0:T(1024)}, u32[]{:S(2)}) copy-start(f32[1024]{0:T(1024)} %copy-done.14) | copy-start | bytes 12292
  451.3 24.7 %collective-permute-start.1 = (bf16[1024,512]{1,0:T(8,128)(2,1)S(1)}, bf16[1024,512]{1,0:T(8,128)(2,1)S(1)}, u32[]{:S(2)}, u32[]{:S(2)}) collective-permute-start(bf16[1024,512]{1,0:T(8,128)(2,1)S(1)} %fusion.21), channel_id=1, source_target_pairs={{0,8},{8,0},{1,9},{9,1},{2,10},{10,2},{3,11},{11,3},{4,12},{12,4},... | collective-permute-start | bytes 3145736 | tf_op jit(solution)/shard_map/ppermute | solution.py:404
Sparse Core Ops, SparseCore 0:
  16.5 55.0 all-gather.4
  73.4 50.1 all-gather.8
  126.1 50.1 all-gather.6
  179.6 109.6 reduce-scatter.2
  292.7 143.6 reduce-scatter.4

commit v3 on v2

--- a/solution.py
+++ b/solution.py
@@ -33,14 +33,6 @@
     dense_act = jax.nn.silu(hidden_pre).astype(BF16)
     dense_out = jnp.dot(dense_act, w_two, preferred_element_type=F32)
     return (x_rows.astype(F32) + dense_out).astype(BF16), hidden_pre
-
-
-def dense_backward(x_rows, hidden_pre, w_one, w_two, grad_h):
-    _, norm_vjp = jax.vjp(rms_norm, x_rows.astype(F32))
-    grad_act = jnp.einsum("th,fh->tf", grad_h.astype(BF16), w_two, preferred_element_type=F32)
-    grad_pre = (grad_act * silu_grad(hidden_pre)).astype(BF16)
-    grad_norm = jnp.einsum("tf,hf->th", grad_pre, w_one, preferred_element_type=F32)
-    return grad_h + norm_vjp(grad_norm)[0]
 
 
 def dot_nn(lhs, rhs):
@@ -340,6 +332,183 @@
     )(chunks, *tables, pos, gate, w_gate, w_up, w_down)
 
 
+def reduce_tail_kernel(part_ref, h_ref, x_ref, grad_ref, pre_ref, w1_ref, w2_ref, out_ref,
+                       sums, core_in, x_in, y_in, x_last, y_last, dx_buf, h_buf, x_buf, grad_buf, pre_buf, w1_buf, w2_buf,
+                       load_sem, row_sem, weight_sem, core_send, core_recv, hop_send, hop_recv, last_send, last_recv, dx_send, dx_recv):
+    n_chunks, half = x_in.shape[0], x_in.shape[2]
+    chunk = 2 * half
+    tok_rows = n_chunks * chunk
+    me = lax.axis_index("ep")
+    core, x_pos, y_pos = lax.rem(me, 2), lax.rem(me // 2, 2), me // 4
+    x_step, y_step = 2 - 4 * x_pos, 4 - 8 * y_pos
+    partner = me + 1 - 2 * core
+    x_peer, y_peer = me + x_step, me + y_step
+    pp_peer = 1 - lax.axis_index("pp")
+    offsets = (0, x_step, y_step, x_step + y_step)
+    mesh_id = pl.DeviceIdType.MESH
+
+    barrier = pltpu.get_barrier_semaphore()
+    for peer in ({"ep": partner}, {"ep": x_peer}, {"ep": y_peer}, {"pp": pp_peer}):
+        pl.semaphore_signal(barrier, inc=1, device_id=peer, device_id_type=mesh_id)
+    pl.semaphore_wait(barrier, 4)
+
+    def part_rows(dest, k):
+        return part_ref.at[pl.ds(pl.multiple_of(dest * tok_rows + k * chunk, chunk), chunk)]
+
+    def core_copy(k, i):
+        return pltpu.make_async_remote_copy(part_rows(partner + offsets[i], k), core_in.at[k, i], core_send.at[k, i], core_recv.at[k, i],
+                                            device_id={"ep": partner}, device_id_type=mesh_id)
+
+    def load_copy(k, i):
+        return pltpu.make_async_copy(part_rows(me + offsets[i], k), sums.at[k, i], load_sem.at[k, i])
+
+    def hop_copies(k):
+        top, low = pl.ds(0, half), pl.ds(half, half)
+        return [
+            pltpu.make_async_remote_copy(sums.at[k, i, rows], land.at[k, j], hop_send.at[k, n], hop_recv.at[k, n],
+                                         device_id={"ep": peer}, device_id_type=mesh_id)
+            for n, (i, rows, land, j, peer) in enumerate((
+                (3, top, x_in, 1, x_peer), (3, low, y_in, 1, y_peer), (1, top, x_in, 0, x_peer), (2, low, y_in, 0, y_peer)))
+        ]
+
+    def last_copies(k):
+        top, low = pl.ds(0, half), pl.ds(half, half)
+        return [
+            pltpu.make_async_remote_copy(sums.at[k, 2, top], y_last.at[k], last_send.at[k, 0], last_recv.at[k, 0],
+                                         device_id={"ep": y_peer}, device_id_type=mesh_id),
+            pltpu.make_async_remote_copy(sums.at[k, 1, low], x_last.at[k], last_send.at[k, 1], last_recv.at[k, 1],
+                                         device_id={"ep": x_peer}, device_id_type=mesh_id),
+        ]
+
+    def chunk_rows(k):
+        return pl.ds(pl.multiple_of(k * chunk, chunk), chunk)
+
+    def row_copies(k):
+        return [pltpu.make_async_copy(src.at[chunk_rows(k)], buf.at[chunk_rows(k)], row_sem.at[k, n])
+                for n, (src, buf) in enumerate(((h_ref, h_buf), (x_ref, x_buf), (grad_ref, grad_buf), (pre_ref, pre_buf)))]
+
+    def weight_loads():
+        return [pltpu.make_async_copy(w1_ref, w1_buf, weight_sem.at[0]), pltpu.make_async_copy(w2_ref, w2_buf, weight_sem.at[1])]
+
+    def dx_copy(k):
+        return pltpu.make_async_remote_copy(dx_buf.at[chunk_rows(k)], out_ref.at[chunk_rows(k)], dx_send.at[k], dx_recv.at[k],
+                                            device_id={"pp": pp_peer}, device_id_type=mesh_id)
+
+    def start_chunk(k, carry):
+        for i in (3, 1, 2, 0):
+            core_copy(k, i).start()
+            load_copy(k, i).start()
+        return carry
+
+    lax.fori_loop(0, n_chunks, start_chunk, 0)
+
+    def add_cores(k, carry):
+        hops = hop_copies(k)
+        for i, ready in ((3, (0, 1)), (1, (2,)), (2, (3,)), (0, ())):
+            load_copy(k, i).wait()
+            core_copy(k, i).wait_recv()
+            sums[k, i] = sums[k, i] + core_in[k, i]
+            for n in ready:
+                hops[n].start()
+        return carry
+
+    lax.fori_loop(0, n_chunks, add_cores, 0)
+
+    for copy in weight_loads():
+        copy.start()
+
+    def start_rows(k, carry):
+        for copy in row_copies(k):
+            copy.start()
+        return carry
+
+    lax.fori_loop(0, n_chunks, start_rows, 0)
+
+    def relay(k, carry):
+        hops, lasts = hop_copies(k), last_copies(k)
+        hops[0].wait_recv()
+        sums[k, 2, :half] = sums[k, 2, :half] + x_in[k, 1]
+        lasts[0].start()
+        hops[1].wait_recv()
+        sums[k, 1, half:] = sums[k, 1, half:] + y_in[k, 1]
+        lasts[1].start()
+        return carry
+
+    lax.fori_loop(0, n_chunks, relay, 0)
+
+    for copy in weight_loads():
+        copy.wait()
+
+    def norm_grad(values, grads):
+        scale = lax.rsqrt(jnp.mean(values * values, axis=-1, keepdims=True) + NORM_EPS)
+        return scale * grads - values * (scale * scale * scale * jnp.mean(grads * values, axis=-1, keepdims=True))
+
+    def finish(k, carry):
+        rows = chunk_rows(k)
+        hops, lasts = hop_copies(k), last_copies(k)
+        for copy in row_copies(k):
+            copy.wait()
+        for copy in hops[2:]:
+            copy.wait_recv()
+        for copy in lasts:
+            copy.wait_recv()
+        sums[k, 0, :half] = sums[k, 0, :half] + x_in[k, 0] + y_last[k]
+        sums[k, 0, half:] = sums[k, 0, half:] + y_in[k, 0] + x_last[k]
+        grad_h = grad_buf[rows, :].astype(F32) + norm_grad(h_buf[rows, :].astype(F32), sums[k, 0])
+        grad_act = dot_nt(grad_h.astype(BF16), w2_buf[...])
+        grad_pre = (grad_act * silu_grad(pre_buf[rows, :])).astype(BF16)
+        grad_norm = dot_nt(grad_pre, w1_buf[...])
+        dx_buf[rows, :] = (grad_h + norm_grad(x_buf[rows, :].astype(F32), grad_norm)).astype(BF16)
+        dx_copy(k).start()
+        return carry
+
+    lax.fori_loop(0, n_chunks, finish, 0)
+
+    def drain(k, carry):
+        for i in range(4):
+            core_copy(k, i).wait_send()
+        for copy in hop_copies(k) + last_copies(k):
+            copy.wait_send()
+        dx_copy(k).wait()
+        return carry
+
+    lax.fori_loop(0, n_chunks, drain, 0)
+
+
+def reduce_tail(part, h_rows, x_rows, grad_rows, hidden_pre, w_one, w_two):
+    tok_rows, hidden = x_rows.shape
+    ff = w_one.shape[1]
+    n_chunks = 4
+    half = tok_rows // (2 * n_chunks)
+    raw = pl.BlockSpec(memory_space=pl.ANY)
+    dma = pltpu.SemaphoreType.DMA
+    rows_buf = pltpu.VMEM((tok_rows, hidden), BF16)
+    return pl.pallas_call(
+        reduce_tail_kernel,
+        out_shape=jax.ShapeDtypeStruct((tok_rows, hidden), BF16),
+        in_specs=[raw] * 7,
+        out_specs=raw,
+        scratch_shapes=[
+            pltpu.VMEM((n_chunks, 4, 2 * half, hidden), F32),
+            pltpu.VMEM((n_chunks, 4, 2 * half, hidden), F32),
+            pltpu.VMEM((n_chunks, 2, half, hidden), F32),
+            pltpu.VMEM((n_chunks, 2, half, hidden), F32),
+            pltpu.VMEM((n_chunks, half, hidden), F32),
+            pltpu.VMEM((n_chunks, half, hidden), F32),
+            rows_buf, rows_buf, rows_buf, rows_buf,
+            pltpu.VMEM((tok_rows, ff), F32),
+            pltpu.VMEM(w_one.shape, BF16),
+            pltpu.VMEM(w_two.shape, BF16),
+            dma((n_chunks, 4)), dma((n_chunks, 4)), dma((2,)),
+            dma((n_chunks, 4)), dma((n_chunks, 4)), dma((n_chunks, 4)), dma((n_chunks, 4)),
+            dma((n_chunks, 2)), dma((n_chunks, 2)), dma((n_chunks,)), dma((n_chunks,)),
+        ],
+        compiler_params=pltpu.CompilerParams(collective_id=0, has_side_effects=True, vmem_limit_bytes=VMEM_BYTES),
+        cost_estimate=pl.CostEstimate(flops=60 * 10 ** 9, bytes_accessed=40 * 10 ** 6, transcendentals=0),
+        name="reduce_tail",
+    )(part, h_rows, x_rows, grad_rows, hidden_pre, w_one, w_two)
+
+
 def route_tables(ids, gates, first, n_local):
     tok_rows = ids.shape[2]
     experts = (first + jnp.arange(n_local)).astype(F32)
@@ -358,7 +527,7 @@
     stages = mesh.shape["pp"]
     ep_size = mesh.shape["ep"]
     next_perm = [(stage_idx, (stage_idx + 1) % stages) for stage_idx in range(stages)]
-    prev_perm = [(stage_idx, (stage_idx - 1) % stages) for stage_idx in range(stages)]
+    assert (stages, ep_size) == (2, 8)
     tok_spec = P("pp", "ep", None)
     dense_spec = P("pp", None, None)
     expert_spec = P("pp", "ep", None, None)
@@ -395,13 +564,8 @@
 
         chunks_b, _ = lax.optimization_barrier((chunks_b, part_fwd))
         part_bwd, dw_gate, dw_up, dw_down = expert_call(True, chunks_b, (all_bwd, all_grad), pos_b, gate_b, w_gate, w_up, w_down)
-        grad_xn = lax.psum_scatter(part_bwd, "ep", scatter_dimension=0, tiled=True)
-        _, rms_vjp = jax.vjp(rms_norm, h_bwd.astype(F32))
-        grad_h = grad_in.astype(F32) + rms_vjp(grad_xn)[0]
-        grad_x = dense_backward(x_saved, hidden_pre, w_one, w_two, grad_h).astype(BF16)
-
         y_next = lax.ppermute(y_out, "pp", next_perm)
-        dx_prev = lax.ppermute(grad_x, "pp", prev_perm)
+        dx_prev = reduce_tail(part_bwd, h_bwd, x_saved, grad_in, hidden_pre, w_one, w_two)
         return y_next[None], dx_prev[None], dw_gate[None], dw_up[None], dw_down[None]
 
     in_specs = (tok_spec,) * 9 + (dense_spec, dense_spec, expert_spec, expert_spec, expert_spec)

time: 487 us -> 421 us (0.86)
  waiting for transfers between devices: 222 us -> 57 us
  Pallas kernels: 172 us -> 287 us
  matrix products: 22.5 us -> 12.6 us
    reduce_scatter x1 -> x0, waiting for transfers between devices: 142 us -> none  [device_step(): grad_xn = lax.psum_scatter(part_bwd, 'ep', scatter_dimension=0, tiled=True)]
    pallas_call x0 -> x1, Pallas kernels: none -> 107 us  [reduce_tail(): pl.pallas_call(reduce_tail_kernel, out_shape=jax.ShapeDtypeStruct((tok_ro...]
    ppermute x1 -> x0, waiting for transfers between devices: 23.2 us -> none  [device_step(): dx_prev = lax.ppermute(grad_x, 'pp', prev_perm)]
    dot_general x1 -> x0, matrix products: 9.88 us -> none  [dense_backward(): jnp.einsum('tf,hf->th', grad_pre, w_one, preferred_element_type=F32)]
    pallas_call x2, Pallas kernels: 172 us -> 181 us  [expert_call(): pl.pallas_call(functools.partial(body, n_src, n_local, cap), grid_spec=pl...]
    reduce_scatter x1, waiting for transfers between devices: 5.2 us -> 0.02 us  [device_step(): mix_sum = lax.psum_scatter(part_fwd, 'ep', scatter_dimension=0, tiled=True)]
  transfers between devices with their start and end apart: 7 -> 5, of which waited for: 5 -> 2; matrix products, arithmetic and copies ran while one was open for 9% -> 6% of each run, Pallas kernels for 35% -> 69%
where the time goes in v3:
time: 421 us; the launch traced here: 418 us
  Pallas kernels  287 us (68%)
  waiting for transfers between devices  57 us (14%)
  local copies, waits for them, and re-layouts  16.5 us (4%)
  other arithmetic  15.5 us (4%)
  blocking collectives  14.3 us (3%)
  between operations  14 us (3%)
  matrix products  12.6 us (3%)
    pallas_call x2, Pallas kernels, expert_call(): pl.pallas_call(functools.partial(body, n_src, n_local, cap), grid_spec=pl...  181 us
    pallas_call x1, Pallas kernels, reduce_tail(): pl.pallas_call(reduce_tail_kernel, out_shape=jax.ShapeDtypeStruct((tok_ro...  107 us
    all_gather x1, waiting for transfers between devices, device_step(): all_bwd = lax.all_gather(xn_bwd, 'ep', axis=0, tiled=True)  32.5 us
    all_gather x1, waiting for transfers between devices, device_step(): all_fwd = lax.all_gather(xn_fwd, 'ep', axis=0, tiled=True)  23.7 us
    all_gather x1, blocking collectives, device_step(): routes = lax.all_gather(routes, 'ep', axis=0, tiled=False).astype(F32)  14.3 us
  transfers between devices with their start and end apart: 5, of which 2 were waited for; matrix products, arithmetic and copies ran while one was open for 6% of the time, Pallas kernels for 69%

profile of v3, /device:TPU:0, one launch (start us, length us, event | category | flops | bytes accessed | tf_op | source)
XLA Modules:
  0.0 417.6 jit_solution(10640180966005399998)
XLA Ops:
  7.2 1.5 fusion.15
  8.7 6.3 %fusion.18 = (f32[1024]{0:T(1024)S(1)}, bf16[1024,512]{1,0:T(8,128)(2,1)S(1)}) fusion(bf16[1,1536,512]{2,1,0:T(8,128)(2,1)} %param.24, bf16[1,1024,512]{2,1,0:T(8,128)(2,1)} %param.14, f32[1024]{0:T(1024)S(1)} %add_rsqrt_fusion.3, bf16[1,512,1536]{2,1,0:T(8,128)(2,1)} %param.23), kind=kOutput, calls=%fused_computation.32 | convolution fusion | flops 3233807360 | bytes 5251072 | tf_op jit(solution)/shard_map/dot_general | solution.py:34
  15.1 1.3 fusion.19
  16.4 0.7 all-gather.9.cloned.1.call-update
  17.2 0.3 fusion.21
  17.5 3.4 fusion.24.pre_ref
  20.9 2.0 fusion.13
  22.9 0.5 copy-done.10
  23.5 0.9 copy-done.2
  24.4 1.3 fusion.14
  25.8 14.3 %all-gather = bf16[256,1024]{1,0:T(8,128)(2,1)S(1)} all-gather(bf16[32,1024]{1,0:T(8,128)(2,1)S(1)} %maximum_bitcast_fusion), channel_id=2, replica_groups=mesh['pp'=2,'ep'=8] {'ep'}, dimensions={0}, use_global_device_ids=true | all-gather | bytes 589824 | tf_op jit(solution)/shard_map/all_gather | solution.py:553
  40.1 0.1 fusion.49
  40.2 3.4 compare_reduce_fusion
  43.7 0.5 select_convert_fusion.1
  44.1 0.3 fusion.35
  44.4 0.6 add_select_fusion.1.chunks_ref
  45.0 2.8 fusion.1
  47.9 23.7 %all-gather.5.cloned.1.call-done.tok_ref = bf16[8192,512]{1,0:T(8,128)(2,1)} async-done(((bf16[1024,512]{1,0:T(8,128)(2,1)}), bf16[8192,512]{1,0:T(8,128)(2,1)}) %all-gather.5.cloned.1.call-update) | async-done | bytes 8388624 | tf_op jit(solution)/shard_map/all_gather | solution.py:545
  71.6 2.6 broadcast_in_dim.45.pos_ref
  74.2 2.6 broadcast_in_dim.83.gate_ref
  76.8 65.7 %expert_forward.1 = f32[8192,512]{1,0:T(8,128)} custom-call(s32[8,16]{1,0:T(8,128)} %add_select_fusion.1.chunks_ref, bf16[8192,512]{1,0:T(8,128)(2,1)} %all-gather.5.cloned.1.call-done.tok_ref, bf16[8,16,16,1024]{3,2,1,0:T(8,128)(2,1)} %broadcast_in_dim.45.pos_ref, bf16[8,16,16,1024]{3,2,1,0:T(8,128)(2,1)} %broadcast_in_dim.83.gate_ref, ...), custom_call_target="tpu_custom_call" | custom-call | flops 60000002048 | bytes 60000000 | tf_op jit(solution)/shard_map/expert_forward/pallas_call | solution.py:319
  142.4 0.5 select_convert_fusion
  142.9 0.3 fusion.33
  143.2 0.6 add_select_fusion.chunks_ref
  143.8 32.5 %all-gather.7.cloned.1.call-done.tok_ref = bf16[8192,512]{1,0:T(8,128)(2,1)} async-done(((bf16[1024,512]{1,0:T(8,128)(2,1)}), bf16[8192,512]{1,0:T(8,128)(2,1)}) %all-gather.7.cloned.1.call-update) | async-done | bytes 8388624 | tf_op jit(solution)/shard_map/all_gather | solution.py:559
  176.3 2.6 broadcast_in_dim.85.pos_ref
  178.9 2.7 broadcast_in_dim.87.gate_ref
  181.6 115.2 %expert_backward.1 = (f32[8192,512]{1,0:T(8,128)}, f32[16,512,384]{2,1,0:T(8,128)}, f32[16,512,384]{2,1,0:T(8,128)}, f32[16,384,512]{2,1,0:T(8,128)}) custom-call(s32[8,16]{1,0:T(8,128)} %add_select_fusion.chunks_ref, bf16[8192,512]{1,0:T(8,128)(2,1)} %all-gather.7.cloned.1.call-done.tok_ref, bf16[8192,512]{1,0:T(8,128)(2,1)} %all-gather.9.cloned.1.call-done.grad_ref, ...), custom_call_target="tpu_custom_call" | custom-call | flops 99999997952 | bytes 60000000 | tf_op jit(solution)/shard_map/expert_backward/pallas_call | solution.py:319
  296.8 3.2 fusion.20
  300.0 106.6 %reduce_tail.1 = bf16[1024,512]{1,0:T(8,128)(2,1)} custom-call(f32[8192,512]{1,0:T(8,128)} %get-tuple-element.15.part_ref, bf16[1024,512]{1,0:T(8,128)(2,1)} %copy-done.2, bf16[1024,512]{1,0:T(8,128)(2,1)} %bitcast.66, bf16[1024,512]{1,0:T(8,128)(2,1)} %bitcast.65, f32[1024,1536]{1,0:T(8,128)} %copy-done.10, bf16[512,1536]{1,0:T(8,128)(2,1)} %bitcast.80, ...), custom_call_target="tpu_custom_call" | custom-call | flops 60000002048 | bytes 40000000 | tf_op jit(solution)/shard_map/reduce_tail/pallas_call | solution.py:486
  406.6 2.3 copy.29
  408.9 2.3 copy.30
  (38 shorter events, 0.3 us)
Async XLA Ops:
  7.2 64.4 %all-gather.5.cloned.1.call-start = ((), (), s32[]{:S(2)}) async-start(), calls=%async_computation.1 | async-start | bytes 9437184 | tf_op jit(solution)/shard_map/all_gather | solution.py:545
  15.0 5.8 %copy-start = (bf16[1024,512]{1,0:T(8,128)(2,1)}, bf16[1024,512]{1,0:T(8,128)(2,1)S(1)}, u32[]{:S(2)}) copy-start(bf16[1024,512]{1,0:T(8,128)(2,1)S(1)} %get-tuple-element.28) | copy-start | bytes 3145732
  15.0 2.1 copy-start.1
  16.4 127.5 %all-gather.9.cloned.1.call-start = ((), (), s32[]{:S(2)}) async-start(), calls=%async_computation.4 | async-start | bytes 9437184 | tf_op jit(solution)/shard_map/all_gather | solution.py:548
  17.1 159.2 %all-gather.7.cloned.1.call-start = ((), (), s32[]{:S(2)}) async-start(), calls=%async_computation.3 | async-start | bytes 9437184 | tf_op jit(solution)/shard_map/all_gather | solution.py:559
  17.4 3.4 copy-start.9
  20.9 2.6 copy-start.10
  23.4 1.0 copy-start.2
  23.4 2.3 copy-start.3
  23.4 2.3 copy-start.4
  23.4 2.3 copy-start.5
  23.4 2.3 copy-start.6
  23.5 2.4 copy-start.7
  23.5 2.4 copy-start.8
  25.7 271.1 %reduce-scatter.2.cloned.1.call-start = ((), (), s32[]{:S(2)}) async-start(), calls=%async_computation.2 | async-start | bytes 18874368 | tf_op jit(solution)/shard_map/reduce_scatter | solution.py:562
  300.0 106.6 %collective-permute-start = (bf16[1024,512]{1,0:T(8,128)(2,1)}, bf16[1024,512]{1,0:T(8,128)(2,1)}, u32[]{:S(2)}, u32[]{:S(2)}) collective-permute-start(bf16[1024,512]{1,0:T(8,128)(2,1)} %fusion.20), channel_id=1, source_target_pairs={{0,8},{8,0},{1,9},{9,1},{2,10},{10,2},{3,11},{11,3},{4,12},{12,4},... | collective-permute-start | bytes 3145736 | tf_op jit(solution)/shard_map/ppermute | solution.py:567
Sparse Core Ops, SparseCore 0:
  16.5 55.0 all-gather.4
  73.4 50.2 all-gather.8
  126.1 50.1 all-gather.6
  179.7 109.6 reduce-scatter.1

commit v4 on v3

--- a/solution.py
+++ b/solution.py
@@ -10,7 +10,9 @@
 NORM_EPS = 1e-6
 CHUNK = 16
 BLOCK = 64
-ROW_TILE = 512
+UNROLL = 4
+ROW_TILE = 1024
+COMB_TILE = 512
 BIG_TILE = 512
 SMALL_TILE = 256
 VMEM_BYTES = 66_500_000
@@ -51,16 +53,21 @@
     return pl.ds(pl.multiple_of(index, CHUNK), count)
 
 
-def fill_onehot(hot_ref, pos_ref, gate_ref, chunks_ref, src, n_local):
-    tok_rows = pos_ref.shape[3]
+def fill_onehot(hot_ref, rep, pos_ref, gate_ref, chunks_ref, src, n_local):
+    tok_rows = pos_ref.shape[2]
     iota = lax.broadcasted_iota(jnp.int32, (CHUNK, tok_rows), 0).astype(F32).astype(BF16)
-
-    def body(expert, start):
+    ones = jnp.ones((CHUNK, tok_rows), BF16)
+    for expert in range(n_local):
+        rep[0, expert] = jnp.broadcast_to(pos_ref[0, expert:expert + 1, :], (CHUNK, tok_rows)).astype(BF16)
+        if gate_ref is not None:
+            rep[1, expert] = jnp.broadcast_to(gate_ref[0, expert:expert + 1, :], (CHUNK, tok_rows)).astype(BF16)
+
+    def one(expert, start):
         n_chunks = chunks_ref[src, expert]
 
         def block(first):
-            pos_rows = pos_ref[0, expert]
-            value = jnp.ones((CHUNK, tok_rows), BF16) if gate_ref is None else gate_ref[0, expert]
+            pos_rows = rep[0, expert]
+            value = ones if gate_ref is None else rep[1, expert]
             for c in range(first, first + BLOCK // CHUNK):
                 hot = jnp.where(iota + jnp.bfloat16(c * CHUNK) == pos_rows, value, jnp.zeros_like(value))
                 hot_ref[rows_at(start + c * CHUNK, CHUNK), :] = hot
@@ -69,7 +76,16 @@
         pl.when(n_chunks > BLOCK // CHUNK)(functools.partial(block, BLOCK // CHUNK))
         return start + n_chunks * CHUNK
 
-    return lax.fori_loop(0, n_local, body, jnp.int32(0))
+    return expert_loop(n_local, one)
+
+
+def expert_loop(n_local, one):
+    def body(group, start):
+        for i in range(UNROLL):
+            start = one(group * UNROLL + i, start)
+        return start
+
+    return lax.fori_loop(0, n_local // UNROLL, body, jnp.int32(0))
 
 
 def zero_tail(ref, offset, length, tile):
@@ -80,11 +96,10 @@
         return carry
 
     lax.fori_loop(length // CHUNK, n_tiles * (tile // CHUNK), body, 0)
-    return n_tiles
 
 
 def move_segments(pack_ref, wide_ref, base_ref, chunks_ref, src, n_local, cap, to_wide):
-    def body(expert, start):
+    def one(expert, start):
         n_chunks = chunks_ref[src, expert]
         base = expert * cap + base_ref[src, expert]
 
@@ -100,7 +115,7 @@
         pl.when(n_chunks > BLOCK // CHUNK)(functools.partial(block, BLOCK))
         return start + n_chunks * CHUNK
 
-    lax.fori_loop(0, n_local, body, jnp.int32(0))
+    expert_loop(n_local, one)
 
 
 def expert_bases(base_ref, total_ref, chunks_ref, n_src, n_local):
@@ -116,46 +131,39 @@
     lax.fori_loop(0, n_src, body, 0)
 
 
-def dispatch(pack_ref, hot_ref, table_ref, wide_ref, base_ref, chunks_ref, src, n_local, cap, length):
-    def body(tile, carry):
-        rows = rows_at(tile * ROW_TILE, ROW_TILE)
-        pack_ref[rows, :] = dot_nn(hot_ref[rows, :], table_ref[...]).astype(BF16)
-        return carry
-
-    lax.fori_loop(0, (length + ROW_TILE - 1) // ROW_TILE, body, 0)
+def dispatch(pack_ref, hot_ref, table_ref, columns, wide_ref, base_ref, chunks_ref, src, n_local, cap, length):
+    def step(rows):
+        pack_ref[rows, :] = dot_nn(hot_ref[rows, :], table_ref[:, columns]).astype(BF16)
+
+    tiled_rows(0, length, step, ROW_TILE, SMALL_TILE)
     move_segments(pack_ref, wide_ref, base_ref, chunks_ref, src, n_local, cap, True)
 
 
-def combine(out_ref, pack_ref, hot_ref, wide_ref, base_ref, chunks_ref, src, n_local, cap, length, tile):
+def combine(out_ref, pack_ref, hot_ref, wide_ref, base_ref, chunks_ref, src, n_local, cap, length):
     move_segments(pack_ref, wide_ref, base_ref, chunks_ref, src, n_local, cap, False)
-    n_tiles = zero_tail(pack_ref, 0, length, tile)
-    zero_tail(hot_ref, 0, length, tile)
+    zero_tail(pack_ref, 0, length, COMB_TILE)
+    zero_tail(hot_ref, 0, length, COMB_TILE)
     out_ref[...] = jnp.zeros_like(out_ref)
 
-    def body(step, carry):
-        rows = rows_at(step * tile, tile)
+    def step(rows):
         out_ref[...] += dot_tn(hot_ref[rows, :], pack_ref[rows, :])
-        return carry
-
-    lax.fori_loop(0, n_tiles, body, 0)
-
-
-def tiled_rows(first, count, step):
-    n_small = (count + SMALL_TILE - 1) // SMALL_TILE
-    per_big = BIG_TILE // SMALL_TILE
+
+    tiled_rows(0, length, step, ROW_TILE, COMB_TILE)
+
+
+def tiled_rows(first, count, step, big_tile, small_tile):
+    n_small = (count + small_tile - 1) // small_tile
+    per_big = big_tile // small_tile
     n_big = n_small // per_big
 
     def big(tile, carry):
-        step(rows_at(first + tile * BIG_TILE, BIG_TILE))
-        return carry
-
-    def small(tile, carry):
-        step(rows_at(first + n_big * BIG_TILE + tile * SMALL_TILE, SMALL_TILE))
+        step(rows_at(first + tile * big_tile, big_tile))
         return carry
 
     lax.fori_loop(0, n_big, big, 0)
-    if per_big > 1:
-        lax.fori_loop(0, n_small - n_big * per_big, small, 0)
+    for left in range(1, per_big):
+        pl.when(n_small - n_big * per_big == left)(
+            functools.partial(step, rows_at(first + n_big * big_tile, left * small_tile)))
 
 
 def weight_copies(expert, slot, wg_ref, wu_ref, wd_ref, gu_buf, dn_buf, sems):
@@ -181,9 +189,9 @@
 
 
 def forward_kernel(n_src, n_local, cap, chunks_ref, tok_ref, pos_ref, gate_ref, wg_ref, wu_ref, wd_ref, out_ref,
-                   wide, hot, pack, gu_buf, dn_buf, base, total, sems):
+                   wide, hot, rep, pack, gu_buf, dn_buf, base, total, sems):
     step = pl.program_id(0)
-    ff = wg_ref.shape[2]
+    hidden, ff = wg_ref.shape[1:]
     w_refs = (wg_ref, wu_ref, wd_ref, gu_buf, dn_buf, sems)
 
     @pl.when(step == 0)
@@ -194,8 +202,8 @@
 
     @pl.when(step < n_src)
     def _():
-        length = fill_onehot(hot, pos_ref, None, chunks_ref, step, n_local)
-        dispatch(pack, hot, tok_ref, wide, base, chunks_ref, step, n_local, cap, length)
+        length = fill_onehot(hot, rep, pos_ref, None, chunks_ref, step, n_local)
+        dispatch(pack, hot, tok_ref, pl.ds(0, hidden), wide, base, chunks_ref, step, n_local, cap, length)
 
     @pl.when((step >= n_src) & (step < n_src + n_local))
     def _():
@@ -208,20 +216,20 @@
             act = (gate * jax.nn.sigmoid(gate) * pre[:, ff:]).astype(BF16)
             wide[rows, :] = dot_nn(act, dn_buf[slot]).astype(BF16)
 
-        tiled_rows(expert * cap, total[expert], rows_step)
+        tiled_rows(expert * cap, total[expert], rows_step, BIG_TILE, SMALL_TILE)
 
     @pl.when(step >= n_src + n_local)
     def _():
         src = step - n_src - n_local
-        length = fill_onehot(hot, pos_ref, gate_ref, chunks_ref, src, n_local)
-        combine(out_ref, pack, hot, wide, base, chunks_ref, src, n_local, cap, length, ROW_TILE)
-
-
-def backward_kernel(n_src, n_local, cap, chunks_ref, tok_ref, grad_ref, pos_ref, gate_ref, wg_ref, wu_ref, wd_ref,
+        length = fill_onehot(hot, rep, pos_ref, gate_ref, chunks_ref, src, n_local)
+        combine(out_ref, pack, hot, wide, base, chunks_ref, src, n_local, cap, length)
+
+
+def backward_kernel(n_src, n_local, cap, chunks_ref, tok_ref, pos_ref, gate_ref, wg_ref, wu_ref, wd_ref,
                     out_ref, dwg_ref, dwu_ref, dwd_ref,
-                    wide_x, wide_q, hot, pack, gu_buf, dn_buf, base, total, sems):
+                    wide_x, wide_q, hot, rep, pack, gu_buf, dn_buf, base, total, sems):
     step = pl.program_id(0)
-    ff = wg_ref.shape[2]
+    hidden, ff = wg_ref.shape[1:]
     w_refs = (wg_ref, wu_ref, wd_ref, gu_buf, dn_buf, sems)
 
     @pl.when(step == 0)
@@ -232,10 +240,10 @@
 
     @pl.when(step < n_src)
     def _():
-        length = fill_onehot(hot, pos_ref, None, chunks_ref, step, n_local)
-        dispatch(pack, hot, tok_ref, wide_x, base, chunks_ref, step, n_local, cap, length)
-        fill_onehot(hot, pos_ref, gate_ref, chunks_ref, step, n_local)
-        dispatch(pack, hot, grad_ref, wide_q, base, chunks_ref, step, n_local, cap, length)
+        length = fill_onehot(hot, rep, pos_ref, None, chunks_ref, step, n_local)
+        dispatch(pack, hot, tok_ref, pl.ds(0, hidden), wide_x, base, chunks_ref, step, n_local, cap, length)
+        fill_onehot(hot, rep, pos_ref, gate_ref, chunks_ref, step, n_local)
+        dispatch(pack, hot, tok_ref, pl.ds(hidden, hidden), wide_q, base, chunks_ref, step, n_local, cap, length)
 
     @pl.when((step >= n_src) & (step < n_src + n_local))
     def _():
@@ -265,17 +273,17 @@
             dwu_ref[0] += dw_pre[:, ff:]
             wide_x[rows, :] = dot_nt(grad_pre, gu_buf[slot]).astype(BF16)
 
-        tiled_rows(expert * cap, total[expert], rows_step)
+        tiled_rows(expert * cap, total[expert], rows_step, BIG_TILE, SMALL_TILE)
 
     @pl.when(step >= n_src + n_local)
     def _():
         src = step - n_src - n_local
-        length = fill_onehot(hot, pos_ref, None, chunks_ref, src, n_local)
-        combine(out_ref, pack, hot, wide_x, base, chunks_ref, src, n_local, cap, length, ROW_TILE)
-
-
-def expert_call(backward, chunks, tables, pos, gate, w_gate, w_up, w_down):
-    n_src, n_local, _, tok_rows = pos.shape
+        length = fill_onehot(hot, rep, pos_ref, None, chunks_ref, src, n_local)
+        combine(out_ref, pack, hot, wide_x, base, chunks_ref, src, n_local, cap, length)
+
+
+def expert_call(backward, chunks, table, pos, gate, w_gate, w_up, w_down):
+    n_src, n_local, tok_rows = pos.shape
     hidden, ff = w_gate.shape[1:]
     cap = n_src * 128 + BLOCK
     pack_rows = n_local * 128 + BLOCK
@@ -290,10 +298,10 @@
     def weight_out(i, *_):
         return (jnp.clip(i - n_src, 0, n_local - 1), 0, 0)
 
-    table_spec = pl.BlockSpec((tok_rows, hidden), src_in)
+    table_spec = pl.BlockSpec((tok_rows, table.shape[1]), src_in)
 
     def route_in(i, *_):
-        return (jnp.where(i < n_src, i, jnp.clip(i - n_src - n_local, 0, n_src - 1)), 0, 0, 0)
+        return (jnp.where(i < n_src, i, jnp.clip(i - n_src - n_local, 0, n_src - 1)), 0, 0)
 
     route_spec = pl.BlockSpec((1,) + pos.shape[1:], route_in)
     raw = pl.BlockSpec(memory_space=pl.ANY)
@@ -307,6 +315,7 @@
         scratch += [wide]
     scratch += [
         pltpu.VMEM((pack_rows, tok_rows), BF16),
+        pltpu.VMEM((2, n_local, CHUNK, tok_rows), BF16),
         pltpu.VMEM((pack_rows, hidden), BF16),
         pltpu.VMEM((2, hidden, 2 * ff), BF16),
         pltpu.VMEM((2, ff, hidden), BF16),
@@ -321,7 +330,7 @@
         grid_spec=pltpu.PrefetchScalarGridSpec(
             num_scalar_prefetch=1,
             grid=(steps,),
-            in_specs=[table_spec] * len(tables) + [route_spec, route_spec, raw, raw, raw],
+            in_specs=[table_spec] + [route_spec, route_spec, raw, raw, raw],
             out_specs=out_specs,
             scratch_shapes=scratch,
         ),
@@ -329,7 +338,7 @@
         compiler_params=pltpu.CompilerParams(dimension_semantics=("arbitrary",), vmem_limit_bytes=VMEM_BYTES),
         cost_estimate=pl.CostEstimate(flops=flops, bytes_accessed=60 * 10 ** 6, transcendentals=0),
         name="expert_backward" if backward else "expert_forward",
-    )(chunks, *tables, pos, gate, w_gate, w_up, w_down)
+    )(chunks, table, pos, gate, w_gate, w_up, w_down)
 
 
 def reduce_tail_kernel(part_ref, h_ref, x_ref, grad_ref, pre_ref, w1_ref, w2_ref, out_ref,
@@ -517,10 +526,9 @@
     gate = jnp.sum(jnp.where(match, gates[:, None], 0.0), axis=2)
     upper = (jnp.arange(tok_rows)[:, None] <= jnp.arange(tok_rows)[None, :]).astype(BF16)
     rank = jnp.einsum("set,tu->seu", kept.astype(BF16), upper, preferred_element_type=F32)
-    pos = jnp.where(kept, rank - 1.0, -1.0).astype(BF16)
+    pos = jnp.where(kept, rank - 1.0, -1.0)
     chunks = (rank[:, :, -1].astype(jnp.int32) + CHUNK - 1) // CHUNK
-    shape = pos.shape[:2] + (CHUNK, tok_rows)
-    return jnp.broadcast_to(pos[:, :, None], shape), jnp.broadcast_to(gate.astype(BF16)[:, :, None], shape), chunks
+    return pos, gate, chunks
 
 
 def solution(mesh):
@@ -545,7 +553,6 @@
         all_fwd = lax.all_gather(xn_fwd, "ep", axis=0, tiled=True)
 
         xn_fwd, x_saved, grad_in = lax.optimization_barrier((xn_fwd, x_saved, grad_in))
-        all_grad = lax.all_gather(grad_in, "ep", axis=0, tiled=True)
         routes = jnp.concatenate([
             jnp.where(slots_fwd >= 0, ids_fwd, -1).astype(BF16), gates_fwd,
             jnp.where(slots_bwd >= 0, ids_bwd, -1).astype(BF16), gates_bwd,
@@ -556,14 +563,14 @@
         pos_b, gate_b, chunks_b = route_tables(id_b, gate_b, first, n_local)
         h_bwd, hidden_pre = dense_forward(x_saved, w_one, w_two)
         xn_bwd = rms_norm(h_bwd.astype(F32)).astype(BF16)
-        all_bwd = lax.all_gather(xn_bwd, "ep", axis=0, tiled=True)
-
-        (part_fwd,) = expert_call(False, chunks_f, (all_fwd,), pos_f, gate_f, w_gate, w_up, w_down)
+        all_bwd = lax.all_gather(jnp.concatenate([xn_bwd, grad_in], axis=1), "ep", axis=0, tiled=True)
+
+        (part_fwd,) = expert_call(False, chunks_f, all_fwd, pos_f, gate_f, w_gate, w_up, w_down)
         mix_sum = lax.psum_scatter(part_fwd, "ep", scatter_dimension=0, tiled=True)
         y_out = (h_fwd.astype(F32) + mix_sum).astype(BF16)
 
         chunks_b, _ = lax.optimization_barrier((chunks_b, part_fwd))
-        part_bwd, dw_gate, dw_up, dw_down = expert_call(True, chunks_b, (all_bwd, all_grad), pos_b, gate_b, w_gate, w_up, w_down)
+        part_bwd, dw_gate, dw_up, dw_down = expert_call(True, chunks_b, all_bwd, pos_b, gate_b, w_gate, w_up, w_down)
         y_next = lax.ppermute(y_out, "pp", next_perm)
         dx_prev = reduce_tail(part_bwd, h_bwd, x_saved, grad_in, hidden_pre, w_one, w_two)
         return y_next[None], dx_prev[None], dw_gate[None], dw_up[None], dw_down[None]

time: 421 us -> 395 us (0.938)
  Pallas kernels: 287 us -> 250 us
  waiting for transfers between devices: 57 us -> 73.4 us
  local copies, waits for them, and re-layouts: 16.5 us -> 6.81 us
    pallas_call x2, Pallas kernels: 181 us -> 148 us  [expert_call(): pl.pallas_call(functools.partial(body, n_src, n_local, cap), grid_spec=pl...]
    reduce_scatter x1, waiting for transfers between devices: 0.02 us -> 18.2 us  [device_step(): mix_sum = lax.psum_scatter(part_fwd, 'ep', scatter_dimension=0, tiled=True)]
    broadcast_in_dim x4 -> x0, local copies, waits for them, and re-layouts: 10.4 us -> none  [the longest x2 5.26 us: route_tables(): jnp.broadcast_to(gate.astype(BF16)[:, :, None], shape)]
    pallas_call x1, Pallas kernels: 107 us -> 102 us  [reduce_tail(): pl.pallas_call(reduce_tail_kernel, out_shape=jax.ShapeDtypeStruct((tok_ro...]
    all_gather x2 -> x1, waiting for transfers between devices: 32.5 us -> 33.5 us  [device_step(): lax.all_gather(jnp.concatenate([xn_bwd, grad_in], axis=1), 'ep', axis=0,...]
  transfers between devices with their start and end apart: 5 -> 4, of which waited for: 2 -> 3; matrix products, arithmetic and copies ran while one was open for 6% -> 5% of each run, Pallas kernels for 69% -> 64%
where the time goes in v4:
time: 395 us; the launch traced here: 391 us
  Pallas kernels  250 us (63%)
  waiting for transfers between devices  73.4 us (19%)
  other arithmetic  16.9 us (4%)
  blocking collectives  14.3 us (4%)
  matrix products  14.2 us (4%)
  between operations  14 us (4%)
  local copies, waits for them, and re-layouts  6.81 us (2%)
    pallas_call x2, Pallas kernels, expert_call(): pl.pallas_call(functools.partial(body, n_src, n_local, cap), grid_spec=pl...  148 us
    pallas_call x1, Pallas kernels, reduce_tail(): pl.pallas_call(reduce_tail_kernel, out_shape=jax.ShapeDtypeStruct((tok_ro...  102 us
    all_gather x1, waiting for transfers between devices, device_step(): lax.all_gather(jnp.concatenate([xn_bwd, grad_in], axis=1), 'ep', axis=0,...  33.5 us
    all_gather x1, waiting for transfers between devices, device_step(): all_fwd = lax.all_gather(xn_fwd, 'ep', axis=0, tiled=True)  21.6 us
    reduce_scatter x1, waiting for transfers between devices, device_step(): mix_sum = lax.psum_scatter(part_fwd, 'ep', scatter_dimension=0, tiled=True)  18.2 us
    all_gather x1, blocking collectives, device_step(): routes = lax.all_gather(routes, 'ep', axis=0, tiled=False).astype(F32)  14.3 us
    dot_general x2, matrix products, dense_forward(): dense_out = jnp.dot(dense_act, w_two, preferred_element_type=F32)  8.33 us
  transfers between devices with their start and end apart: 4, of which 3 were waited for; matrix products, arithmetic and copies ran while one was open for 5% of the time, Pallas kernels for 64%

profile of v4, /device:TPU:0, one launch (start us, length us, event | category | flops | bytes accessed | tf_op | source)
XLA Modules:
  0.0 391.0 jit_solution(2903787161332211993)
XLA Ops:
  7.2 1.5 fusion.15
  8.7 6.3 %fusion.18 = (f32[1024]{0:T(1024)S(1)}, bf16[1024,512]{1,0:T(8,128)(2,1)S(1)}) fusion(bf16[1,1536,512]{2,1,0:T(8,128)(2,1)} %param.24, bf16[1,1024,512]{2,1,0:T(8,128)(2,1)} %param.14, f32[1024]{0:T(1024)S(1)} %add_rsqrt_fusion.3, bf16[1,512,1536]{2,1,0:T(8,128)(2,1)} %param.23), kind=kOutput, calls=%fused_computation.32 | convolution fusion | flops 3233807360 | bytes 5251072 | tf_op jit(solution)/shard_map/dot_general | solution.py:36
  15.1 1.3 fusion.19
  16.3 0.0 all-gather.6.cloned.1.call-start
  16.4 0.6 copy-done.1
  17.0 0.3 fusion.21
  17.3 3.4 fusion.24.pre_ref
  20.7 2.0 fusion.13
  22.8 0.5 copy-done.11
  23.3 1.0 copy-done.2
  24.3 0.3 fusion.14
  24.7 1.6 pad_maximum_fusion
  26.5 14.3 %all-gather = bf16[256,1024]{1,0:T(8,128)(2,1)S(1)} all-gather(bf16[32,1024]{1,0:T(8,128)(2,1)S(1)} %maximum_bitcast_fusion), channel_id=2, replica_groups=mesh['pp'=2,'ep'=8] {'ep'}, dimensions={0}, use_global_device_ids=true | all-gather | bytes 589824 | tf_op jit(solution)/shard_map/all_gather | solution.py:560
  40.7 0.1 fusion.49
  40.9 3.4 compare_reduce_fusion
  44.3 1.2 add_select_fusion.1
  45.5 0.3 fusion.35
  45.8 0.6 add_select_fusion.3.chunks_ref
  46.4 3.6 fusion.1
  50.0 21.6 %all-gather.4.cloned.1.call-done.tok_ref = bf16[8192,512]{1,0:T(8,128)(2,1)} async-done(((bf16[1024,512]{1,0:T(8,128)(2,1)}), bf16[8192,512]{1,0:T(8,128)(2,1)}) %all-gather.4.cloned.1.call-update) | async-done | bytes 8388624 | tf_op jit(solution)/shard_map/all_gather | solution.py:553
  71.6 52.7 %expert_forward.1 = f32[8192,512]{1,0:T(8,128)} custom-call(s32[8,16]{1,0:T(8,128)} %add_select_fusion.3.chunks_ref, bf16[8192,512]{1,0:T(8,128)(2,1)} %all-gather.4.cloned.1.call-done.tok_ref, f32[8,16,1024]{2,1,0:T(8,128)} %get-tuple-element.29.pos_ref, f32[8,16,1024]{2,1,0:T(8,128)} %get-tuple-element.20.gate_ref, bf16[16,512,384]{2,1,0:T(8,128)(2,1)} %bitcast.73, ...), custom_call_target="tpu_custom_call" | custom-call | flops 60000002048 | bytes 60000000 | tf_op jit(solution)/shard_map/expert_forward/pallas_call | solution.py:328
  124.4 1.2 add_select_fusion
  125.6 0.3 fusion.33
  125.9 0.6 add_select_fusion.2.chunks_ref
  126.5 33.5 %all-gather.6.cloned.1.call-done.tok_ref = bf16[8192,1024]{1,0:T(8,128)(2,1)} async-done(((bf16[1024,1024]{1,0:T(8,128)(2,1)}), bf16[8192,1024]{1,0:T(8,128)(2,1)}) %all-gather.6.cloned.1.call-update) | async-done | bytes 16777232 | tf_op jit(solution)/shard_map/all_gather | solution.py:566
  160.0 94.9 %expert_backward.1 = (f32[8192,512]{1,0:T(8,128)}, f32[16,512,384]{2,1,0:T(8,128)}, f32[16,512,384]{2,1,0:T(8,128)}, f32[16,384,512]{2,1,0:T(8,128)}) custom-call(s32[8,16]{1,0:T(8,128)} %add_select_fusion.2.chunks_ref, bf16[8192,1024]{1,0:T(8,128)(2,1)} %all-gather.6.cloned.1.call-done.tok_ref, f32[8,16,1024]{2,1,0:T(8,128)} %get-tuple-element.33.pos_ref, ...), custom_call_target="tpu_custom_call" | custom-call | flops 99999997952 | bytes 60000000 | tf_op jit(solution)/shard_map/expert_backward/pallas_call | solution.py:328
  254.9 18.2 %reduce-scatter.2.cloned.1.call-done = f32[1024,512]{1,0:T(8,128)} async-done(((f32[8192,512]{1,0:T(8,128)}), f32[1024,512]{1,0:T(8,128)}) %reduce-scatter.2.cloned.1.call-update) | async-done | bytes 2097168 | tf_op jit(solution)/shard_map/reduce_scatter | solution.py:569
  273.2 3.2 fusion.20
  276.4 1.5 collective-permute-start
  277.8 102.1 %reduce_tail.1 = bf16[1024,512]{1,0:T(8,128)(2,1)} custom-call(f32[8192,512]{1,0:T(8,128)} %get-tuple-element.15.part_ref, bf16[1024,512]{1,0:T(8,128)(2,1)} %copy-done.2, bf16[1024,512]{1,0:T(8,128)(2,1)} %bitcast.64, bf16[1024,512]{1,0:T(8,128)(2,1)} %bitcast.69, f32[1024,1536]{1,0:T(8,128)} %copy-done.11, bf16[512,1536]{1,0:T(8,128)(2,1)} %bitcast.80, ...), custom_call_target="tpu_custom_call" | custom-call | flops 60000002048 | bytes 40000000 | tf_op jit(solution)/shard_map/reduce_tail/pallas_call | solution.py:495
  380.0 2.3 copy.29
  382.2 2.3 copy.30
  (34 shorter events, 0.2 us)
Async XLA Ops:
  7.2 64.4 %all-gather.4.cloned.1.call-start = ((), (), s32[]{:S(2)}) async-start(), calls=%async_computation.1 | async-start | bytes 9437184 | tf_op jit(solution)/shard_map/all_gather | solution.py:553
  15.0 5.7 %copy-start = (bf16[1024,512]{1,0:T(8,128)(2,1)}, bf16[1024,512]{1,0:T(8,128)(2,1)S(1)}, u32[]{:S(2)}) copy-start(bf16[1024,512]{1,0:T(8,128)(2,1)S(1)} %get-tuple-element.28) | copy-start | bytes 3145732
  15.0 2.0 copy-start.1
  16.3 143.7 %all-gather.6.cloned.1.call-start = ((), (), s32[]{:S(2)}) async-start(), calls=%async_computation.3 | async-start | bytes 18874368 | tf_op jit(solution)/shard_map/all_gather | solution.py:566
  17.3 3.4 copy-start.10
  20.7 2.6 copy-start.11
  20.7 3.8 copy-start.3
  23.3 1.0 copy-start.2
  24.6 1.8 copy-start.4
  24.6 1.8 copy-start.5
  24.6 1.8 copy-start.6
  24.6 1.8 copy-start.7
  24.6 1.8 copy-start.8
  24.6 1.8 copy-start.9
  26.3 246.9 %reduce-scatter.2.cloned.1.call-start = ((), (), s32[]{:S(2)}) async-start(), calls=%async_computation.2 | async-start | bytes 18874368 | tf_op jit(solution)/shard_map/reduce_scatter | solution.py:569
  276.4 103.6 %collective-permute-start = (bf16[1024,512]{1,0:T(8,128)(2,1)}, bf16[1024,512]{1,0:T(8,128)(2,1)}, u32[]{:S(2)}, u32[]{:S(2)}) collective-permute-start(bf16[1024,512]{1,0:T(8,128)(2,1)} %fusion.20), channel_id=1, source_target_pairs={{0,8},{8,0},{1,9},{9,1},{2,10},{10,2},{3,11},{11,3},{4,12},{12,4},... | collective-permute-start | bytes 3145736 | tf_op jit(solution)/shard_map/ppermute | solution.py:574
Sparse Core Ops, SparseCore 0:
  16.5 55.0 all-gather.3
  74.0 85.9 all-gather.5
  163.5 109.6 reduce-scatter.1

commit v5 on v4

--- a/solution.py
+++ b/solution.py
@@ -27,14 +27,6 @@
 def silu_grad(values):
     sigmoid_vals = jax.nn.sigmoid(values)
     return sigmoid_vals * (1.0 + values * (1.0 - sigmoid_vals))
-
-
-def dense_forward(x_rows, w_one, w_two):
-    normed = rms_norm(x_rows.astype(F32)).astype(BF16)
-    hidden_pre = jnp.dot(normed, w_one, preferred_element_type=F32)
-    dense_act = jax.nn.silu(hidden_pre).astype(BF16)
-    dense_out = jnp.dot(dense_act, w_two, preferred_element_type=F32)
-    return (x_rows.astype(F32) + dense_out).astype(BF16), hidden_pre
 
 
 def dot_nn(lhs, rhs):
@@ -518,17 +510,223 @@
     )(part, h_rows, x_rows, grad_rows, hidden_pre, w_one, w_two)
 
 
-def route_tables(ids, gates, first, n_local):
-    tok_rows = ids.shape[2]
-    experts = (first + jnp.arange(n_local)).astype(F32)
-    match = ids[:, None] == experts[None, :, None, None]
-    kept = jnp.any(match, axis=2)
-    gate = jnp.sum(jnp.where(match, gates[:, None], 0.0), axis=2)
-    upper = (jnp.arange(tok_rows)[:, None] <= jnp.arange(tok_rows)[None, :]).astype(BF16)
-    rank = jnp.einsum("set,tu->seu", kept.astype(BF16), upper, preferred_element_type=F32)
-    pos = jnp.where(kept, rank - 1.0, -1.0)
-    chunks = (rank[:, :, -1].astype(jnp.int32) + CHUNK - 1) // CHUNK
-    return pos, gate, chunks
+def head_kernel(x_ref, saved_ref, grad_ref, w1_ref, w2_ref, routes_ref,
+                all_ref, h_ref, saved_h_ref, pre_ref, pair_ref, pos_f_ref, gate_f_ref, pos_b_ref, gate_b_ref, count_ref,
+                normed, pre_buf, routes, kept, own_sem, pre_sem, first_send, first_recv, hop_send, hop_recv, core_send, core_recv):
+    tok_rows = x_ref.shape[0]
+    n_chunks = first_send.shape[0] - 1
+    n_src = routes.shape[0]
+    n_local = kept.shape[0] // (2 * n_src)
+    top_k = routes_ref.shape[0] // 4
+    chunk = tok_rows // n_chunks
+    me = lax.axis_index("ep")
+    core, x_pos, y_pos = lax.rem(me, 2), lax.rem(me // 2, 2), me // 4
+    x_step, y_step = 2 - 4 * x_pos, 4 - 8 * y_pos
+    partner = me + 1 - 2 * core
+    x_peer, y_peer, far_peer = me + x_step, me + y_step, me + x_step + y_step
+    mesh_id = pl.DeviceIdType.MESH
+
+    barrier = pltpu.get_barrier_semaphore()
+    for peer in (partner, x_peer, y_peer):
+        pl.semaphore_signal(barrier, inc=1, device_id={"ep": peer}, device_id_type=mesh_id)
+    pl.semaphore_wait(barrier, 3)
+
+    def chunk_rows(c):
+        return pl.ds(pl.multiple_of(c * chunk, chunk), chunk)
+
+    def view(c, src, part):
+        if isinstance(c, int) and c == n_chunks:
+            size = routes.shape[1] // 2
+            return routes.at[src] if part is None else routes.at[src, pl.ds(part * size, size)]
+        first = src * tok_rows + c * chunk
+        if part is None:
+            return all_ref.at[pl.ds(pl.multiple_of(first, chunk), chunk)]
+        return all_ref.at[pl.ds(pl.multiple_of(first + part * (chunk // 2), chunk // 2), chunk // 2)]
+
+    def remote(src, dst, send, recv, peer):
+        return pltpu.make_async_remote_copy(src, dst, send, recv, device_id={"ep": peer}, device_id_type=mesh_id)
+
+    def first_copy(c, n):
+        own = routes_ref if isinstance(c, int) and c == n_chunks else normed.at[chunk_rows(c)]
+        return remote(own, view(c, me, None), first_send.at[c, n], first_recv.at[c, n], (partner, x_peer, y_peer)[n])
+
+    def hop_copy(c, n):
+        piece = view(c, (x_peer, y_peer)[n], n)
+        return remote(piece, piece, hop_send.at[c, n], hop_recv.at[c, n], (y_peer, x_peer)[n])
+
+    def core_copy(c, n):
+        piece = view(c, *((x_peer, None), (y_peer, None), (far_peer, 0), (far_peer, 1))[n])
+        return remote(piece, piece, core_send.at[c, n], core_recv.at[c, n], partner)
+
+    def own_copy(c):
+        return pltpu.make_async_copy(normed.at[chunk_rows(c)], view(c, me, None), own_sem.at[c])
+
+    def pass_on(c):
+        for n in range(2):
+            first_copy(c, n + 1).wait_recv()
+            hop_copy(c, n).start()
+            core_copy(c, n).start()
+
+    def pass_far(c):
+        for n in range(2):
+            hop_copy(c, n).wait_recv()
+            core_copy(c, n + 2).start()
+
+    def arrive(c):
+        first_copy(c, 0).wait_recv()
+        for n in range(4):
+            core_copy(c, n).wait_recv()
+
+    def drain(c):
+        for n in range(3):
+            first_copy(c, n).wait_send()
+        for n in range(2):
+            hop_copy(c, n).wait_send()
+        for n in range(4):
+            core_copy(c, n).wait_send()
+
+    def dense_rows(x_rows):
+        pre = dot_nn(rms_norm(x_rows).astype(BF16), w1_ref[...])
+        act = (pre * jax.nn.sigmoid(pre)).astype(BF16)
+        hidden = (x_rows + dot_nn(act, w2_ref[...])).astype(BF16)
+        return pre, hidden, rms_norm(hidden.astype(F32)).astype(BF16)
+
+    def dense(c):
+        rows = chunk_rows(c)
+        _, h_ref[rows, :], normed[rows, :] = dense_rows(x_ref[rows, :].astype(F32))
+
+    def pre_copy(c):
+        return pltpu.make_async_copy(pre_buf.at[chunk_rows(c)], pre_ref.at[chunk_rows(c)], pre_sem.at[c])
+
+    def dense_saved(c):
+        rows = chunk_rows(c)
+        width = grad_ref.shape[1]
+        pre_buf[rows, :], saved_h_ref[rows, :], pair_ref[rows, :width] = dense_rows(saved_ref[rows, :].astype(F32))
+        pair_ref[rows, width:] = grad_ref[rows, :]
+        pre_copy(c).start()
+
+    def send(c):
+        for n in (1, 2, 0):
+            first_copy(c, n).start()
+        own_copy(c).start()
+
+    def tables(src):
+        pieces = [routes[src, pl.ds(i * top_k, top_k), :].astype(F32) for i in range(4)] if top_k % CHUNK == 0 else None
+        whole = routes[src].astype(F32) if pieces is None else None
+        if pieces is None:
+            pieces = [whole[i * top_k:(i + 1) * top_k] for i in range(4)]
+        lines = lax.broadcasted_iota(jnp.int32, (n_local, tok_rows), 0)
+
+        def body(expert, carry):
+            wanted = (me * n_local + expert).astype(F32)
+            out = []
+            for batch in range(2):
+                match = pieces[2 * batch] == wanted
+                here = lines == expert
+                hit = jnp.max(jnp.where(match, 1.0, 0.0), axis=0, keepdims=True)
+                gate = jnp.sum(jnp.where(match, pieces[2 * batch + 1], 0.0), axis=0, keepdims=True)
+                out += [jnp.where(here, hit, carry[2 * batch]), jnp.where(here, gate, carry[2 * batch + 1])]
+            return tuple(out)
+
+        zero = jnp.zeros((n_local, tok_rows), F32)
+        hit_f, gate_f, hit_b, gate_b = lax.fori_loop(0, n_local, body, (zero,) * 4)
+        rows = pl.ds(pl.multiple_of(src * n_local, n_local), n_local)
+        low_rows = pl.ds(pl.multiple_of((n_src + src) * n_local, n_local), n_local)
+        gate_f_ref[rows, :] = gate_f
+        gate_b_ref[rows, :] = gate_b
+        kept[rows, :] = hit_f.astype(BF16)
+        kept[low_rows, :] = hit_b.astype(BF16)
+
+    def ranks():
+        width = 256
+        hits = kept[...]
+        half = n_src * n_local
+        for first in range(0, tok_rows, width):
+            upto = lax.broadcasted_iota(jnp.int32, (tok_rows, width), 1) + first
+            upper = jnp.where(lax.broadcasted_iota(jnp.int32, (tok_rows, width), 0) <= upto, 1.0, 0.0).astype(BF16)
+            rank = dot_nn(hits, upper)
+            pos = jnp.where(kept[:, first:first + width].astype(F32) > 0.0, rank - 1.0, -1.0)
+            pos_f_ref[:, first:first + width] = pos[:half]
+            pos_b_ref[:, first:first + width] = pos[half:]
+            if first + width == tok_rows:
+                count_ref[...] = rank[:, width - 128:]
+
+    routes[me] = routes_ref[...]
+    for n in (1, 2, 0):
+        first_copy(n_chunks, n).start()
+    dense(0)
+    pass_on(n_chunks)
+    send(0)
+
+    def dense_send(c, carry):
+        dense(c)
+        send(c)
+        return carry
+
+    lax.fori_loop(1, n_chunks, dense_send, 0)
+    pass_far(n_chunks)
+    arrive(n_chunks)
+
+    def forward(c, carry):
+        pass_on(c)
+        for i in range(n_src // n_chunks):
+            tables(c * (n_src // n_chunks) + i)
+        dense_saved(c)
+        return carry
+
+    lax.fori_loop(0, n_chunks, forward, 0)
+
+    def far(c, carry):
+        pass_far(c)
+        return carry
+
+    lax.fori_loop(0, n_chunks - 1, far, 0)
+    ranks()
+    lax.fori_loop(n_chunks - 1, n_chunks, far, 0)
+
+    def finish(c, carry):
+        arrive(c)
+        own_copy(c).wait()
+        pre_copy(c).wait()
+        drain(c)
+        return carry
+
+    lax.fori_loop(0, n_chunks, finish, 0)
+    drain(n_chunks)
+
+
+def head(x_rows, saved_rows, grad_rows, w_one, w_two, routes, n_src, n_local):
+    tok_rows, hidden = x_rows.shape
+    ff = w_one.shape[1]
+    n_chunks = 4
+    dma = pltpu.SemaphoreType.DMA
+    vmem = pl.BlockSpec(memory_space=pltpu.VMEM)
+    raw = pl.BlockSpec(memory_space=pl.ANY)
+    table = jax.ShapeDtypeStruct((n_src * n_local, tok_rows), F32)
+    return pl.pallas_call(
+        head_kernel,
+        out_shape=[
+            jax.ShapeDtypeStruct((n_src * tok_rows, hidden), BF16), jax.ShapeDtypeStruct((tok_rows, hidden), BF16),
+            jax.ShapeDtypeStruct((tok_rows, hidden), BF16), jax.ShapeDtypeStruct((tok_rows, ff), F32),
+            jax.ShapeDtypeStruct((tok_rows, 2 * hidden), BF16),
+            table, table, table, table, jax.ShapeDtypeStruct((2 * n_src * n_local, 128), F32),
+        ],
+        in_specs=[vmem] * 6,
+        out_specs=[raw, vmem, vmem, raw] + [vmem] * 6,
+        scratch_shapes=[
+            pltpu.VMEM((tok_rows, hidden), BF16),
+            pltpu.VMEM((tok_rows, ff), F32),
+            pltpu.VMEM((n_src,) + routes.shape, BF16),
+            pltpu.VMEM((2 * n_src * n_local, tok_rows), BF16),
+            dma((n_chunks,)), dma((n_chunks,)),
+            dma((n_chunks + 1, 3)), dma((n_chunks + 1, 3)),
+            dma((n_chunks + 1, 2)), dma((n_chunks + 1, 2)),
+            dma((n_chunks + 1, 4)), dma((n_chunks + 1, 4)),
+        ],
+        compiler_params=pltpu.CompilerParams(collective_id=1, has_side_effects=True, vmem_limit_bytes=VMEM_BYTES),
+        cost_estimate=pl.CostEstimate(flops=30 * 10 ** 9, bytes_accessed=20 * 10 ** 6, transcendentals=0),
+        name="head",
+    )(x_rows, saved_rows, grad_rows, w_one, w_two, routes)
 
 
 def solution(mesh):
@@ -544,32 +742,24 @@
         x_fwd, ids_fwd, slots_fwd, gates_fwd = x_fwd[0], ids_fwd[0], slots_fwd[0], gates_fwd[0]
         x_saved, grad_in, ids_bwd, slots_bwd, gates_bwd = x_saved[0], grad_in[0], ids_bwd[0], slots_bwd[0], gates_bwd[0]
         w_one, w_two, w_gate, w_up, w_down = w_one[0], w_two[0], w_gate[0], w_up[0], w_down[0]
-        top_k = ids_fwd.shape[1]
         n_local = w_gate.shape[0]
-        first = lax.axis_index("ep") * n_local
-
-        h_fwd, _ = dense_forward(x_fwd, w_one, w_two)
-        xn_fwd = rms_norm(h_fwd.astype(F32)).astype(BF16)
-        all_fwd = lax.all_gather(xn_fwd, "ep", axis=0, tiled=True)
-
-        xn_fwd, x_saved, grad_in = lax.optimization_barrier((xn_fwd, x_saved, grad_in))
+
         routes = jnp.concatenate([
             jnp.where(slots_fwd >= 0, ids_fwd, -1).astype(BF16), gates_fwd,
             jnp.where(slots_bwd >= 0, ids_bwd, -1).astype(BF16), gates_bwd,
         ], axis=1).T
-        routes = lax.all_gather(routes, "ep", axis=0, tiled=False).astype(F32)
-        id_f, gate_f, id_b, gate_b = (routes[:, i * top_k:(i + 1) * top_k] for i in range(4))
-        pos_f, gate_f, chunks_f = route_tables(id_f, gate_f, first, n_local)
-        pos_b, gate_b, chunks_b = route_tables(id_b, gate_b, first, n_local)
-        h_bwd, hidden_pre = dense_forward(x_saved, w_one, w_two)
-        xn_bwd = rms_norm(h_bwd.astype(F32)).astype(BF16)
-        all_bwd = lax.all_gather(jnp.concatenate([xn_bwd, grad_in], axis=1), "ep", axis=0, tiled=True)
+        all_fwd, h_fwd, h_bwd, hidden_pre, pair, pos_f, gate_f, pos_b, gate_b, counts = head(
+            x_fwd, x_saved, grad_in, w_one, w_two, routes, ep_size, n_local)
+        all_bwd = lax.all_gather(pair, "ep", axis=0, tiled=True)
+        pos_f, gate_f, pos_b, gate_b = (t.reshape(ep_size, n_local, -1) for t in (pos_f, gate_f, pos_b, gate_b))
+        chunks = (counts[:, -1].reshape(2, ep_size, n_local).astype(jnp.int32) + CHUNK - 1) // CHUNK
+        chunks_f, chunks_b = chunks[0], chunks[1]
 
         (part_fwd,) = expert_call(False, chunks_f, all_fwd, pos_f, gate_f, w_gate, w_up, w_down)
+        part_fwd, all_bwd = lax.optimization_barrier((part_fwd, all_bwd))
         mix_sum = lax.psum_scatter(part_fwd, "ep", scatter_dimension=0, tiled=True)
         y_out = (h_fwd.astype(F32) + mix_sum).astype(BF16)
 
-        chunks_b, _ = lax.optimization_barrier((chunks_b, part_fwd))
         part_bwd, dw_gate, dw_up, dw_down = expert_call(True, chunks_b, all_bwd, pos_b, gate_b, w_gate, w_up, w_down)
         y_next = lax.ppermute(y_out, "pp", next_perm)
         dx_prev = reduce_tail(part_bwd, h_bwd, x_saved, grad_in, hidden_pre, w_one, w_two)

time: 395 us -> 380 us (0.962)
  Pallas kernels: 250 us -> 321 us
  waiting for transfers between devices: 73.4 us -> 24.8 us
  blocking collectives: 14.3 us -> 0 us
  matrix products: 14.2 us -> 0 us
  other arithmetic: 16.9 us -> 6.46 us
    pallas_call x0 -> x1, Pallas kernels: none -> 49.4 us  [head(): pl.pallas_call(head_kernel, out_shape=[jax.ShapeDtypeStruct((n_src * tok_...]
    all_gather x2 -> x1, waiting for transfers between devices: 55.1 us -> 16.8 us  [device_step(): all_bwd = lax.all_gather(pair, 'ep', axis=0, tiled=True)]
    pallas_call x2, Pallas kernels: 148 us -> 173 us  [expert_call(): pl.pallas_call(functools.partial(body, n_src, n_local, cap), grid_spec=pl...]
    all_gather x1 -> x0, blocking collectives: 14.3 us -> none  [device_step(): routes = lax.all_gather(routes, 'ep', axis=0, tiled=False).astype(F32)]
    dot_general x5 -> x0, matrix products: 14.2 us -> none  [the longest x2 8.33 us: dense_forward(): dense_out = jnp.dot(dense_act, w_two, preferred_element_type=F32)]
    reduce_scatter x1, waiting for transfers between devices: 18.2 us -> 7.91 us  [device_step(): mix_sum = lax.psum_scatter(part_fwd, 'ep', scatter_dimension=0, tiled=True)]
    reduce_sum x3 -> x0, other arithmetic: 5.34 us -> none  [the longest x1 3.57 us: route_tables(): gate = jnp.sum(jnp.where(match, gates[:, None], 0.0), axis=2)]
  transfers between devices with their start and end apart: 4 -> 3, of which waited for: 3 -> 2; matrix products, arithmetic and copies ran while one was open for 5% -> 0% of each run, Pallas kernels for 64% -> 73%
where the time goes in v5:
time: 380 us; the launch traced here: 373 us
  Pallas kernels  321 us (84%)
  waiting for transfers between devices  24.8 us (7%)
  between operations  14.1 us (4%)
  other arithmetic  6.46 us (2%)
  local copies, waits for them, and re-layouts  5.21 us (1%)
    pallas_call x2, Pallas kernels, expert_call(): pl.pallas_call(functools.partial(body, n_src, n_local, cap), grid_spec=pl...  173 us
    pallas_call x1, Pallas kernels, reduce_tail(): pl.pallas_call(reduce_tail_kernel, out_shape=jax.ShapeDtypeStruct((tok_ro...  99.2 us
    pallas_call x1, Pallas kernels, head(): pl.pallas_call(head_kernel, out_shape=[jax.ShapeDtypeStruct((n_src * tok_...  49.4 us
    all_gather x1, waiting for transfers between devices, device_step(): all_bwd = lax.all_gather(pair, 'ep', axis=0, tiled=True)  16.8 us
    reduce_scatter x1, waiting for transfers between devices, device_step(): mix_sum = lax.psum_scatter(part_fwd, 'ep', scatter_dimension=0, tiled=True)  7.91 us
  transfers between devices with their start and end apart: 3, of which 2 were waited for; matrix products, arithmetic and copies ran while one was open for 0% of the time, Pallas kernels for 73%

profile of v5, /device:TPU:0, one launch (start us, length us, event | category | flops | bytes accessed | tf_op | source)
XLA Modules:
  0.0 373.3 jit_solution(12854833881784032918)
XLA Ops:
  7.2 0.0 all-gather.2.cloned.1.call-start
  7.2 0.8 fusion
  8.0 1.4 maximum_bitcast_fusion.routes_ref
  9.4 49.4 %head.1 = (bf16[8192,512]{1,0:T(8,128)(2,1)}, bf16[1024,512]{1,0:T(8,128)(2,1)}, bf16[1024,512]{1,0:T(8,128)(2,1)}, f32[1024,1536]{1,0:T(8,128)}, bf16[1024,1024...) custom-call(bf16[1024,512]{1,0:T(8,128)(2,1)} %bitcast.42, ...), custom_call_target="tpu_custom_call" | custom-call | flops 30000001024 | bytes 20000000 | tf_op jit(solution)/shard_map/head/pallas_call | solution.py:706
  58.8 0.0 all-gather.2.cloned.1.call-update
  58.9 0.0 reduce-scatter.2.cloned.1.call-start
  58.9 1.1 add_reduce_fusion
  60.0 0.1 sub.18
  60.1 0.6 slice_bitcast_fusion
  60.7 67.3 %expert_forward.1 = f32[8192,512]{1,0:T(8,128)} custom-call(s32[8,16]{1,0:T(8,128)} %get-tuple-element.38.chunks_ref, bf16[8192,512]{1,0:T(8,128)(2,1)} %get-tuple-element.23.tok_ref, f32[8,16,1024]{2,1,0:T(8,128)} %bitcast.52, f32[8,16,1024]{2,1,0:T(8,128)} %bitcast.53, bf16[16,512,384]{2,1,0:T(8,128)(2,1)} %bitcast.32, bf16[16,512,384]{2,1,0:T(8,128)(2,1)} %bitcast.34, ...), custom_call_target="tpu_custom_call" | custom-call | flops 60000002048 | bytes 60000000 | tf_op jit(solution)/shard_map/expert_forward/pallas_call | solution.py:320
  128.0 16.8 %all-gather.2.cloned.1.call-done.tok_ref = bf16[8192,1024]{1,0:T(8,128)(2,1)} async-done(((bf16[1024,1024]{1,0:T(8,128)(2,1)}), bf16[8192,1024]{1,0:T(8,128)(2,1)}) %all-gather.2.cloned.1.call-update) | async-done | bytes 16777232 | tf_op jit(solution)/shard_map/all_gather | solution.py:753
  144.8 0.0 reduce-scatter.2.cloned.1.call-update
  144.9 105.3 %expert_backward.1 = (f32[8192,512]{1,0:T(8,128)}, f32[16,512,384]{2,1,0:T(8,128)}, f32[16,512,384]{2,1,0:T(8,128)}, f32[16,384,512]{2,1,0:T(8,128)}) custom-call(s32[8,16]{1,0:T(8,128)} %get-tuple-element.37.chunks_ref, bf16[8192,1024]{1,0:T(8,128)(2,1)} %all-gather.2.cloned.1.call-done.tok_ref, f32[8,16,1024]{2,1,0:T(8,128)} %bitcast.50, ...), custom_call_target="tpu_custom_call" | custom-call | flops 99999997952 | bytes 60000000 | tf_op jit(solution)/shard_map/expert_backward/pallas_call | solution.py:320
  250.2 7.9 %reduce-scatter.2.cloned.1.call-done = f32[1024,512]{1,0:T(8,128)} async-done(((f32[8192,512]{1,0:T(8,128)}), f32[1024,512]{1,0:T(8,128)}) %reduce-scatter.2.cloned.1.call-update) | async-done | bytes 2097168 | tf_op jit(solution)/shard_map/reduce_scatter | solution.py:760
  258.1 3.2 add_convert_fusion
  261.3 1.5 collective-permute-start
  262.8 99.2 %reduce_tail.1 = bf16[1024,512]{1,0:T(8,128)(2,1)} custom-call(f32[8192,512]{1,0:T(8,128)} %get-tuple-element.31.part_ref, bf16[1024,512]{1,0:T(8,128)(2,1)} %get-tuple-element.32.h_ref, bf16[1024,512]{1,0:T(8,128)(2,1)} %bitcast.44, bf16[1024,512]{1,0:T(8,128)(2,1)} %bitcast.46, f32[1024,1536]{1,0:T(8,128)} %get-tuple-element.33.pre_ref, ...), custom_call_target="tpu_custom_call" | custom-call | flops 60000002048 | bytes 40000000 | tf_op jit(solution)/shard_map/reduce_tail/pallas_call | solution.py:487
  361.9 0.0 collective-permute-done
  361.9 2.3 copy.21
  364.2 2.3 copy.22
  (1 shorter events, 0.0 us)
Async XLA Ops:
  7.2 137.7 %all-gather.2.cloned.1.call-start = ((), (), s32[]{:S(2)}) async-start(), calls=%async_computation.1 | async-start | bytes 18874368 | tf_op jit(solution)/shard_map/all_gather | solution.py:753
  58.9 199.2 %reduce-scatter.2.cloned.1.call-start = ((), (), s32[]{:S(2)}) async-start(), calls=%async_computation.2 | async-start | bytes 18874368 | tf_op jit(solution)/shard_map/reduce_scatter | solution.py:760
  261.3 100.7 %collective-permute-start = (bf16[1024,512]{1,0:T(8,128)(2,1)}, bf16[1024,512]{1,0:T(8,128)(2,1)}, u32[]{:S(2)}, u32[]{:S(2)}) collective-permute-start(bf16[1024,512]{1,0:T(8,128)(2,1)} %add_convert_fusion), channel_id=1, source_target_pairs={{0,8},{8,0},{1,9},{9,1},{2,10},{10,2},{3,11},{11,3},{4,12},{12,4},... | collective-permute-start | bytes 3145736 | tf_op jit(solution)/shard_map/ppermute | solution.py:764
Sparse Core Ops, SparseCore 0:
  59.0 85.8 all-gather.1
  148.4 109.7 reduce-scatter.1

commit v6 on v5

--- a/solution.py
+++ b/solution.py
@@ -10,10 +10,10 @@
 NORM_EPS = 1e-6
 CHUNK = 16
 BLOCK = 64
-UNROLL = 4
+UNROLL = 8
 ROW_TILE = 1024
-COMB_TILE = 512
-BIG_TILE = 512
+COMB_TILE = 256
+BIG_TILE = 1024
 SMALL_TILE = 256
 VMEM_BYTES = 66_500_000
 BF16 = jnp.bfloat16
@@ -218,7 +218,7 @@
 
 
 def backward_kernel(n_src, n_local, cap, chunks_ref, tok_ref, pos_ref, gate_ref, wg_ref, wu_ref, wd_ref,
-                    out_ref, dwg_ref, dwu_ref, dwd_ref,
+                    rows_ref, dwg_ref, dwu_ref, dwd_ref,
                     wide_x, wide_q, hot, rep, pack, gu_buf, dn_buf, base, total, sems):
     step = pl.program_id(0)
     hidden, ff = wg_ref.shape[1:]
@@ -263,15 +263,18 @@
             dw_pre = dot_tn(x_rows, grad_pre)
             dwg_ref[0] += dw_pre[:, :ff]
             dwu_ref[0] += dw_pre[:, ff:]
-            wide_x[rows, :] = dot_nt(grad_pre, gu_buf[slot]).astype(BF16)
+            rows_ref[0, rows_at(rows.start - expert * cap, rows.size), :] = dot_nt(grad_pre, gu_buf[slot]).astype(BF16)
 
         tiled_rows(expert * cap, total[expert], rows_step, BIG_TILE, SMALL_TILE)
 
-    @pl.when(step >= n_src + n_local)
-    def _():
-        src = step - n_src - n_local
-        length = fill_onehot(hot, rep, pos_ref, None, chunks_ref, src, n_local)
-        combine(out_ref, pack, hot, wide_x, base, chunks_ref, src, n_local, cap, length)
+        done = (total[expert] + SMALL_TILE - 1) // SMALL_TILE * (SMALL_TILE // CHUNK)
+        end = jnp.minimum(total[expert] // CHUNK + 128 // CHUNK, cap // CHUNK)
+
+        def clear(c, carry):
+            rows_ref[0, rows_at(c * CHUNK, CHUNK), :] = jnp.zeros((CHUNK, hidden), BF16)
+            return carry
+
+        lax.fori_loop(done, jnp.maximum(done, end), clear, 0)
 
 
 def expert_call(backward, chunks, table, pos, gate, w_gate, w_up, w_down):
@@ -279,7 +282,7 @@
     hidden, ff = w_gate.shape[1:]
     cap = n_src * 128 + BLOCK
     pack_rows = n_local * 128 + BLOCK
-    steps = 2 * n_src + n_local
+    steps = n_src + n_local if backward else 2 * n_src + n_local
 
     def src_in(i, *_):
         return (jnp.minimum(i, n_src - 1), 0)
@@ -302,6 +305,8 @@
     wide = pltpu.VMEM((n_local * cap, hidden), BF16)
     scratch = [wide]
     if backward:
+        out_shape = [jax.ShapeDtypeStruct((n_local, cap, hidden), BF16)]
+        out_specs = [pl.BlockSpec((1, cap, hidden), weight_out)]
         out_shape += [jax.ShapeDtypeStruct(w.shape, F32) for w in (w_gate, w_up, w_down)]
         out_specs += [pl.BlockSpec((1,) + w.shape[1:], weight_out) for w in (w_gate, w_up, w_down)]
         scratch += [wide]
@@ -333,111 +338,139 @@
     )(chunks, table, pos, gate, w_gate, w_up, w_down)
 
 
-def reduce_tail_kernel(part_ref, h_ref, x_ref, grad_ref, pre_ref, w1_ref, w2_ref, out_ref,
-                       sums, core_in, x_in, y_in, x_last, y_last, dx_buf, h_buf, x_buf, grad_buf, pre_buf, w1_buf, w2_buf,
-                       load_sem, row_sem, weight_sem, core_send, core_recv, hop_send, hop_recv, last_send, last_recv, dx_send, dx_recv):
+def reduce_tail_kernel(base_ref, rows_ref, pos_ref, h_ref, x_ref, grad_ref, pre_ref, w1_ref, w2_ref, out_ref,
+                       rows_buf, hot, pack, rep, work, sums, core_in, x_in, y_in, x_last, y_last,
+                       dx_buf, h_buf, x_buf, grad_buf, pre_buf, w1_buf, w2_buf,
+                       rows_sem, load_sem, pre_sem, core_send, core_recv, hop_send, hop_recv, last_send, last_recv, dx_send, dx_recv):
     n_chunks, half = x_in.shape[0], x_in.shape[2]
     chunk = 2 * half
+    n_local, cap = rows_ref.shape[:2]
     tok_rows = n_chunks * chunk
+    group = hot.shape[0] // 128
+    far, near_x, near_y, own = range(4)
     me = lax.axis_index("ep")
     core, x_pos, y_pos = lax.rem(me, 2), lax.rem(me // 2, 2), me // 4
     x_step, y_step = 2 - 4 * x_pos, 4 - 8 * y_pos
     partner = me + 1 - 2 * core
     x_peer, y_peer = me + x_step, me + y_step
     pp_peer = 1 - lax.axis_index("pp")
-    offsets = (0, x_step, y_step, x_step + y_step)
     mesh_id = pl.DeviceIdType.MESH
 
     barrier = pltpu.get_barrier_semaphore()
     for peer in ({"ep": partner}, {"ep": x_peer}, {"ep": y_peer}, {"pp": pp_peer}):
         pl.semaphore_signal(barrier, inc=1, device_id=peer, device_id_type=mesh_id)
-    pl.semaphore_wait(barrier, 4)
-
-    def part_rows(dest, k):
-        return part_ref.at[pl.ds(pl.multiple_of(dest * tok_rows + k * chunk, chunk), chunk)]
-
-    def core_copy(k, i):
-        return pltpu.make_async_remote_copy(part_rows(partner + offsets[i], k), core_in.at[k, i], core_send.at[k, i], core_recv.at[k, i],
-                                            device_id={"ep": partner}, device_id_type=mesh_id)
-
-    def load_copy(k, i):
-        return pltpu.make_async_copy(part_rows(me + offsets[i], k), sums.at[k, i], load_sem.at[k, i])
-
-    def hop_copies(k):
-        top, low = pl.ds(0, half), pl.ds(half, half)
-        return [
-            pltpu.make_async_remote_copy(sums.at[k, i, rows], land.at[k, j], hop_send.at[k, n], hop_recv.at[k, n],
-                                         device_id={"ep": peer}, device_id_type=mesh_id)
-            for n, (i, rows, land, j, peer) in enumerate((
-                (3, top, x_in, 1, x_peer), (3, low, y_in, 1, y_peer), (1, top, x_in, 0, x_peer), (2, low, y_in, 0, y_peer)))
-        ]
-
-    def last_copies(k):
-        top, low = pl.ds(0, half), pl.ds(half, half)
-        return [
-            pltpu.make_async_remote_copy(sums.at[k, 2, top], y_last.at[k], last_send.at[k, 0], last_recv.at[k, 0],
-                                         device_id={"ep": y_peer}, device_id_type=mesh_id),
-            pltpu.make_async_remote_copy(sums.at[k, 1, low], x_last.at[k], last_send.at[k, 1], last_recv.at[k, 1],
-                                         device_id={"ep": x_peer}, device_id_type=mesh_id),
-        ]
+
+    def expert_rows(e):
+        return pltpu.make_async_copy(rows_ref.at[e], rows_buf.at[pl.ds(e * cap, cap)], rows_sem.at[e])
+
+    def start_rows(e, carry):
+        expert_rows(e).start()
+        return carry
+
+    lax.fori_loop(0, n_local, start_rows, 0)
+    rows_buf[n_local * cap:] = jnp.zeros((rows_buf.shape[0] - n_local * cap,) + rows_buf.shape[1:], BF16)
+
+    def loads():
+        pairs = ((h_ref, h_buf), (x_ref, x_buf), (grad_ref, grad_buf), (w1_ref, w1_buf), (w2_ref, w2_buf))
+        return [pltpu.make_async_copy(src, dst, load_sem.at[n]) for n, (src, dst) in enumerate(pairs)]
 
     def chunk_rows(k):
         return pl.ds(pl.multiple_of(k * chunk, chunk), chunk)
 
-    def row_copies(k):
-        return [pltpu.make_async_copy(src.at[chunk_rows(k)], buf.at[chunk_rows(k)], row_sem.at[k, n])
-                for n, (src, buf) in enumerate(((h_ref, h_buf), (x_ref, x_buf), (grad_ref, grad_buf), (pre_ref, pre_buf)))]
-
-    def weight_loads():
-        return [pltpu.make_async_copy(w1_ref, w1_buf, weight_sem.at[0]), pltpu.make_async_copy(w2_ref, w2_buf, weight_sem.at[1])]
+    def half_rows(k, low):
+        return pl.ds(pl.multiple_of(k * chunk + low * half, half), half)
+
+    def pre_copy(k):
+        return pltpu.make_async_copy(pre_ref.at[chunk_rows(k)], pre_buf.at[lax.rem(k, 2)], pre_sem.at[k])
+
+    def core_copy(t):
+        return pltpu.make_async_remote_copy(work.at[0], core_in.at[t], core_send.at[t], core_recv.at[t],
+                                            device_id={"ep": partner}, device_id_type=mesh_id)
+
+    def hop_copy(k, n):
+        t, low, land, j, peer = ((far, 0, x_in, 1, x_peer), (far, 1, y_in, 1, y_peer), (near_x, 0, x_in, 0, x_peer), (near_y, 1, y_in, 0, y_peer))[n]
+        return pltpu.make_async_remote_copy(sums.at[t, half_rows(k, low)], land.at[k, j], hop_send.at[k, n], hop_recv.at[k, n],
+                                            device_id={"ep": peer}, device_id_type=mesh_id)
+
+    def last_copy(k, n):
+        t, low, land, peer = ((near_y, 0, y_last, y_peer), (near_x, 1, x_last, x_peer))[n]
+        return pltpu.make_async_remote_copy(sums.at[t, half_rows(k, low)], land.at[k], last_send.at[k, n], last_recv.at[k, n],
+                                            device_id={"ep": peer}, device_id_type=mesh_id)
 
     def dx_copy(k):
         return pltpu.make_async_remote_copy(dx_buf.at[chunk_rows(k)], out_ref.at[chunk_rows(k)], dx_send.at[k], dx_recv.at[k],
                                             device_id={"pp": pp_peer}, device_id_type=mesh_id)
 
-    def start_chunk(k, carry):
-        for i in (3, 1, 2, 0):
-            core_copy(k, i).start()
-            load_copy(k, i).start()
-        return carry
-
-    lax.fori_loop(0, n_chunks, start_chunk, 0)
-
-    def add_cores(k, carry):
-        hops = hop_copies(k)
-        for i, ready in ((3, (0, 1)), (1, (2,)), (2, (3,)), (0, ())):
-            load_copy(k, i).wait()
-            core_copy(k, i).wait_recv()
-            sums[k, i] = sums[k, i] + core_in[k, i]
-            for n in ready:
-                hops[n].start()
-        return carry
-
-    lax.fori_loop(0, n_chunks, add_cores, 0)
-
-    for copy in weight_loads():
+    iota = lax.broadcasted_iota(jnp.int32, (CHUNK, tok_rows), 0).astype(F32).astype(BF16)
+    ones = jnp.ones((CHUNK, tok_rows), BF16)
+
+    def combine_dest(dest, slot):
+        for expert in range(n_local):
+            rep[expert] = jnp.broadcast_to(pos_ref[dest, expert:expert + 1, :], (CHUNK, tok_rows)).astype(BF16)
+        work[slot] = jnp.zeros(work.shape[1:], F32)
+
+        def part(g, carry):
+            for i in range(group):
+                expert = g * group + i
+                pos_rows = rep[expert]
+                for c in range(128 // CHUNK):
+                    line = i * 128 + c * CHUNK
+                    hot[line:line + CHUNK, :] = jnp.where(iota + jnp.bfloat16(c * CHUNK) == pos_rows, ones, jnp.zeros_like(ones))
+                pack[i * 128:(i + 1) * 128, :] = rows_buf[pl.ds(expert * cap + base_ref[dest, expert], 128 // CHUNK)].reshape(128, pack.shape[1])
+            work[slot] += dot_tn(hot[...], pack[...])
+            return carry
+
+        lax.fori_loop(0, n_local // group, part, 0)
+
+    def wait_rows(e, carry):
+        expert_rows(e).wait()
+        return carry
+
+    lax.fori_loop(0, n_local, wait_rows, 0)
+    for copy in loads():
         copy.start()
-
-    def start_rows(k, carry):
-        for copy in row_copies(k):
-            copy.start()
-        return carry
-
-    lax.fori_loop(0, n_chunks, start_rows, 0)
+    for k in range(2):
+        pre_copy(k).start()
+    pl.semaphore_wait(barrier, 4)
+
+    def start_hops(*which):
+        def body(k, carry):
+            for n in which:
+                hop_copy(k, n).start()
+            return carry
+
+        lax.fori_loop(0, n_chunks, body, 0)
+
+    def one_chip(t, carry):
+        shift = x_step * (1 - t // 2) + y_step * (1 - lax.rem(t, 2))
+
+        @pl.when(t > 0)
+        def _():
+            core_copy(t - 1).wait_send()
+
+        combine_dest(partner + shift, 0)
+        core_copy(t).start()
+        combine_dest(me + shift, 1)
+        core_copy(t).wait_recv()
+        sums[t] = work[1] + core_in[t]
+        pl.when(t == far)(functools.partial(start_hops, 0, 1))
+        pl.when(t == near_x)(functools.partial(start_hops, 2))
+        pl.when(t == near_y)(functools.partial(start_hops, 3))
+        return carry
+
+    lax.fori_loop(0, 4, one_chip, 0)
+    core_copy(3).wait_send()
 
     def relay(k, carry):
-        hops, lasts = hop_copies(k), last_copies(k)
-        hops[0].wait_recv()
-        sums[k, 2, :half] = sums[k, 2, :half] + x_in[k, 1]
-        lasts[0].start()
-        hops[1].wait_recv()
-        sums[k, 1, half:] = sums[k, 1, half:] + y_in[k, 1]
-        lasts[1].start()
+        for n, (t, low, land) in enumerate(((near_y, 0, x_in), (near_x, 1, y_in))):
+            hop_copy(k, n).wait_recv()
+            sums[t, half_rows(k, low), :] = sums[t, half_rows(k, low), :] + land[k, 1]
+            last_copy(k, n).start()
         return carry
 
     lax.fori_loop(0, n_chunks, relay, 0)
 
-    for copy in weight_loads():
+    for copy in loads():
         copy.wait()
 
     def norm_grad(values, grads):
@@ -446,18 +479,20 @@
 
     def finish(k, carry):
         rows = chunk_rows(k)
-        hops, lasts = hop_copies(k), last_copies(k)
-        for copy in row_copies(k):
-            copy.wait()
-        for copy in hops[2:]:
-            copy.wait_recv()
-        for copy in lasts:
-            copy.wait_recv()
-        sums[k, 0, :half] = sums[k, 0, :half] + x_in[k, 0] + y_last[k]
-        sums[k, 0, half:] = sums[k, 0, half:] + y_in[k, 0] + x_last[k]
-        grad_h = grad_buf[rows, :].astype(F32) + norm_grad(h_buf[rows, :].astype(F32), sums[k, 0])
+        pre_copy(k).wait()
+        for n in range(2):
+            hop_copy(k, n + 2).wait_recv()
+            last_copy(k, n).wait_recv()
+        sums[own, half_rows(k, 0), :] = sums[own, half_rows(k, 0), :] + x_in[k, 0] + y_last[k]
+        sums[own, half_rows(k, 1), :] = sums[own, half_rows(k, 1), :] + y_in[k, 0] + x_last[k]
+        grad_h = grad_buf[rows, :].astype(F32) + norm_grad(h_buf[rows, :].astype(F32), sums[own, rows, :])
         grad_act = dot_nt(grad_h.astype(BF16), w2_buf[...])
-        grad_pre = (grad_act * silu_grad(pre_buf[rows, :])).astype(BF16)
+        grad_pre = (grad_act * silu_grad(pre_buf[lax.rem(k, 2)])).astype(BF16)
+
+        @pl.when(k + 2 < n_chunks)
+        def _():
+            pre_copy(k + 2).start()
+
         grad_norm = dot_nt(grad_pre, w1_buf[...])
         dx_buf[rows, :] = (grad_h + norm_grad(x_buf[rows, :].astype(F32), grad_norm)).astype(BF16)
         dx_copy(k).start()
@@ -466,48 +501,56 @@
     lax.fori_loop(0, n_chunks, finish, 0)
 
     def drain(k, carry):
-        for i in range(4):
-            core_copy(k, i).wait_send()
-        for copy in hop_copies(k) + last_copies(k):
-            copy.wait_send()
+        for n in range(4):
+            hop_copy(k, n).wait_send()
+        for n in range(2):
+            last_copy(k, n).wait_send()
         dx_copy(k).wait()
         return carry
 
     lax.fori_loop(0, n_chunks, drain, 0)
 
 
-def reduce_tail(part, h_rows, x_rows, grad_rows, hidden_pre, w_one, w_two):
+def reduce_tail(base, expert_out, pos, h_rows, x_rows, grad_rows, hidden_pre, w_one, w_two):
     tok_rows, hidden = x_rows.shape
+    n_local, cap = expert_out.shape[0], expert_out.shape[1] // CHUNK
+    expert_out = expert_out.reshape(n_local, cap, CHUNK, hidden)
     ff = w_one.shape[1]
     n_chunks = 4
     half = tok_rows // (2 * n_chunks)
     raw = pl.BlockSpec(memory_space=pl.ANY)
     dma = pltpu.SemaphoreType.DMA
     rows_buf = pltpu.VMEM((tok_rows, hidden), BF16)
+    group = n_local // 2
     return pl.pallas_call(
         reduce_tail_kernel,
         out_shape=jax.ShapeDtypeStruct((tok_rows, hidden), BF16),
-        in_specs=[raw] * 7,
+        in_specs=[pl.BlockSpec(memory_space=pltpu.SMEM), raw, pl.BlockSpec(memory_space=pltpu.VMEM)] + [raw] * 6,
         out_specs=raw,
         scratch_shapes=[
-            pltpu.VMEM((n_chunks, 4, 2 * half, hidden), F32),
-            pltpu.VMEM((n_chunks, 4, 2 * half, hidden), F32),
+            pltpu.VMEM((n_local * cap + (128 - BLOCK) // CHUNK, CHUNK, hidden), BF16),
+            pltpu.VMEM((group * 128, tok_rows), BF16),
+            pltpu.VMEM((group * 128, hidden), BF16),
+            pltpu.VMEM((n_local, CHUNK, tok_rows), BF16),
+            pltpu.VMEM((2, tok_rows, hidden), F32),
+            pltpu.VMEM((4, tok_rows, hidden), F32),
+            pltpu.VMEM((4, tok_rows, hidden), F32),
             pltpu.VMEM((n_chunks, 2, half, hidden), F32),
             pltpu.VMEM((n_chunks, 2, half, hidden), F32),
             pltpu.VMEM((n_chunks, half, hidden), F32),
             pltpu.VMEM((n_chunks, half, hidden), F32),
             rows_buf, rows_buf, rows_buf, rows_buf,
-            pltpu.VMEM((tok_rows, ff), F32),
+            pltpu.VMEM((2, 2 * half, ff), F32),
             pltpu.VMEM(w_one.shape, BF16),
             pltpu.VMEM(w_two.shape, BF16),
-            dma((n_chunks, 4)), dma((n_chunks, 4)), dma((2,)),
-            dma((n_chunks, 4)), dma((n_chunks, 4)), dma((n_chunks, 4)), dma((n_chunks, 4)),
+            dma((n_local,)), dma((5,)), dma((n_chunks,)),
+            dma((4,)), dma((4,)), dma((n_chunks, 4)), dma((n_chunks, 4)),
             dma((n_chunks, 2)), dma((n_chunks, 2)), dma((n_chunks,)), dma((n_chunks,)),
         ],
         compiler_params=pltpu.CompilerParams(collective_id=0, has_side_effects=True, vmem_limit_bytes=VMEM_BYTES),
         cost_estimate=pl.CostEstimate(flops=60 * 10 ** 9, bytes_accessed=40 * 10 ** 6, transcendentals=0),
         name="reduce_tail",
-    )(part, h_rows, x_rows, grad_rows, hidden_pre, w_one, w_two)
+    )(base, expert_out, pos, h_rows, x_rows, grad_rows, hidden_pre, w_one, w_two)
 
 
 def head_kernel(x_ref, saved_ref, grad_ref, w1_ref, w2_ref, routes_ref,
@@ -760,9 +803,11 @@
         mix_sum = lax.psum_scatter(part_fwd, "ep", scatter_dimension=0, tiled=True)
         y_out = (h_fwd.astype(F32) + mix_sum).astype(BF16)
 
-        part_bwd, dw_gate, dw_up, dw_down = expert_call(True, chunks_b, all_bwd, pos_b, gate_b, w_gate, w_up, w_down)
+        earlier = (jnp.arange(ep_size)[:, None] > jnp.arange(ep_size)[None, :]).astype(jnp.int32)
+        base_b = jnp.sum(earlier[:, :, None] * chunks_b[None], axis=1)
+        rows_bwd, dw_gate, dw_up, dw_down = expert_call(True, chunks_b, all_bwd, pos_b, gate_b, w_gate, w_up, w_down)
         y_next = lax.ppermute(y_out, "pp", next_perm)
-        dx_prev = reduce_tail(part_bwd, h_bwd, x_saved, grad_in, hidden_pre, w_one, w_two)
+        dx_prev = reduce_tail(base_b, rows_bwd, pos_b, h_bwd, x_saved, grad_in, hidden_pre, w_one, w_two)
         return y_next[None], dx_prev[None], dw_gate[None], dw_up[None], dw_down[None]
 
     in_specs = (tok_spec,) * 9 + (dense_spec, dense_spec, expert_spec, expert_spec, expert_spec)

time: 380 us -> 368 us (0.968); the launches traced: 373 us -> 367 us
  Pallas kernels: 321 us -> 271 us
  waiting for transfers between devices: 24.8 us -> 67.7 us
    pallas_call x2, Pallas kernels: 173 us -> 129 us  [expert_call(): pl.pallas_call(functools.partial(body, n_src, n_local, cap), grid_spec=pl...]
    reduce_scatter x1, waiting for transfers between devices: 7.91 us -> 39 us  [device_step(): mix_sum = lax.psum_scatter(part_fwd, 'ep', scatter_dimension=0, tiled=True)]
    all_gather x1, waiting for transfers between devices: 16.8 us -> 28.7 us  [device_step(): all_bwd = lax.all_gather(pair, 'ep', axis=0, tiled=True)]
    pallas_call x1, Pallas kernels: 99.2 us -> 92.7 us  [reduce_tail(): pl.pallas_call(reduce_tail_kernel, out_shape=jax.ShapeDtypeStruct((tok_ro...]
  transfers between devices with their start and end apart: 3 -> 3, of which waited for: 2 -> 2; matrix products, arithmetic and copies ran while one was open for 0% -> 1% of each run, Pallas kernels for 73% -> 60%
where the time goes in v6:
time: 368 us; the launch traced here: 367 us
  Pallas kernels  271 us (74%)
  waiting for transfers between devices  67.7 us (18%)
  between operations  14.1 us (4%)
  other arithmetic  7.15 us (2%)
  local copies, waits for them, and re-layouts  5.2 us (1%)
    pallas_call x2, Pallas kernels, expert_call(): pl.pallas_call(functools.partial(body, n_src, n_local, cap), grid_spec=pl...  129 us
    pallas_call x1, Pallas kernels, reduce_tail(): pl.pallas_call(reduce_tail_kernel, out_shape=jax.ShapeDtypeStruct((tok_ro...  92.7 us
    pallas_call x1, Pallas kernels, head(): pl.pallas_call(head_kernel, out_shape=[jax.ShapeDtypeStruct((n_src * tok_...  49.4 us
    reduce_scatter x1, waiting for transfers between devices, device_step(): mix_sum = lax.psum_scatter(part_fwd, 'ep', scatter_dimension=0, tiled=True)  39 us
    all_gather x1, waiting for transfers between devices, device_step(): all_bwd = lax.all_gather(pair, 'ep', axis=0, tiled=True)  28.7 us
  transfers between devices with their start and end apart: 3, of which 2 were waited for; matrix products, arithmetic and copies ran while one was open for 1% of the time, Pallas kernels for 60%

profile of v6, /device:TPU:0, one launch (start us, length us, event | category | flops | bytes accessed | tf_op | source)
XLA Modules:
  0.0 366.8 jit_solution(1043353433604841738)
XLA Ops:
  7.2 0.0 all-gather.2.cloned.1.call-start
  7.2 0.8 fusion
  8.0 1.4 maximum_bitcast_fusion.routes_ref
  9.4 49.4 %head.1 = (bf16[8192,512]{1,0:T(8,128)(2,1)}, bf16[1024,512]{1,0:T(8,128)(2,1)}, bf16[1024,512]{1,0:T(8,128)(2,1)}, f32[1024,1536]{1,0:T(8,128)}, bf16[1024,1024...) custom-call(bf16[1024,512]{1,0:T(8,128)(2,1)} %bitcast.43, ...), custom_call_target="tpu_custom_call" | custom-call | flops 30000001024 | bytes 20000000 | tf_op jit(solution)/shard_map/head/pallas_call | solution.py:749
  58.9 0.0 all-gather.2.cloned.1.call-update
  58.9 0.2 reduce-scatter.2.cloned.1.call-start
  59.1 1.1 add_reduce_fusion
  60.2 0.1 sub.18
  60.3 0.6 slice_bitcast_fusion
  60.9 0.0 copy-start
  60.9 55.2 %expert_forward.1 = f32[8192,512]{1,0:T(8,128)} custom-call(s32[8,16]{1,0:T(8,128)} %get-tuple-element.38.chunks_ref, bf16[8192,512]{1,0:T(8,128)(2,1)} %get-tuple-element.23.tok_ref, f32[8,16,1024]{2,1,0:T(8,128)} %bitcast.55, f32[8,16,1024]{2,1,0:T(8,128)} %bitcast.56, bf16[16,512,384]{2,1,0:T(8,128)(2,1)} %bitcast.33, bf16[16,512,384]{2,1,0:T(8,128)(2,1)} %bitcast.35, ...), custom_call_target="tpu_custom_call" | custom-call | flops 60000002048 | bytes 60000000 | tf_op jit(solution)/shard_map/expert_forward/pallas_call | solution.py:325
  116.2 28.7 %all-gather.2.cloned.1.call-done.tok_ref = bf16[8192,1024]{1,0:T(8,128)(2,1)} async-done(((bf16[1024,1024]{1,0:T(8,128)(2,1)}), bf16[8192,1024]{1,0:T(8,128)(2,1)}) %all-gather.2.cloned.1.call-update) | async-done | bytes 16777232 | tf_op jit(solution)/shard_map/all_gather | solution.py:796
  144.9 0.0 reduce-scatter.2.cloned.1.call-update
  144.9 0.0 copy-done
  144.9 0.7 multiply_reduce_fusion.base_ref
  145.6 73.5 %expert_backward.1 = (bf16[16,1088,512]{2,1,0:T(8,128)(2,1)}, f32[16,512,384]{2,1,0:T(8,128)}, f32[16,512,384]{2,1,0:T(8,128)}, f32[16,384,512]{2,1,0:T(8,128)}) custom-call(s32[8,16]{1,0:T(8,128)} %copy-done, bf16[8192,1024]{1,0:T(8,128)(2,1)} %all-gather.2.cloned.1.call-done.tok_ref, f32[8,16,1024]{2,1,0:T(8,128)} %bitcast.52, f32[8,16,1024]{2,1,0:T(8,128)} %bitcast.54, ...), custom_call_target="tpu_custom_call" | custom-call | flops 99999997952 | bytes 60000000 | tf_op jit(solution)/shard_map/expert_backward/pallas_call | solution.py:325
  219.1 39.0 %reduce-scatter.2.cloned.1.call-done = f32[1024,512]{1,0:T(8,128)} async-done(((f32[8192,512]{1,0:T(8,128)}), f32[1024,512]{1,0:T(8,128)}) %reduce-scatter.2.cloned.1.call-update) | async-done | bytes 2097168 | tf_op jit(solution)/shard_map/reduce_scatter | solution.py:803
  258.1 3.2 add_convert_fusion
  261.2 1.5 collective-permute-start
  262.7 92.7 %reduce_tail.1 = bf16[1024,512]{1,0:T(8,128)(2,1)} custom-call(s32[8,16]{1,0:T(8,128)} %multiply_reduce_fusion.base_ref, bf16[16,68,16,512]{3,2,1,0:T(8,128)(2,1)} %bitcast.48, f32[8,16,1024]{2,1,0:T(8,128)} %bitcast.53, bf16[1024,512]{1,0:T(8,128)(2,1)} %get-tuple-element.32.h_ref, bf16[1024,512]{1,0:T(8,128)(2,1)} %bitcast.45, bf16[1024,512]{1,0:T(8,128)(2,1)} %bitcast.47, ...), custom_call_target="tpu_custom_call" | custom-call | flops 60000002048 | bytes 40000000 | tf_op jit(solution)/shard_map/reduce_tail/pallas_call | solution.py:525
  355.5 0.0 collective-permute-done
  355.5 2.3 copy.21
  357.7 2.3 copy.22
  (2 shorter events, 0.0 us)
Async XLA Ops:
  7.2 137.7 %all-gather.2.cloned.1.call-start = ((), (), s32[]{:S(2)}) async-start(), calls=%async_computation.1 | async-start | bytes 18874368 | tf_op jit(solution)/shard_map/all_gather | solution.py:796
  58.9 199.2 %reduce-scatter.2.cloned.1.call-start = ((), (), s32[]{:S(2)}) async-start(), calls=%async_computation.2 | async-start | bytes 18874368 | tf_op jit(solution)/shard_map/reduce_scatter | solution.py:803
  60.9 84.0 %copy-start = (s32[8,16]{1,0:T(8,128)}, s32[8,16]{1,0:T(8,128)S(1)}, u32[]{:S(2)}) copy-start(s32[8,16]{1,0:T(8,128)S(1)} %get-tuple-element.37.chunks_ref) | copy-start | bytes 1540
  261.2 94.2 %collective-permute-start = (bf16[1024,512]{1,0:T(8,128)(2,1)}, bf16[1024,512]{1,0:T(8,128)(2,1)}, u32[]{:S(2)}, u32[]{:S(2)}) collective-permute-start(bf16[1024,512]{1,0:T(8,128)(2,1)} %add_convert_fusion), channel_id=1, source_target_pairs={{0,8},{8,0},{1,9},{9,1},{2,10},{10,2},{3,11},{11,3},{4,12},{12,4},... | collective-permute-start | bytes 3145736 | tf_op jit(solution)/shard_map/ppermute | solution.py:809
Sparse Core Ops, SparseCore 0:
  59.0 85.8 all-gather.1
  148.4 109.6 reduce-scatter.1

commit v7 on v6

--- a/solution.py
+++ b/solution.py
@@ -801,13 +801,15 @@
         (part_fwd,) = expert_call(False, chunks_f, all_fwd, pos_f, gate_f, w_gate, w_up, w_down)
         part_fwd, all_bwd = lax.optimization_barrier((part_fwd, all_bwd))
         mix_sum = lax.psum_scatter(part_fwd, "ep", scatter_dimension=0, tiled=True)
-        y_out = (h_fwd.astype(F32) + mix_sum).astype(BF16)
+        mix_sum = lax.ppermute(mix_sum, "pp", next_perm)
+        h_fwd = lax.ppermute(h_fwd, "pp", next_perm)
 
         earlier = (jnp.arange(ep_size)[:, None] > jnp.arange(ep_size)[None, :]).astype(jnp.int32)
         base_b = jnp.sum(earlier[:, :, None] * chunks_b[None], axis=1)
         rows_bwd, dw_gate, dw_up, dw_down = expert_call(True, chunks_b, all_bwd, pos_b, gate_b, w_gate, w_up, w_down)
-        y_next = lax.ppermute(y_out, "pp", next_perm)
         dx_prev = reduce_tail(base_b, rows_bwd, pos_b, h_bwd, x_saved, grad_in, hidden_pre, w_one, w_two)
+        mix_sum, h_fwd, dx_prev = lax.optimization_barrier((mix_sum, h_fwd, dx_prev))
+        y_next = (h_fwd.astype(F32) + mix_sum).astype(BF16)
         return y_next[None], dx_prev[None], dw_gate[None], dw_up[None], dw_down[None]
 
     in_specs = (tok_spec,) * 9 + (dense_spec, dense_spec, expert_spec, expert_spec, expert_spec)

time: 368 us -> 365 us (level)
  waiting for transfers between devices: 67.7 us -> 39.3 us
  Pallas kernels: 271 us -> 298 us
    pallas_call x2, Pallas kernels: 129 us -> 156 us  [expert_call(): pl.pallas_call(functools.partial(body, n_src, n_local, cap), grid_spec=pl...]
    reduce_scatter x1, waiting for transfers between devices: 39 us -> 18.9 us  [device_step(): mix_sum = lax.psum_scatter(part_fwd, 'ep', scatter_dimension=0, tiled=True)]
    all_gather x1, waiting for transfers between devices: 28.7 us -> 20.3 us  [device_step(): all_bwd = lax.all_gather(pair, 'ep', axis=0, tiled=True)]
  transfers between devices with their start and end apart: 3 -> 4, of which waited for: 2 -> 2; matrix products, arithmetic and copies ran while one was open for 1% -> 1% of each run, Pallas kernels for 60% -> 68%
where the time goes in v7:
time: 365 us
  Pallas kernels  298 us (82%)
  waiting for transfers between devices  39.3 us (11%)
  between operations  14.1 us (4%)
  other arithmetic  7.15 us (2%)
    pallas_call x2, Pallas kernels, expert_call(): pl.pallas_call(functools.partial(body, n_src, n_local, cap), grid_spec=pl...  156 us
    pallas_call x1, Pallas kernels, reduce_tail(): pl.pallas_call(reduce_tail_kernel, out_shape=jax.ShapeDtypeStruct((tok_ro...  92.7 us
    pallas_call x1, Pallas kernels, head(): pl.pallas_call(head_kernel, out_shape=[jax.ShapeDtypeStruct((n_src * tok_...  49.4 us
    all_gather x1, waiting for transfers between devices, device_step(): all_bwd = lax.all_gather(pair, 'ep', axis=0, tiled=True)  20.3 us
    reduce_scatter x1, waiting for transfers between devices, device_step(): mix_sum = lax.psum_scatter(part_fwd, 'ep', scatter_dimension=0, tiled=True)  18.9 us
  transfers between devices with their start and end apart: 4, of which 2 were waited for; matrix products, arithmetic and copies ran while one was open for 1% of the time, Pallas kernels for 68%

profile of v7, /device:TPU:0, one launch (start us, length us, event | category | flops | bytes accessed | tf_op | source)
XLA Modules:
  0.0 364.6 jit_solution(9032444563126080293)
XLA Ops:
  7.2 0.0 all-gather.2.cloned.1.call-start
  7.2 0.8 fusion.1
  8.0 1.4 maximum_bitcast_fusion.routes_ref
  9.4 49.4 %head.1 = (bf16[8192,512]{1,0:T(8,128)(2,1)}, bf16[1024,512]{1,0:T(8,128)(2,1)}, bf16[1024,512]{1,0:T(8,128)(2,1)}, f32[1024,1536]{1,0:T(8,128)}, bf16[1024,1024...) custom-call(bf16[1024,512]{1,0:T(8,128)(2,1)} %bitcast.44, ...), custom_call_target="tpu_custom_call" | custom-call | flops 30000001024 | bytes 20000000 | tf_op jit(solution)/shard_map/head/pallas_call | solution.py:749
  58.8 0.0 all-gather.2.cloned.1.call-update
  58.9 0.2 reduce-scatter.2.cloned.1.call-start
  59.1 1.1 add_reduce_fusion
  60.2 0.1 sub.18
  60.3 0.6 slice_bitcast_fusion
  60.9 0.0 copy-start
  60.9 63.7 %expert_forward.1 = f32[8192,512]{1,0:T(8,128)} custom-call(s32[8,16]{1,0:T(8,128)} %get-tuple-element.44.chunks_ref, bf16[8192,512]{1,0:T(8,128)(2,1)} %get-tuple-element.25.tok_ref, f32[8,16,1024]{2,1,0:T(8,128)} %bitcast.56, f32[8,16,1024]{2,1,0:T(8,128)} %bitcast.57, bf16[16,512,384]{2,1,0:T(8,128)(2,1)} %bitcast.34, bf16[16,512,384]{2,1,0:T(8,128)(2,1)} %bitcast.36, ...), custom_call_target="tpu_custom_call" | custom-call | flops 60000002048 | bytes 60000000 | tf_op jit(solution)/shard_map/expert_forward/pallas_call | solution.py:325
  124.6 20.3 %all-gather.2.cloned.1.call-done.tok_ref = bf16[8192,1024]{1,0:T(8,128)(2,1)} async-done(((bf16[1024,1024]{1,0:T(8,128)(2,1)}), bf16[8192,1024]{1,0:T(8,128)(2,1)}) %all-gather.2.cloned.1.call-update) | async-done | bytes 16777232 | tf_op jit(solution)/shard_map/all_gather | solution.py:796
  144.9 0.0 reduce-scatter.2.cloned.1.call-update
  144.9 1.5 collective-permute-start.1
  146.4 0.0 copy-done
  146.4 0.7 multiply_reduce_fusion.base_ref
  147.1 92.0 %expert_backward.1 = (bf16[16,1088,512]{2,1,0:T(8,128)(2,1)}, f32[16,512,384]{2,1,0:T(8,128)}, f32[16,512,384]{2,1,0:T(8,128)}, f32[16,384,512]{2,1,0:T(8,128)}) custom-call(s32[8,16]{1,0:T(8,128)} %copy-done, bf16[8192,1024]{1,0:T(8,128)(2,1)} %all-gather.2.cloned.1.call-done.tok_ref, f32[8,16,1024]{2,1,0:T(8,128)} %bitcast.53, f32[8,16,1024]{2,1,0:T(8,128)} %bitcast.55, ...), custom_call_target="tpu_custom_call" | custom-call | flops 99999997952 | bytes 60000000 | tf_op jit(solution)/shard_map/expert_backward/pallas_call | solution.py:325
  239.1 18.9 %reduce-scatter.2.cloned.1.call-done = f32[1024,512]{1,0:T(8,128)} async-done(((f32[8192,512]{1,0:T(8,128)}), f32[1024,512]{1,0:T(8,128)}) %reduce-scatter.2.cloned.1.call-update) | async-done | bytes 2097168 | tf_op jit(solution)/shard_map/reduce_scatter | solution.py:803
  258.1 1.5 collective-permute-start
  259.5 92.7 %reduce_tail.1 = bf16[1024,512]{1,0:T(8,128)(2,1)} custom-call(s32[8,16]{1,0:T(8,128)} %multiply_reduce_fusion.base_ref, bf16[16,68,16,512]{3,2,1,0:T(8,128)(2,1)} %bitcast.49, f32[8,16,1024]{2,1,0:T(8,128)} %bitcast.54, bf16[1024,512]{1,0:T(8,128)(2,1)} %get-tuple-element.35.h_ref, bf16[1024,512]{1,0:T(8,128)(2,1)} %bitcast.46, bf16[1024,512]{1,0:T(8,128)(2,1)} %bitcast.48, ...), custom_call_target="tpu_custom_call" | custom-call | flops 60000002048 | bytes 40000000 | tf_op jit(solution)/shard_map/reduce_tail/pallas_call | solution.py:525
  352.3 0.0 collective-permute-done.1
  352.3 0.0 collective-permute-done
  352.3 3.2 fusion
  355.5 2.3 copy.20
  (2 shorter events, 0.0 us)
Async XLA Ops:
  7.2 137.7 %all-gather.2.cloned.1.call-start = ((), (), s32[]{:S(2)}) async-start(), calls=%async_computation.1 | async-start | bytes 18874368 | tf_op jit(solution)/shard_map/all_gather | solution.py:796
  58.9 199.2 %reduce-scatter.2.cloned.1.call-start = ((), (), s32[]{:S(2)}) async-start(), calls=%async_computation.2 | async-start | bytes 18874368 | tf_op jit(solution)/shard_map/reduce_scatter | solution.py:803
  60.9 85.5 %copy-start = (s32[8,16]{1,0:T(8,128)}, s32[8,16]{1,0:T(8,128)S(1)}, u32[]{:S(2)}) copy-start(s32[8,16]{1,0:T(8,128)S(1)} %get-tuple-element.43.chunks_ref) | copy-start | bytes 1540
  144.9 207.4 %collective-permute-start.1 = (bf16[1024,512]{1,0:T(8,128)(2,1)}, bf16[1024,512]{1,0:T(8,128)(2,1)}, u32[]{:S(2)}, u32[]{:S(2)}) collective-permute-start(bf16[1024,512]{1,0:T(8,128)(2,1)} %get-tuple-element.30), channel_id=1, source_target_pairs={{0,8},{8,0},{1,9},{9,1},{2,10},{10,2},{3,11},{11,3},{4,12},{12,4},... | collective-permute-start | bytes 3145736 | tf_op jit(solution)/shard_map/ppermute | solution.py:805
  258.1 94.3 %collective-permute-start = (f32[1024,512]{1,0:T(8,128)}, f32[1024,512]{1,0:T(8,128)}, u32[]{:S(2)}, u32[]{:S(2)}) collective-permute-start(f32[1024,512]{1,0:T(8,128)} %reduce-scatter.2.cloned.1.call-done), channel_id=1, source_target_pairs={{0,8},{8,0},{1,9},{9,1},{2,10},{10,2},{3,11},{11,3},{4,12},{12,4},... | collective-permute-start | bytes 6291464 | tf_op jit(solution)/shard_map/ppermute | solution.py:804
Sparse Core Ops, SparseCore 0:
  59.0 85.8 all-gather.1
  148.4 109.6 reduce-scatter.1
